TPU v7x, 32 devices: a whole 2x2x4 slice. The times are simulated.
32 devices in a mesh: dp: 8 (over y, x, core), mp: 4 (over z).
Axes of the slice: x: 2, y: 2, z: 4, core: 2. Of those that a mesh axis runs over, the one named last changes fastest.
Arguments:
- inputs: bfloat16 [8192, 2048], P(('dp', 'mp')), may hold values from -6 to 6
- segments: int32 [8, 1024], P('dp'), may hold values from 0 to 5, never falling along the last dimension, each value on 1 to 512 neighbouring positions
- first_norm_gain: float32 [2048], replicated, may hold values from 0.1 to 1.9
- w_query: bfloat16 [2048, 2048], P('dp', 'mp'), may hold values from -0.125 to 0.125
- w_key: bfloat16 [2048, 2048], P('dp', 'mp'), may hold values from -0.125 to 0.125
- w_value: bfloat16 [2048, 3456], P('dp', 'mp'), may hold values from -0.125 to 0.125
- w_gate: bfloat16 [2048, 3456], P('dp', 'mp'), may hold values from -0.125 to 0.125
- w_out: bfloat16 [3456, 2048], P('mp', 'dp'), may hold values from -0.21875 to 0.21875
- second_norm_gain: float32 [2048], replicated, may hold values from 0.1 to 1.9
- w_glu_gate: bfloat16 [2048, 3456], P('dp', 'mp'), may hold values from -0.125 to 0.125
- w_glu_up: bfloat16 [2048, 3456], P('dp', 'mp'), may hold values from -0.125 to 0.125
- w_down: bfloat16 [3456, 2048], P('mp', 'dp'), may hold values from -0.21875 to 0.21875
- cotangent: bfloat16 [8192, 2048], P(('dp', 'mp')), may hold values from -9 to 9
Outputs:
- outputs: bfloat16 [8192, 2048], P(('dp', 'mp'))
- input_gradient: float32 [8192, 2048], P(('dp', 'mp'))
- grad_norm1_gain: float32 [2048], replicated
- grad_w_query: float32 [2048, 2048], P('dp', 'mp')
- grad_w_key: float32 [2048, 2048], P('dp', 'mp')
- grad_w_value: float32 [2048, 3456], P('dp', 'mp')
- grad_w_gate: float32 [2048, 3456], P('dp', 'mp')
- grad_w_out: float32 [3456, 2048], P('mp', 'dp')
- grad_norm2_gain: float32 [2048], replicated
- grad_w_glu_gate: float32 [2048, 3456], P('dp', 'mp')
- grad_w_glu_up: float32 [2048, 3456], P('dp', 'mp')
- grad_w_down: float32 [3456, 2048], P('mp', 'dp')
Inputs may be any that keep to these rules, and one draw needn't show every extreme that they name: `segments`: within a sequence the document numbers never fall; each document holds 1 to 512 tokens and one holds exactly 512.
All inputs are finite; a program needn't handle non-finite values.
Results may differ from a plain program's by a relative error of at most 0.024.
Values may be sent and summed in bfloat16 or wider, within the bound.
A program may use at most 256 MiB of HBM per device.

v0:
```python
import jax
import jax.numpy as jnp
from jax import lax
from jax.sharding import PartitionSpec as P

H = 8
HK = 256
HV = 432
LEN = 1024


epsilon = 1e-05
group_epsilon = 1.0


def apply_layer_norm(values_in, offset):
    centre = jnp.mean(values_in, axis=-1, keepdims=True)
    centred = values_in - centre
    variance = jnp.mean(centred * centred, axis=-1, keepdims=True)
    scaling = lax.rsqrt(variance + offset)
    return (centred * scaling, scaling)


def norm_backward_rule(grad_hat, normed_hat, scaling):
    first_mean = jnp.mean(grad_hat, axis=-1, keepdims=True)
    second_mean = jnp.mean(grad_hat * normed_hat, axis=-1, keepdims=True)
    return scaling * (grad_hat - first_mean - normed_hat * second_mean)


def glu_act(gate_pre, up_pre):
    return jax.nn.gelu(gate_pre, approximate=True) * up_pre


def contract_last(left_side, right_side):
    return lax.dot_general(
        left_side, right_side, (((1,), (1,)), ((), ())), preferred_element_type=jnp.float32
    )


def contract_first(left_side, right_side):
    return lax.dot_general(
        left_side, right_side, (((0,), (0,)), ((), ())), preferred_element_type=jnp.float32
    )


def decay_mask(seg_row, head_start, head_count):
    places = jnp.arange(LEN)
    distance = places[:, None] - places[None, :]
    allowed = (distance >= 0) & (seg_row[:, None] == seg_row[None, :])
    heads = (head_start + jnp.arange(head_count)).astype(jnp.float32)
    log_gamma = jnp.log1p(-jnp.exp2(-5.0 - heads))
    exponent = jnp.where(
        allowed[None], distance[None].astype(jnp.float32) * log_gamma[:, None, None], 0.0
    )
    return jnp.where(allowed[None], jnp.exp(exponent), 0.0)


def retain_weights(query_heads, key_heads, mask):
    scores = (
        jnp.einsum("thk,shk->hts", query_heads, key_heads, preferred_element_type=jnp.float32)
        * mask
    )
    return scores.astype(jnp.bfloat16)


def retain(query_heads, key_heads, value_heads, mask):
    weights = retain_weights(query_heads, key_heads, mask)
    return jnp.einsum("hts,shv->thv", weights, value_heads, preferred_element_type=jnp.float32)


def retain_back(query_heads, key_heads, value_heads, mask, grad_out):
    weights = retain_weights(query_heads, key_heads, mask)
    grad_value = jnp.einsum(
        "hts,thv->shv", weights, grad_out, preferred_element_type=jnp.float32
    ).astype(jnp.bfloat16)
    grad_weights = jnp.einsum(
        "thv,shv->hts", grad_out, value_heads, preferred_element_type=jnp.float32
    )
    grad_scores = (grad_weights * mask).astype(jnp.bfloat16)
    grad_query = jnp.einsum(
        "hts,shk->thk", grad_scores, key_heads, preferred_element_type=jnp.float32
    ).astype(jnp.bfloat16)
    grad_key = (
        jnp.einsum("hts,thk->shk", grad_scores, query_heads, preferred_element_type=jnp.float32)
        * HK ** (-0.5)
    ).astype(jnp.bfloat16)
    return (grad_query, grad_key, grad_value)


def body(
    inputs,
    segments,
    first_norm_gain,
    w_query,
    w_key,
    w_value,
    w_gate,
    w_out,
    second_norm_gain,
    w_glu_gate,
    w_glu_up,
    w_down,
    cotangent,
):
    local_heads = H // lax.axis_size("mp")
    head_start = lax.axis_index("mp") * local_heads
    gathered = (
        lax.all_gather(w_query, "dp", axis=0, tiled=True),
        lax.all_gather(w_key, "dp", axis=0, tiled=True),
        lax.all_gather(w_value, "dp", axis=0, tiled=True),
        lax.all_gather(w_gate, "dp", axis=0, tiled=True),
        lax.all_gather(w_out, "dp", axis=1, tiled=True),
        lax.all_gather(w_glu_gate, "dp", axis=0, tiled=True),
        lax.all_gather(w_glu_up, "dp", axis=0, tiled=True),
        lax.all_gather(w_down, "dp", axis=1, tiled=True),
    )
    (
        query_weight,
        key_weight,
        value_weight,
        gate_weight,
        out_weight,
        glu_gate_weight,
        glu_up_weight,
        down_weight,
    ) = gathered
    inputs_float = inputs.astype(jnp.float32)
    first_standardized, first_inverse_scale = apply_layer_norm(inputs_float, epsilon)
    first_normed_rows = (first_standardized * first_norm_gain).astype(jnp.bfloat16)
    rows_one = lax.all_gather(first_normed_rows, "mp", axis=0, tiled=True)
    token_count = rows_one.shape[0]
    seq_count = token_count // LEN
    query_all = jnp.dot(rows_one, query_weight, preferred_element_type=jnp.float32).astype(
        jnp.bfloat16
    )
    key_all = (
        jnp.dot(rows_one, key_weight, preferred_element_type=jnp.float32) * HK ** (-0.5)
    ).astype(jnp.bfloat16)
    value_all = jnp.dot(rows_one, value_weight, preferred_element_type=jnp.float32).astype(
        jnp.bfloat16
    )
    gate_pre = jnp.dot(rows_one, gate_weight, preferred_element_type=jnp.float32)
    query_heads = query_all.reshape(seq_count, LEN, local_heads, HK)
    key_heads = key_all.reshape(seq_count, LEN, local_heads, HK)
    value_heads = value_all.reshape(seq_count, LEN, local_heads, HV)

    def forward_seq(item):
        query_seq, key_seq, value_seq, seg_row = item
        return retain(query_seq, key_seq, value_seq, decay_mask(seg_row, head_start, local_heads))

    retained = lax.map(forward_seq, (query_heads, key_heads, value_heads, segments))
    normalized, scale_group = apply_layer_norm(retained, group_epsilon)
    normal_flat = normalized.reshape(token_count, local_heads * HV)
    swish = jax.nn.silu(gate_pre)
    gated = (swish * normal_flat).astype(jnp.bfloat16)
    attn_part = jnp.dot(gated, out_weight, preferred_element_type=jnp.float32)
    middle_state = inputs_float + lax.psum_scatter(
        attn_part.astype(jnp.bfloat16), "mp", scatter_dimension=0, tiled=True
    ).astype(jnp.float32)
    second_standardized, second_inverse_scale = apply_layer_norm(middle_state, epsilon)
    second_normed_rows = (second_standardized * second_norm_gain).astype(jnp.bfloat16)
    rows_two = lax.all_gather(second_normed_rows, "mp", axis=0, tiled=True)
    glu_gate = jnp.dot(rows_two, glu_gate_weight, preferred_element_type=jnp.float32)
    glu_up = jnp.dot(rows_two, glu_up_weight, preferred_element_type=jnp.float32)
    hidden = glu_act(glu_gate, glu_up).astype(jnp.bfloat16)
    mlp_part = jnp.dot(hidden, down_weight, preferred_element_type=jnp.float32)
    outputs = (
        middle_state
        + lax.psum_scatter(
            mlp_part.astype(jnp.bfloat16), "mp", scatter_dimension=0, tiled=True
        ).astype(jnp.float32)
    ).astype(jnp.bfloat16)
    regathered = (
        lax.all_gather(w_query, "dp", axis=0, tiled=True),
        lax.all_gather(w_key, "dp", axis=0, tiled=True),
        lax.all_gather(w_value, "dp", axis=0, tiled=True),
        lax.all_gather(w_gate, "dp", axis=0, tiled=True),
        lax.all_gather(w_out, "dp", axis=1, tiled=True),
        lax.all_gather(w_glu_gate, "dp", axis=0, tiled=True),
        lax.all_gather(w_glu_up, "dp", axis=0, tiled=True),
        lax.all_gather(w_down, "dp", axis=1, tiled=True),
    )
    (
        query_weight,
        key_weight,
        value_weight,
        gate_weight,
        out_weight,
        glu_gate_weight,
        glu_up_weight,
        down_weight,
    ) = regathered
    rows_one, rows_two = (
        lax.all_gather(first_normed_rows, "mp", axis=0, tiled=True),
        lax.all_gather(second_normed_rows, "mp", axis=0, tiled=True),
    )
    cot_rows = lax.all_gather(cotangent, "mp", axis=0, tiled=True)
    d_hidden = contract_last(cot_rows, down_weight)
    unused, pullback = jax.vjp(glu_act, glu_gate, glu_up)
    d_glu_gate, d_glu_up = pullback(d_hidden)
    d_glu_gate = d_glu_gate.astype(jnp.bfloat16)
    d_glu_up = d_glu_up.astype(jnp.bfloat16)
    grad_w_down = contract_first(hidden, cot_rows)
    grad_w_glu_gate = contract_first(rows_two, d_glu_gate)
    grad_w_glu_up = contract_first(rows_two, d_glu_up)
    mlp_input_part = contract_last(d_glu_gate, glu_gate_weight) + contract_last(
        d_glu_up, glu_up_weight
    )
    second_normed_gradient = lax.psum_scatter(
        mlp_input_part.astype(jnp.bfloat16), "mp", scatter_dimension=0, tiled=True
    ).astype(jnp.float32)
    second_gain_gradient = jnp.sum(second_standardized * second_normed_gradient, axis=0)
    middle_gradient = cotangent.astype(jnp.float32) + norm_backward_rule(
        second_normed_gradient * second_norm_gain, second_standardized, second_inverse_scale
    )
    d_mid_round = middle_gradient.astype(jnp.bfloat16)
    mid_rows = lax.all_gather(d_mid_round, "mp", axis=0, tiled=True)
    grad_w_out = contract_first(gated, mid_rows)
    d_gated = contract_last(mid_rows, out_weight)
    sigmoid_gate = jax.nn.sigmoid(gate_pre)
    d_gate_pre = (
        d_gated * normal_flat * (sigmoid_gate + gate_pre * sigmoid_gate * (1.0 - sigmoid_gate))
    ).astype(jnp.bfloat16)
    d_normalized = (d_gated * swish).reshape(seq_count, LEN, local_heads, HV)
    d_retained = norm_backward_rule(d_normalized, normalized, scale_group).astype(jnp.bfloat16)

    def backward_seq(item):
        query_seq, key_seq, value_seq, seg_row, grad_seq = item
        return retain_back(
            query_seq, key_seq, value_seq, decay_mask(seg_row, head_start, local_heads), grad_seq
        )

    d_query, d_key, d_value = lax.map(
        backward_seq, (query_heads, key_heads, value_heads, segments, d_retained)
    )
    d_query = d_query.reshape(token_count, local_heads * HK)
    d_key = d_key.reshape(token_count, local_heads * HK)
    d_value = d_value.reshape(token_count, local_heads * HV)
    grad_w_query = contract_first(rows_one, d_query)
    grad_w_key = contract_first(rows_one, d_key)
    grad_w_value = contract_first(rows_one, d_value)
    grad_w_gate = contract_first(rows_one, d_gate_pre)
    attn_input_part = (
        contract_last(d_query, query_weight)
        + contract_last(d_key, key_weight)
        + contract_last(d_value, value_weight)
        + contract_last(d_gate_pre, gate_weight)
    )
    first_normed_gradient = lax.psum_scatter(
        attn_input_part.astype(jnp.bfloat16), "mp", scatter_dimension=0, tiled=True
    ).astype(jnp.float32)
    first_gain_gradient = jnp.sum(first_standardized * first_normed_gradient, axis=0)
    input_gradient = middle_gradient + norm_backward_rule(
        first_normed_gradient * first_norm_gain, first_standardized, first_inverse_scale
    )
    summed = (
        lax.psum_scatter(
            grad_w_query.astype(jnp.bfloat16), "dp", scatter_dimension=0, tiled=True
        ).astype(jnp.float32),
        lax.psum_scatter(
            grad_w_key.astype(jnp.bfloat16), "dp", scatter_dimension=0, tiled=True
        ).astype(jnp.float32),
        lax.psum_scatter(
            grad_w_value.astype(jnp.bfloat16), "dp", scatter_dimension=0, tiled=True
        ).astype(jnp.float32),
        lax.psum_scatter(
            grad_w_gate.astype(jnp.bfloat16), "dp", scatter_dimension=0, tiled=True
        ).astype(jnp.float32),
        lax.psum_scatter(
            grad_w_out.astype(jnp.bfloat16), "dp", scatter_dimension=1, tiled=True
        ).astype(jnp.float32),
        lax.psum_scatter(
            grad_w_glu_gate.astype(jnp.bfloat16), "dp", scatter_dimension=0, tiled=True
        ).astype(jnp.float32),
        lax.psum_scatter(
            grad_w_glu_up.astype(jnp.bfloat16), "dp", scatter_dimension=0, tiled=True
        ).astype(jnp.float32),
        lax.psum_scatter(
            grad_w_down.astype(jnp.bfloat16), "dp", scatter_dimension=1, tiled=True
        ).astype(jnp.float32),
    )
    gain_first, gain_second = lax.psum((first_gain_gradient, second_gain_gradient), ("dp", "mp"))
    return (
        outputs,
        input_gradient,
        gain_first,
        summed[0],
        summed[1],
        summed[2],
        summed[3],
        summed[4],
        gain_second,
        summed[5],
        summed[6],
        summed[7],
    )


def solution(mesh):
    placed = (
        P(("dp", "mp"), None),
        P("dp", None),
        P(),
        P("dp", "mp"),
        P("dp", "mp"),
        P("dp", "mp"),
        P("dp", "mp"),
        P("mp", "dp"),
        P(),
        P("dp", "mp"),
        P("dp", "mp"),
        P("mp", "dp"),
        P(("dp", "mp"), None),
    )
    return jax.shard_map(
        body,
        mesh=mesh,
        in_specs=placed,
        out_specs=(
            P(("dp", "mp"), None),
            P(("dp", "mp"), None),
            P(),
            P("dp", "mp"),
            P("dp", "mp"),
            P("dp", "mp"),
            P("dp", "mp"),
            P("mp", "dp"),
            P(),
            P("dp", "mp"),
            P("dp", "mp"),
            P("mp", "dp"),
        ),
        check_vma=False,
    )
```

profile of v0, /device:TPU:0, one launch (start us, length us, event | category | flops | bytes accessed | tf_op | source)
XLA Modules:
  0.0 1370.5 jit_solution(15056165965562661758)
XLA Ops:
  19.6 20.8 %all-gather.21.cloned.1.call-done = bf16[2048,512]{1,0:T(8,128)(2,1)} async-done(((bf16[256,512]{1,0:T(8,128)(2,1)}), bf16[2048,512]{1,0:T(8,128)(2,1)}) %all-gather.21.cloned.1.call-update) | async-done | bytes 2097168 | tf_op jit(solution)/shard_map/all_gather | solution.py:109
  40.4 82.9 %all-gather.13.cloned.1.call-done = bf16[1024,2048]{1,0:T(8,128)(2,1)} async-done(((bf16[256,2048]{1,0:T(8,128)(2,1)}), bf16[1024,2048]{1,0:T(8,128)(2,1)}) %all-gather.13.cloned.1.call-update) | async-done | bytes 4194320 | tf_op jit(solution)/shard_map/all_gather | solution.py:130
  128.6 22.9 %all-gather.19.cloned.1.call-done = bf16[2048,512]{1,0:T(8,128)(2,1)} async-done(((bf16[256,512]{1,0:T(8,128)(2,1)}), bf16[2048,512]{1,0:T(8,128)(2,1)}) %all-gather.19.cloned.1.call-update) | async-done | bytes 2097168 | tf_op jit(solution)/shard_map/all_gather | solution.py:108
  162.5 25.2 %all-gather.17.cloned.1.call-done = bf16[2048,864]{0,1:T(8,128)(2,1)} async-done(((bf16[256,864]{0,1:T(8,128)(2,1)}), bf16[2048,864]{0,1:T(8,128)(2,1)}) %all-gather.17.cloned.1.call-update) | async-done | bytes 3538960 | tf_op jit(solution)/shard_map/all_gather | solution.py:110
  201.1 22.8 %all-gather.15.cloned.1.call-done = bf16[2048,864]{0,1:T(8,128)(2,1)} async-done(((bf16[256,864]{0,1:T(8,128)(2,1)}), bf16[2048,864]{0,1:T(8,128)(2,1)}) %all-gather.15.cloned.1.call-update) | async-done | bytes 3538960 | tf_op jit(solution)/shard_map/all_gather | solution.py:111
  223.9 10.2 fusion.10
  234.2 26.0 %all-gather.23.cloned.1.call-done = bf16[864,2048]{1,0:T(8,128)(2,1)} async-done(((bf16[864,256]{1,0:T(8,128)(2,1)}), bf16[864,2048]{1,0:T(8,128)(2,1)}) %all-gather.23.cloned.1.call-update) | async-done | bytes 3538960 | tf_op jit(solution)/shard_map/all_gather | solution.py:112
  269.5 76.2 %reduce-scatter.13.cloned.1.call-done = bf16[256,2048]{1,0:T(8,128)(2,1)} async-done(((bf16[1024,2048]{1,0:T(8,128)(2,1)}), bf16[256,2048]{1,0:T(8,128)(2,1)}) %reduce-scatter.13.cloned.1.call-update) | async-done | bytes 1048592 | tf_op jit(solution)/shard_map/reduce_scatter | solution.py:157
  352.5 30.0 %all-gather.29.cloned.1.call-done = bf16[2048,864]{0,1:T(8,128)(2,1)} async-done(((bf16[256,864]{0,1:T(8,128)(2,1)}), bf16[2048,864]{0,1:T(8,128)(2,1)}) %all-gather.29.cloned.1.call-update) | async-done | bytes 3538960 | tf_op jit(solution)/shard_map/all_gather | solution.py:114
  382.5 82.9 %all-gather.25.cloned.1.call-done = bf16[1024,2048]{1,0:T(8,128)(2,1)} async-done(((bf16[256,2048]{1,0:T(8,128)(2,1)}), bf16[1024,2048]{1,0:T(8,128)(2,1)}) %all-gather.25.cloned.1.call-update) | async-done | bytes 4194320 | tf_op jit(solution)/shard_map/all_gather | solution.py:162
  465.4 8.9 fusion.42
  474.3 25.8 %all-gather.27.cloned.1.call-done = bf16[2048,864]{0,1:T(8,128)(2,1)} async-done(((bf16[256,864]{0,1:T(8,128)(2,1)}), bf16[2048,864]{0,1:T(8,128)(2,1)}) %all-gather.27.cloned.1.call-update) | async-done | bytes 3538960 | tf_op jit(solution)/shard_map/all_gather | solution.py:113
  500.1 9.0 fusion.41
  509.1 27.4 %all-gather.31.cloned.1.call-done = bf16[864,2048]{1,0:T(8,128)(2,1)} async-done(((bf16[864,256]{1,0:T(8,128)(2,1)}), bf16[864,2048]{1,0:T(8,128)(2,1)}) %all-gather.31.cloned.1.call-update) | async-done | bytes 3538960 | tf_op jit(solution)/shard_map/all_gather | solution.py:115
  536.5 82.2 %all-gather.33.cloned.1.call-done = bf16[1024,2048]{1,0:T(8,128)(2,1)} async-done(((bf16[256,2048]{1,0:T(8,128)(2,1)}), bf16[1024,2048]{1,0:T(8,128)(2,1)}) %all-gather.33.cloned.1.call-update) | async-done | bytes 4194320 | tf_op jit(solution)/shard_map/all_gather | solution.py:197
  618.7 12.0 multiply_convert_fusion.3
  642.0 75.4 %reduce-scatter.17.cloned.1.call-done = bf16[256,2048]{1,0:T(8,128)(2,1)} async-done(((bf16[1024,2048]{1,0:T(8,128)(2,1)}), bf16[256,2048]{1,0:T(8,128)(2,1)}) %reduce-scatter.17.cloned.1.call-update) | async-done | bytes 1048592 | tf_op jit(solution)/shard_map/reduce_scatter | solution.py:209
  730.7 8.7 convolution_convert_fusion.2
  748.3 55.0 %all-gather.35.cloned.1.call-done = bf16[1024,2048]{1,0:T(8,128)(2,1)} async-done(((bf16[256,2048]{1,0:T(8,128)(2,1)}), bf16[1024,2048]{1,0:T(8,128)(2,1)}) %all-gather.35.cloned.1.call-update) | async-done | bytes 4194320 | tf_op jit(solution)/shard_map/all_gather | solution.py:217
  803.3 11.4 fusion.38
  860.6 8.7 convolution_convert_fusion.4
  891.0 13.0 add_convert_fusion
  904.3 9.2 convolution_convert_fusion
  917.6 37.9 %reduce-scatter.31.cloned.1.call-done = bf16[256,864]{0,1:T(8,128)(2,1)} async-done(((bf16[2048,864]{0,1:T(8,128)(2,1)}), bf16[256,864]{0,1:T(8,128)(2,1)}) %reduce-scatter.31.cloned.1.call-update) | async-done | bytes 442384 | tf_op jit(solution)/shard_map/reduce_scatter | solution.py:272
  957.5 42.3 %reduce-scatter.23.cloned.1.call-done = bf16[256,512]{1,0:T(8,128)(2,1)} async-done(((bf16[2048,512]{1,0:T(8,128)(2,1)}), bf16[256,512]{1,0:T(8,128)(2,1)}) %reduce-scatter.23.cloned.1.call-update) | async-done | bytes 262160 | tf_op jit(solution)/shard_map/reduce_scatter | solution.py:260
  1001.6 43.2 %reduce-scatter.21.cloned.1.call-done = bf16[256,512]{1,0:T(8,128)(2,1)} async-done(((bf16[2048,512]{1,0:T(8,128)(2,1)}), bf16[256,512]{1,0:T(8,128)(2,1)}) %reduce-scatter.21.cloned.1.call-update) | async-done | bytes 262160 | tf_op jit(solution)/shard_map/reduce_scatter | solution.py:257
  1046.6 49.4 %reduce-scatter.29.cloned.1.call-done = bf16[864,256]{1,0:T(8,128)(2,1)} async-done(((bf16[864,2048]{1,0:T(8,128)(2,1)}), bf16[864,256]{1,0:T(8,128)(2,1)}) %reduce-scatter.29.cloned.1.call-update) | async-done | bytes 442384 | tf_op jit(solution)/shard_map/reduce_scatter | solution.py:269
  1098.0 49.4 %reduce-scatter.25.cloned.1.call-done = bf16[256,864]{0,1:T(8,128)(2,1)} async-done(((bf16[2048,864]{0,1:T(8,128)(2,1)}), bf16[256,864]{0,1:T(8,128)(2,1)}) %reduce-scatter.25.cloned.1.call-update) | async-done | bytes 442384 | tf_op jit(solution)/shard_map/reduce_scatter | solution.py:263
  1149.4 49.4 %reduce-scatter.27.cloned.1.call-done = bf16[256,864]{0,1:T(8,128)(2,1)} async-done(((bf16[2048,864]{0,1:T(8,128)(2,1)}), bf16[256,864]{0,1:T(8,128)(2,1)}) %reduce-scatter.27.cloned.1.call-update) | async-done | bytes 442384 | tf_op jit(solution)/shard_map/reduce_scatter | solution.py:266
  1200.8 77.1 %reduce-scatter.19.cloned.1.call-done = bf16[256,2048]{1,0:T(8,128)(2,1)} async-done(((bf16[1024,2048]{1,0:T(8,128)(2,1)}), bf16[256,2048]{1,0:T(8,128)(2,1)}) %reduce-scatter.19.cloned.1.call-update) | async-done | bytes 1048592 | tf_op jit(solution)/shard_map/reduce_scatter | solution.py:249
  1280.2 46.1 %all-reduce = (f32[2048]{0:T(1024)}, f32[2048]{0:T(1024)}) all-reduce(f32[2048]{0:T(1024)S(1)} %get-tuple-element.57, f32[2048]{0:T(1024)S(1)} %get-tuple-element.55), channel_id=1, replica_groups=mesh['dp'=8,'mp'=4] {'dp','mp'}, use_global_device_ids=true, to_apply=%region_17.18 | all-reduce | flops 4096 | bytes 32768 | tf_op jit(solution)/shard_map/psum | solution.py:282
  1326.2 32.3 %reduce-scatter.15.cloned.1.call-done = bf16[256,2048]{1,0:T(8,128)(2,1)} async-done(((bf16[1024,2048]{1,0:T(8,128)(2,1)}), bf16[256,2048]{1,0:T(8,128)(2,1)}) %reduce-scatter.15.cloned.1.call-update) | async-done | bytes 1048592 | tf_op jit(solution)/shard_map/reduce_scatter | solution.py:169
  (191 shorter events, 181.4 us)
Async XLA Ops:
  7.2 33.2 %all-gather.21.cloned.1.call-start = ((), (), s32[]{:S(2)}) async-start(), calls=%async_computation.16 | async-start | bytes 2359296 | tf_op jit(solution)/shard_map/all_gather | solution.py:109
  7.9 115.4 %all-gather.13.cloned.1.call-start = ((), (), s32[]{:S(2)}) async-start(), calls=%async_computation.12 | async-start | bytes 5242880 | tf_op jit(solution)/shard_map/all_gather | solution.py:130
  13.7 137.8 %all-gather.19.cloned.1.call-start = ((), (), s32[]{:S(2)}) async-start(), calls=%async_computation.15 | async-start | bytes 2359296 | tf_op jit(solution)/shard_map/all_gather | solution.py:108
  14.4 173.3 %all-gather.17.cloned.1.call-start = ((), (), s32[]{:S(2)}) async-start(), calls=%async_computation.14 | async-start | bytes 3981312 | tf_op jit(solution)/shard_map/all_gather | solution.py:110
  15.0 208.9 %all-gather.15.cloned.1.call-start = ((), (), s32[]{:S(2)}) async-start(), calls=%async_computation.13 | async-start | bytes 3981312 | tf_op jit(solution)/shard_map/all_gather | solution.py:111
  15.6 244.6 %all-gather.23.cloned.1.call-start = ((), (), s32[]{:S(2)}) async-start(), calls=%async_computation.17 | async-start | bytes 3981312 | tf_op jit(solution)/shard_map/all_gather | solution.py:112
  16.2 329.5 %reduce-scatter.13.cloned.1.call-start = ((), (), s32[]{:S(2)}) async-start(), calls=%async_computation.18 | async-start | bytes 5242880 | tf_op jit(solution)/shard_map/reduce_scatter | solution.py:157
  16.9 140.0 %copy-start.12 = (pred[1024,1024]{1,0:T(8,128)(4,1)}, pred[1024,1024]{1,0:T(8,128)(4,1)S(1)}, u32[]{:S(2)}) copy-start(pred[1024,1024]{1,0:T(8,128)(4,1)S(1)} %fusion.2) | copy-start | bytes 3145732
  128.6 28.4 %copy-start.32 = (bf16[1024,512]{0,1:T(8,128)(2,1)}, bf16[1024,512]{0,1:T(8,128)(2,1)S(1)}, u32[]{:S(2)}) copy-start(bf16[1024,512]{0,1:T(8,128)(2,1)S(1)} %multiply_convert_fusion.7) | copy-start | bytes 3145732
  268.7 77.0 %copy-start = (bf16[256,2048]{1,0:T(8,128)(2,1)S(1)}, bf16[256,2048]{1,0:T(8,128)(2,1)}, u32[]{:S(2)}) copy-start(bf16[256,2048]{1,0:T(8,128)(2,1)} %param.13) | copy-start | bytes 3145732
  268.7 80.4 %copy-start.14 = (f32[2048]{0:T(1024)S(1)}, f32[2048]{0:T(1024)}, u32[]{:S(2)}) copy-start(f32[2048]{0:T(1024)} %param.21) | copy-start | bytes 24580
  268.7 113.8 %all-gather.29.cloned.1.call-start = ((), (), s32[]{:S(2)}) async-start(), calls=%async_computation.21 | async-start | bytes 3981312 | tf_op jit(solution)/shard_map/all_gather | solution.py:114
  269.4 196.0 %all-gather.25.cloned.1.call-start = ((), (), s32[]{:S(2)}) async-start(), calls=%async_computation.19 | async-start | bytes 5242880 | tf_op jit(solution)/shard_map/all_gather | solution.py:162
  350.5 149.6 %all-gather.27.cloned.1.call-start = ((), (), s32[]{:S(2)}) async-start(), calls=%async_computation.20 | async-start | bytes 3981312 | tf_op jit(solution)/shard_map/all_gather | solution.py:113
  351.1 185.4 %all-gather.31.cloned.1.call-start = ((), (), s32[]{:S(2)}) async-start(), calls=%async_computation.22 | async-start | bytes 3981312 | tf_op jit(solution)/shard_map/all_gather | solution.py:115
  351.9 266.8 %all-gather.33.cloned.1.call-start = ((), (), s32[]{:S(2)}) async-start(), calls=%async_computation.24 | async-start | bytes 5242880 | tf_op jit(solution)/shard_map/all_gather | solution.py:197
  352.4 364.9 %reduce-scatter.17.cloned.1.call-start = ((), (), s32[]{:S(2)}) async-start(), calls=%async_computation.25 | async-start | bytes 5242880 | tf_op jit(solution)/shard_map/reduce_scatter | solution.py:209
  641.9 77.9 %copy-start.4 = (bf16[256,2048]{1,0:T(8,128)(2,1)S(1)}, bf16[256,2048]{1,0:T(8,128)(2,1)}, u32[]{:S(2)}) copy-start(bf16[256,2048]{1,0:T(8,128)(2,1)} %param.25) | copy-start | bytes 3145732
  641.9 161.4 %all-gather.35.cloned.1.call-start = ((), (), s32[]{:S(2)}) async-start(), calls=%async_computation.26 | async-start | bytes 5242880 | tf_op jit(solution)/shard_map/all_gather | solution.py:217
  721.9 191.6 %reduce-scatter.35.cloned.1.call-start = ((), (), s32[]{:S(2)}) async-start(), calls=%async_computation.35 | async-start | bytes 3981312 | tf_op jit(solution)/shard_map/reduce_scatter | solution.py:278
  730.6 184.9 %reduce-scatter.33.cloned.1.call-start = ((), (), s32[]{:S(2)}) async-start(), calls=%async_computation.34 | async-start | bytes 3981312 | tf_op jit(solution)/shard_map/reduce_scatter | solution.py:275
  739.4 216.1 %reduce-scatter.31.cloned.1.call-start = ((), (), s32[]{:S(2)}) async-start(), calls=%async_computation.33 | async-start | bytes 3981312 | tf_op jit(solution)/shard_map/reduce_scatter | solution.py:272
  747.9 251.9 %reduce-scatter.23.cloned.1.call-start = ((), (), s32[]{:S(2)}) async-start(), calls=%async_computation.29 | async-start | bytes 2359296 | tf_op jit(solution)/shard_map/reduce_scatter | solution.py:260
  831.3 213.5 %reduce-scatter.21.cloned.1.call-start = ((), (), s32[]{:S(2)}) async-start(), calls=%async_computation.28 | async-start | bytes 2359296 | tf_op jit(solution)/shard_map/reduce_scatter | solution.py:257
  840.3 255.7 %reduce-scatter.29.cloned.1.call-start = ((), (), s32[]{:S(2)}) async-start(), calls=%async_computation.32 | async-start | bytes 3981312 | tf_op jit(solution)/shard_map/reduce_scatter | solution.py:269
  848.8 298.6 %reduce-scatter.25.cloned.1.call-start = ((), (), s32[]{:S(2)}) async-start(), calls=%async_computation.30 | async-start | bytes 3981312 | tf_op jit(solution)/shard_map/reduce_scatter | solution.py:263
  860.3 338.5 %reduce-scatter.27.cloned.1.call-start = ((), (), s32[]{:S(2)}) async-start(), calls=%async_computation.31 | async-start | bytes 3981312 | tf_op jit(solution)/shard_map/reduce_scatter | solution.py:266
  869.4 408.6 %reduce-scatter.19.cloned.1.call-start = ((), (), s32[]{:S(2)}) async-start(), calls=%async_computation.27 | async-start | bytes 5242880 | tf_op jit(solution)/shard_map/reduce_scatter | solution.py:249
  904.0 454.5 %reduce-scatter.15.cloned.1.call-start = ((), (), s32[]{:S(2)}) async-start(), calls=%async_computation.23 | async-start | bytes 5242880 | tf_op jit(solution)/shard_map/reduce_scatter | solution.py:169
  917.6 360.3 %copy-start.15 = (f32[2048]{0:T(1024)S(1)}, f32[2048]{0:T(1024)}, u32[]{:S(2)}) copy-start(f32[2048]{0:T(1024)} %param.15) | copy-start | bytes 24580
  917.6 360.3 %copy-start.17 = (f32[256]{0:T(256)S(1)}, f32[256]{0:T(256)}, u32[]{:S(2)}) copy-start(f32[256]{0:T(256)} %copy-done.16) | copy-start | bytes 3076
  917.6 360.3 %copy-start.20 = (f32[256]{0:T(256)S(1)}, f32[256]{0:T(256)}, u32[]{:S(2)}) copy-start(f32[256]{0:T(256)} %copy-done.19) | copy-start | bytes 3076
  (34 other events, 189.5 us)
Sparse Core Ops, SparseCore 0:
  9.9 30.4 all-gather.20
  42.5 80.7 all-gather.12
  125.2 26.2 all-gather.18
  153.2 34.4 all-gather.16
  189.5 34.4 all-gather.14
  225.7 34.4 all-gather.22
  268.8 76.7 reduce-scatter.12
  347.5 34.9 all-gather.28
  384.6 80.7 all-gather.24
  467.1 32.9 all-gather.26
  502.0 34.4 all-gather.30
  537.9 80.7 all-gather.32
  642.0 75.2 reduce-scatter.16
  722.0 81.2 all-gather.34
  806.7 46.3 reduce-scatter.34
  856.4 47.8 reduce-scatter.32
  907.6 47.8 reduce-scatter.30
  958.7 41.0 reduce-scatter.22
  1003.6 41.1 reduce-scatter.20
  1048.1 47.8 reduce-scatter.28
  1099.5 47.8 reduce-scatter.24
  1150.9 47.8 reduce-scatter.26
  1201.1 76.7 reduce-scatter.18
  1280.1 78.3 reduce-scatter.14
where the time goes:
time: 1380 us; the launch traced here: 1370 us
  waiting for transfers between devices  1040 us (75%)
  matrix products  209 us (15%)
  blocking collectives  46.1 us (3%)
  other arithmetic  45.4 us (3%)
  between operations  15.3 us (1%)
    all_gather x1, waiting for transfers between devices, body(): rows_two = lax.all_gather(second_normed_rows, 'mp', axis=0, tiled=True)  82.9 us
    all_gather x1, waiting for transfers between devices, body(): rows_one = lax.all_gather(first_normed_rows, 'mp', axis=0, tiled=True)  82.9 us
    all_gather x1, waiting for transfers between devices, body(): cot_rows = lax.all_gather(cotangent, 'mp', axis=0, tiled=True)  82.2 us
    reduce_scatter x1, waiting for transfers between devices, body(): lax.psum_scatter(attn_input_part.astype(jnp.bfloat16), 'mp', scatter_dime...  77.1 us
    reduce_scatter x1, waiting for transfers between devices, body(): lax.psum_scatter(attn_part.astype(jnp.bfloat16), 'mp', scatter_dimension=...  76.2 us
    reduce_scatter x1, waiting for transfers between devices, body(): lax.psum_scatter(mlp_input_part.astype(jnp.bfloat16), 'mp', scatter_dimen...  75.4 us
    dot_general x8, matrix products, contract_last(): lax.dot_general(left_side, right_side, (((1,), (1,)), ((), ())), preferre...  69.1 us
    dot_general x8, matrix products, contract_first(): lax.dot_general(left_side, right_side, (((0,), (0,)), ((), ())), preferre...  55.5 us
  transfers between devices with their start and end apart: 24, of which 22 were waited for; matrix products, arithmetic and copies ran while one was open for 16% of the time, Pallas kernels for 0%

commit v1 on v0

v1 whole, which is shorter than its diff:
```python
import jax
import jax.numpy as jnp
from jax import lax
from jax.sharding import PartitionSpec as P

H = 8
HK = 256
HV = 432
LEN = 1024
CHUNKS = 2

epsilon = 1e-05
group_epsilon = 1.0
BF = jnp.bfloat16
F32 = jnp.float32


def layer_norm(values_in, offset):
    centre = jnp.mean(values_in, axis=-1, keepdims=True)
    centred = values_in - centre
    variance = jnp.mean(centred * centred, axis=-1, keepdims=True)
    scaling = lax.rsqrt(variance + offset)
    return (centred * scaling, scaling)


def norm_back(grad_hat, normed_hat, scaling):
    first_mean = jnp.mean(grad_hat, axis=-1, keepdims=True)
    second_mean = jnp.mean(grad_hat * normed_hat, axis=-1, keepdims=True)
    return scaling * (grad_hat - first_mean - normed_hat * second_mean)


def glu_act(gate_pre, up_pre):
    return jax.nn.gelu(gate_pre, approximate=True) * up_pre


def dot_nt(a, b):
    return lax.dot_general(a, b, (((1,), (1,)), ((), ())), preferred_element_type=F32)


def dot_nn(a, b):
    return lax.dot_general(a, b, (((1,), (0,)), ((), ())), preferred_element_type=F32)


def dot_tn(a, b):
    return lax.dot_general(a, b, (((0,), (0,)), ((), ())), preferred_element_type=F32)


def line_gather(own, n, place):
    right, left = [None], [None]
    r = l = own
    for step in range(1, n):
        r = lax.ppermute(r, "mp", [(i, i + 1) for i in range(step - 1, n - 1)])
        l = lax.ppermute(l, "mp", [(i, i - 1) for i in range(1, n - step + 1)])
        right.append(r)
        left.append(l)
    return [own] + [jnp.where(place >= k, right[k], left[n - k]) for k in range(1, n)]


def line_scatter(slots, n):
    r = l = None
    for step in range(1, n):
        send_r, send_l = slots[step], slots[n - step]
        if r is not None:
            send_r = (send_r.astype(F32) + r.astype(F32)).astype(BF)
            send_l = (send_l.astype(F32) + l.astype(F32)).astype(BF)
        r = lax.ppermute(send_r, "mp", [(i, i + 1) for i in range(step)])
        l = lax.ppermute(send_l, "mp", [(i, i - 1) for i in range(n - step, n)])
    return slots[0].astype(F32) + r.astype(F32) + l.astype(F32)


def body(
    inputs,
    segments,
    first_norm_gain,
    w_query,
    w_key,
    w_value,
    w_gate,
    w_out,
    second_norm_gain,
    w_glu_gate,
    w_glu_up,
    w_down,
    cotangent,
):
    n = lax.axis_size("mp")
    place = lax.axis_index("mp")
    heads = H // n
    head_start = place * heads
    rows, width = inputs.shape
    piece = rows // CHUNKS
    per = n * piece
    nk, nv, nf = heads * HK, heads * HV, w_down.shape[0]

    pack_one = jnp.concatenate([w_query.T, w_key.T, w_value.T, w_gate.T], axis=0)
    weight_one = lax.all_gather(pack_one, "dp", axis=1, tiled=True)
    out_weight = lax.all_gather(w_out, "dp", axis=1, tiled=True)
    pack_two = jnp.concatenate([w_glu_gate.T, w_glu_up.T, w_down], axis=0)
    weight_two = lax.all_gather(pack_two, "dp", axis=1, tiled=True)
    glu_weight, down_weight = weight_two[: 2 * nf], weight_two[2 * nf :]

    def cut(array):
        return [array[h * piece : (h + 1) * piece] for h in range(CHUNKS)]

    def gather(block):
        return jnp.concatenate(line_gather(block, n, place), axis=0)

    def scatter(part):
        return line_scatter([part[k * piece : (k + 1) * piece] for k in range(n)], n)

    inputs_cut = [c.astype(F32) for c in cut(inputs)]
    first_hat, first_scale, first_rows = [], [], []
    for x in inputs_cut:
        hat, scale = layer_norm(x, epsilon)
        first_hat.append(hat)
        first_scale.append(scale)
        first_rows.append((hat * first_norm_gain).astype(BF))
    rows_one = jnp.concatenate([gather(block) for block in first_rows], axis=0)
    tokens = rows_one.shape[0]

    slot_shard = lax.rem(place - jnp.arange(n) + n, n)
    places = (
        slot_shard[None, :, None] * rows
        + jnp.arange(CHUNKS)[:, None, None] * piece
        + jnp.arange(piece)[None, None, :]
    ).reshape(tokens)
    seg = segments.reshape(n, CHUNKS, piece)[::-1]
    seg = lax.dynamic_slice_in_dim(jnp.concatenate([seg, seg], axis=0), n - 1 - place, n, axis=0)
    seg = seg.transpose(1, 0, 2).reshape(tokens)

    query_key = dot_nt(rows_one, weight_one[: 2 * nk]).astype(BF)
    value = dot_nt(rows_one, weight_one[2 * nk : 2 * nk + nv]).astype(BF)
    gate_pre = dot_nt(rows_one, weight_one[2 * nk + nv :])
    query = query_key[:, :nk].reshape(tokens, heads, HK)
    key = query_key[:, nk:].reshape(tokens, heads, HK)
    value = value.reshape(tokens, heads, HV)

    distance = places[:, None] - places[None, :]
    allowed = (distance >= 0) & (seg[:, None] == seg[None, :])
    log_gamma = jnp.log1p(-jnp.exp2(-5.0 - (head_start + jnp.arange(heads)).astype(F32)))
    exponent = jnp.where(
        allowed[None], distance[None].astype(F32) * log_gamma[:, None, None], 0.0
    )
    mask = jnp.where(allowed[None], jnp.exp(exponent), 0.0) * HK ** (-0.5)

    scores = (jnp.einsum("thk,shk->hts", query, key, preferred_element_type=F32) * mask).astype(BF)
    retained = jnp.einsum("hts,shv->thv", scores, value, preferred_element_type=F32)
    normalized, scale_group = layer_norm(retained, group_epsilon)
    normal_flat = normalized.reshape(tokens, nv)
    swish = jax.nn.silu(gate_pre)
    gated = (swish * normal_flat).astype(BF)

    cot_cut = cut(cotangent)
    cot_rows = [gather(c) for c in cot_cut]

    def group(array, h):
        return array[h * per : (h + 1) * per]

    outputs, second_gain, middle_grad = [], [], []
    rows_two, hidden_all, d_glu_all, mid_rows = [], [], [], []
    for h in range(CHUNKS):
        attn_part = dot_nn(group(gated, h), out_weight).astype(BF)
        middle = inputs_cut[h] + scatter(attn_part)
        hat, scale = layer_norm(middle, epsilon)
        rows_h = gather((hat * second_norm_gain).astype(BF))
        rows_two.append(rows_h)
        glu = dot_nt(rows_h, glu_weight)
        glu_gate, glu_up = glu[:, :nf], glu[:, nf:]
        d_hidden = dot_nt(cot_rows[h], down_weight)
        hidden, pullback = jax.vjp(glu_act, glu_gate, glu_up)
        hidden = hidden.astype(BF)
        d_glu = jnp.concatenate([d.astype(BF) for d in pullback(d_hidden)], axis=1)
        hidden_all.append(hidden)
        d_glu_all.append(d_glu)
        second_grad = scatter(dot_nn(d_glu, glu_weight).astype(BF))
        second_gain.append(jnp.sum(hat * second_grad, axis=0))
        grad_h = cot_cut[h].astype(F32) + norm_back(second_grad * second_norm_gain, hat, scale)
        middle_grad.append(grad_h)
        mid_rows.append(gather(grad_h.astype(BF)))
        outputs.append(middle + scatter(dot_nn(hidden, down_weight).astype(BF)))

    cot_all = jnp.concatenate(cot_rows, axis=0)
    grads_two = jnp.concatenate(
        [
            dot_tn(jnp.concatenate(d_glu_all, axis=0), jnp.concatenate(rows_two, axis=0)),
            dot_tn(jnp.concatenate(hidden_all, axis=0), cot_all),
        ],
        axis=0,
    ).astype(BF)
    summed_two = lax.psum_scatter(grads_two, "dp", scatter_dimension=1, tiled=True).astype(F32)

    mid_all = jnp.concatenate(mid_rows, axis=0)
    d_gated = dot_nt(mid_all, out_weight)
    sigmoid_gate = jax.nn.sigmoid(gate_pre)
    d_gate_pre = (
        d_gated * normal_flat * (sigmoid_gate + gate_pre * sigmoid_gate * (1.0 - sigmoid_gate))
    ).astype(BF)
    d_normalized = (d_gated * swish).reshape(tokens, heads, HV)
    d_retained = norm_back(d_normalized, normalized, scale_group).astype(BF)
    grads_out = jnp.concatenate(
        [dot_tn(gated, mid_all).astype(BF), dot_tn(d_gate_pre, rows_one).astype(BF)], axis=0
    )
    summed_out = lax.psum_scatter(grads_out, "dp", scatter_dimension=1, tiled=True).astype(F32)

    d_value = jnp.einsum("hts,thv->shv", scores, d_retained, preferred_element_type=F32).astype(BF)
    d_scores = (
        jnp.einsum("thv,shv->hts", d_retained, value, preferred_element_type=F32) * mask
    ).astype(BF)
    d_query = jnp.einsum("hts,shk->thk", d_scores, key, preferred_element_type=F32).astype(BF)
    d_key = jnp.einsum("hts,thk->shk", d_scores, query, preferred_element_type=F32).astype(BF)
    d_qkv = jnp.concatenate(
        [d_query.reshape(tokens, nk), d_key.reshape(tokens, nk), d_value.reshape(tokens, nv)], axis=1
    )
    grads_one = dot_tn(d_qkv, rows_one).astype(BF)
    summed_one = lax.psum_scatter(grads_one, "dp", scatter_dimension=1, tiled=True).astype(F32)

    d_one = jnp.concatenate([d_qkv, d_gate_pre], axis=1)
    input_gradient, first_gain = [], []
    for h in range(CHUNKS):
        first_grad = scatter(dot_nn(group(d_one, h), weight_one).astype(BF))
        first_gain.append(jnp.sum(first_hat[h] * first_grad, axis=0))
        input_gradient.append(
            middle_grad[h] + norm_back(first_grad * first_norm_gain, first_hat[h], first_scale[h])
        )

    gains = lax.psum(jnp.stack([sum(first_gain), sum(second_gain)]), ("dp", "mp"))
    return (
        jnp.concatenate(outputs, axis=0).astype(BF),
        jnp.concatenate(input_gradient, axis=0),
        gains[0],
        summed_one[:nk].T,
        summed_one[nk : 2 * nk].T,
        summed_one[2 * nk :].T,
        summed_out[nv:].T,
        summed_out[:nv],
        gains[1],
        summed_two[:nf].T,
        summed_two[nf : 2 * nf].T,
        summed_two[2 * nf :],
    )


def solution(mesh):
    split = P(("dp", "mp"), None)
    wide, tall = P("dp", "mp"), P("mp", "dp")
    return jax.shard_map(
        body,
        mesh=mesh,
        in_specs=(
            split, P("dp", None), P(), wide, wide, wide, wide, tall, P(), wide, wide, tall, split,
        ),
        out_specs=(
            split, split, P(), wide, wide, wide, wide, tall, P(), wide, wide, tall,
        ),
        check_vma=False,
    )
```

time: 1380 us -> 856 us (0.62)
  waiting for transfers between devices: 1040 us -> 283 us
  starting transfers between devices: 2.22 us -> 234 us
  matrix products: 209 us -> 159 us
  other arithmetic: 45.4 us -> 87.5 us
  local copies, waits for them, and re-layouts: 10.2 us -> 25.8 us
    reduce_scatter x12 -> x3, waiting for transfers between devices: 533 us -> 19.8 us  [the longest x1 19.8 us: body(): lax.psum_scatter(grads_two, 'dp', scatter_dimension=1, tiled=True)]
    all_gather x12 -> x3, waiting for transfers between devices: 504 us -> 0.01 us  [the longest x1 0.01 us: body(): weight_one = lax.all_gather(pack_one, 'dp', axis=1, tiled=True)]
    ppermute x0 -> x96, waiting for transfers between devices: none -> 262 us  [the longest x24 155 us: line_gather(): l = lax.ppermute(l, 'mp', [(i, i - 1) for i in range(1, n - step + 1)])]
    ppermute x0 -> x96, starting transfers between devices: none -> 233 us  [the longest x24 113 us: line_scatter(): r = lax.ppermute(send_r, 'mp', [(i, i + 1) for i in range(step)])]
    dot_general x30 -> x27, matrix products: 209 us -> 159 us  [the longest x5 51.7 us: dot_tn(): lax.dot_general(a, b, (((0,), (0,)), ((), ())), preferred_element_type=F32)]
    concatenate x0 -> x12, other arithmetic: none -> 32.7 us  [the longest x1 12.8 us: body(): jnp.concatenate([dot_tn(jnp.concatenate(d_glu_all, axis=0), jnp.concatena...]
    unnamed x0 -> x27, other arithmetic: none -> 24.3 us
  transfers between devices with their start and end apart: 24 -> 102, of which waited for: 22 -> 44; matrix products, arithmetic and copies ran while one was open for 16% -> 24% of each run, Pallas kernels for 0% -> 0%
where the time goes in v1:
time: 856 us; the launch traced here: 847 us
  waiting for transfers between devices  283 us (33%)
  starting transfers between devices  234 us (27%)
  matrix products  159 us (19%)
  other arithmetic  87.5 us (10%)
  blocking collectives  40.5 us (5%)
  local copies, waits for them, and re-layouts  25.8 us (3%)
  between operations  17 us (2%)
    ppermute x24, waiting for transfers between devices, line_gather(): l = lax.ppermute(l, 'mp', [(i, i - 1) for i in range(1, n - step + 1)])  155 us
    ppermute x24, starting transfers between devices, line_scatter(): r = lax.ppermute(send_r, 'mp', [(i, i + 1) for i in range(step)])  113 us
    ppermute x24, waiting for transfers between devices, line_scatter(): r = lax.ppermute(send_r, 'mp', [(i, i + 1) for i in range(step)])  79 us
    ppermute x24, starting transfers between devices, line_gather(): r = lax.ppermute(r, 'mp', [(i, i + 1) for i in range(step - 1, n - 1)])  66.2 us
    dot_general x5, matrix products, dot_tn(): lax.dot_general(a, b, (((0,), (0,)), ((), ())), preferred_element_type=F32)  51.7 us
    dot_general x8, matrix products, dot_nt(): lax.dot_general(a, b, (((1,), (1,)), ((), ())), preferred_element_type=F32)  48.2 us
    dot_general x8, matrix products, dot_nn(): lax.dot_general(a, b, (((1,), (0,)), ((), ())), preferred_element_type=F32)  43.3 us
    psum x1, blocking collectives, body(): lax.psum(jnp.stack([sum(first_gain), sum(second_gain)]), ('dp', 'mp'))  40.5 us
  transfers between devices with their start and end apart: 102, of which 44 were waited for; matrix products, arithmetic and copies ran while one was open for 24% of the time, Pallas kernels for 0%

profile of v1, /device:TPU:0, one launch (start us, length us, event | category | flops | bytes accessed | tf_op | source)
XLA Modules:
  0.0 846.6 jit_solution(8839183228155669539)
XLA Ops:
  21.3 10.0 %collective-permute-done.1 = bf16[128,2048]{1,0:T(8,128)(2,1)S(1)} collective-permute-done((bf16[128,2048]{1,0:T(8,128)(2,1)S(1)}, bf16[128,2048]{1,0:T(8,128)(2,1)S(1)}, u32[]{:S(2)}, u32[]{:S(2)}) %collective-permute-start.1) | collective-permute-done | bytes 524320 | tf_op jit(solution)/shard_map/ppermute | solution.py:53
  33.3 13.1 %collective-permute-done.2 = bf16[128,2048]{1,0:T(8,128)(2,1)S(1)} collective-permute-done((bf16[128,2048]{1,0:T(8,128)(2,1)S(1)}, bf16[128,2048]{1,0:T(8,128)(2,1)S(1)}, u32[]{:S(2)}, u32[]{:S(2)}) %collective-permute-start.2) | collective-permute-done | bytes 524320 | tf_op jit(solution)/shard_map/ppermute | solution.py:53
  48.6 12.1 %collective-permute-done.3 = bf16[128,2048]{1,0:T(8,128)(2,1)} collective-permute-done((bf16[128,2048]{1,0:T(8,128)(2,1)S(1)}, bf16[128,2048]{1,0:T(8,128)(2,1)}, u32[]{:S(2)}, u32[]{:S(2)}) %collective-permute-start.3) | collective-permute-done | bytes 524320 | tf_op jit(solution)/shard_map/ppermute | solution.py:53
  83.5 8.2 collective-permute-done.8
  95.1 8.5 %collective-permute-done.9 = bf16[128,2048]{1,0:T(8,128)(2,1)} collective-permute-done((bf16[128,2048]{1,0:T(8,128)(2,1)S(1)}, bf16[128,2048]{1,0:T(8,128)(2,1)}, u32[]{:S(2)}, u32[]{:S(2)}) %collective-permute-start.9) | collective-permute-done | bytes 524320 | tf_op jit(solution)/shard_map/ppermute | solution.py:53
  107.4 8.1 fusion.74
  197.0 8.1 collective-permute-start.48
  221.1 17.0 %collective-permute-start.18 = (bf16[128,2048]{1,0:T(8,128)(2,1)S(1)}, bf16[128,2048]{1,0:T(8,128)(2,1)S(1)}, u32[]{:S(2)}, u32[]{:S(2)}) collective-permute-start(bf16[128,2048]{1,0:T(8,128)(2,1)S(1)} %get-tuple-element.72), channel_id=1, source_target_pairs={{0,1},{1,2},{2,3},{4,5},{5,6},{6,7},{8,9},{9,10},{10,11},{12,13},{... | collective-permute-start | bytes 1572872 | tf_op jit(solution)/shard_map/ppermute | solution.py:52
  240.2 8.5 %collective-permute-done.51 = bf16[128,2048]{1,0:T(8,128)(2,1)S(1)} collective-permute-done((bf16[128,2048]{1,0:T(8,128)(2,1)S(1)}, bf16[128,2048]{1,0:T(8,128)(2,1)S(1)}, u32[]{:S(2)}, u32[]{:S(2)}) %collective-permute-start.51) | collective-permute-done | bytes 524320 | tf_op jit(solution)/shard_map/ppermute | solution.py:53
  259.6 7.6 collective-permute-done.21
  270.7 7.8 fusion.6
  309.1 17.2 %collective-permute-start.25 = (bf16[128,2048]{1,0:T(8,128)(2,1)S(1)}, bf16[128,2048]{1,0:T(8,128)(2,1)S(1)}, u32[]{:S(2)}, u32[]{:S(2)}) collective-permute-start(bf16[128,2048]{1,0:T(8,128)(2,1)S(1)} %get-tuple-element.135), channel_id=1, source_target_pairs={{0,1},{1,2},{4,5},{5,6},{8,9},{9,10},{12,13},{13,14},{16,17},{17,1... | collective-permute-start | bytes 1572872 | tf_op jit(solution)/shard_map/ppermute | solution.py:66
  327.6 11.8 %collective-permute-start.56 = (bf16[128,2048]{1,0:T(8,128)(2,1)S(1)}, bf16[128,2048]{1,0:T(8,128)(2,1)S(1)}, u32[]{:S(2)}, u32[]{:S(2)}) collective-permute-start(bf16[128,2048]{1,0:T(8,128)(2,1)S(1)} %get-tuple-element.127), channel_id=1, source_target_pairs={{0,1},{1,2},{2,3},{4,5},{5,6},{6,7},{8,9},{9,10},{10,11},{12,13},{... | collective-permute-start | bytes 1572872 | tf_op jit(solution)/shard_map/ppermute | solution.py:66
  341.1 10.1 %collective-permute-start.26 = (bf16[128,2048]{1,0:T(8,128)(2,1)S(1)}, bf16[128,2048]{1,0:T(8,128)(2,1)S(1)}, u32[]{:S(2)}, u32[]{:S(2)}) collective-permute-start(bf16[128,2048]{1,0:T(8,128)(2,1)S(1)} %get-tuple-element.133), channel_id=1, source_target_pairs={{0,1},{1,2},{2,3},{4,5},{5,6},{6,7},{8,9},{9,10},{10,11},{12,13},{... | collective-permute-start | bytes 1572872 | tf_op jit(solution)/shard_map/ppermute | solution.py:66
  357.9 12.8 %collective-permute-done.29 = bf16[128,2048]{1,0:T(8,128)(2,1)S(1)} collective-permute-done((bf16[128,2048]{1,0:T(8,128)(2,1)S(1)}, bf16[128,2048]{1,0:T(8,128)(2,1)S(1)}, u32[]{:S(2)}, u32[]{:S(2)}) %collective-permute-start.29) | collective-permute-done | bytes 524320 | tf_op jit(solution)/shard_map/ppermute | solution.py:67
  392.9 9.9 %collective-permute-done.61 = bf16[128,2048]{1,0:T(8,128)(2,1)S(1)} collective-permute-done((bf16[128,2048]{1,0:T(8,128)(2,1)S(1)}, bf16[128,2048]{1,0:T(8,128)(2,1)S(1)}, u32[]{:S(2)}, u32[]{:S(2)}) %collective-permute-start.61) | collective-permute-done | bytes 524320 | tf_op jit(solution)/shard_map/ppermute | solution.py:53
  405.6 8.5 %collective-permute-done.37 = bf16[128,2048]{1,0:T(8,128)(2,1)S(1)} collective-permute-done((bf16[128,2048]{1,0:T(8,128)(2,1)S(1)}, bf16[128,2048]{1,0:T(8,128)(2,1)S(1)}, u32[]{:S(2)}, u32[]{:S(2)}) %collective-permute-start.37) | collective-permute-done | bytes 524320 | tf_op jit(solution)/shard_map/ppermute | solution.py:53
  416.1 9.2 %collective-permute-done.68 = bf16[128,2048]{1,0:T(8,128)(2,1)S(1)} collective-permute-done((bf16[128,2048]{1,0:T(8,128)(2,1)S(1)}, bf16[128,2048]{1,0:T(8,128)(2,1)S(1)}, u32[]{:S(2)}, u32[]{:S(2)}) %collective-permute-start.68) | collective-permute-done | bytes 524320 | tf_op jit(solution)/shard_map/ppermute | solution.py:53
  428.6 7.7 collective-permute-done.38
  444.4 8.7 %collective-permute-done.39 = bf16[128,2048]{1,0:T(8,128)(2,1)S(1)} collective-permute-done((bf16[128,2048]{1,0:T(8,128)(2,1)S(1)}, bf16[128,2048]{1,0:T(8,128)(2,1)S(1)}, u32[]{:S(2)}, u32[]{:S(2)}) %collective-permute-start.39) | collective-permute-done | bytes 524320 | tf_op jit(solution)/shard_map/ppermute | solution.py:53
  477.1 7.2 fusion.34
  546.9 7.6 collective-permute-start.78
  563.1 9.1 %collective-permute-done.80 = bf16[128,2048]{1,0:T(8,128)(2,1)S(1)} collective-permute-done((bf16[128,2048]{1,0:T(8,128)(2,1)S(1)}, bf16[128,2048]{1,0:T(8,128)(2,1)S(1)}, u32[]{:S(2)}, u32[]{:S(2)}) %collective-permute-start.80) | collective-permute-done | bytes 524320 | tf_op jit(solution)/shard_map/ppermute | solution.py:53
  574.1 9.1 %collective-permute-done.81 = bf16[128,2048]{1,0:T(8,128)(2,1)S(1)} collective-permute-done((bf16[128,2048]{1,0:T(8,128)(2,1)S(1)}, bf16[128,2048]{1,0:T(8,128)(2,1)S(1)}, u32[]{:S(2)}, u32[]{:S(2)}) %collective-permute-start.81) | collective-permute-done | bytes 524320 | tf_op jit(solution)/shard_map/ppermute | solution.py:53
  602.2 7.3 pad_maximum_fusion.1
  628.2 13.3 %convolution_convert_fusion.1 = bf16[1888,2048]{1,0:T(8,128)(2,1)} fusion(bf16[1024,2048]{1,0:T(8,128)(2,1)S(1)} %copy-done.50, bf16[1024,864]{0,1:T(8,128)(2,1)S(1)} %bitcast.92, bf16[1024,512]{0,1:T(8,128)(2,1)S(1)} %bitcast.100, bf16[1024,512]{0,1:T(8,128)(2,1)S(1)} %bitcast.102), kind=kOutput, calls=%fused_computation.5 | convolution fusion | flops 7934312448 | bytes 15794176 | tf_op jit(solution)/shard_map/dot_general | solution.py:45
  648.5 21.0 %convolution_convert_fusion = bf16[1728,2048]{1,0:T(8,128)(2,1)S(1)} fusion(bf16[1024,2048]{1,0:T(8,128)(2,1)} %get-tuple-element.57, bf16[512,864]{0,1:T(8,128)(2,1)S(1)} %copy-done.88, bf16[512,864]{0,1:T(8,128)(2,1)S(1)} %copy-done.86, bf16[512,864]{0,1:T(8,128)(2,1)S(1)} %copy-done.84, bf16[512,864]{0,1:T(8,128)(2,1)S(1)} %copy-done.82), kind=kOutput, calls=%fused_computation.4 | convolution fusion | flops 7265452032 | bytes 14811136 | tf_op jit(solution)/shard_map/dot_general | solution.py:45
  669.5 12.8 %pad_maximum_fusion = bf16[2592,2048]{1,0:T(8,128)(2,1)} fusion(bf16[864,2048]{1,0:T(8,128)(2,1)S(1)} %convolution_convert_fusion.2, bf16[1728,2048]{1,0:T(8,128)(2,1)S(1)} %convolution_convert_fusion), kind=kLoop, calls=%fused_computation | loop fusion | flops 21233664 | bytes 21233664 | tf_op jit(solution)/shard_map/concatenate | solution.py:183
  688.0 10.2 %convolution_convert_fusion.6 = bf16[512,2048]{1,0:T(8,128)(2,1)S(1)} fusion(bf16[2752,2048]{1,0:T(8,128)(2,1)} %all-gather.4.cloned.1.call-done, bf16[1024,2752]{0,1:T(8,128)(2,1)S(1)} %pad_maximum_fusion.2), kind=kOutput, calls=%fused_computation.55 | convolution fusion | flops 5772410880 | bytes 16187392 | tf_op jit(solution)/shard_map/dot_general | solution.py:41
  740.8 8.0 collective-permute-start.92
  761.1 40.5 %psum.7 = f32[2,2048]{1,0:T(2,128)S(1)} all-reduce(f32[2,2048]{1,0:T(2,128)S(1)} %pad_maximum_fusion.7), channel_id=1, replica_groups=mesh['dp'=8,'mp'=4] {'dp','mp'}, use_global_device_ids=true, to_apply=%region_24.25 | all-reduce | flops 4096 | bytes 32768 | tf_op jit(solution)/shard_map/psum | solution.py:226
  815.8 19.8 %reduce-scatter.8.cloned.1.call-done = bf16[2592,256]{1,0:T(8,128)(2,1)} async-done(((bf16[2592,2048]{1,0:T(8,128)(2,1)}), bf16[2592,256]{1,0:T(8,128)(2,1)}) %reduce-scatter.8.cloned.1.call-update) | async-done | bytes 1327120 | tf_op jit(solution)/shard_map/reduce_scatter | solution.py:190
  (519 shorter events, 458.8 us)
Async XLA Ops:
  7.2 100.2 %all-gather.4.cloned.1.call-start = ((), (), s32[]{:S(2)}) async-start(), calls=%async_computation.3 | async-start | bytes 12681216 | tf_op jit(solution)/shard_map/all_gather | solution.py:96
  11.9 126.8 %all-gather.6.cloned.1.call-start = ((), (), s32[]{:S(2)}) async-start(), calls=%async_computation.4 | async-start | bytes 3981312 | tf_op jit(solution)/shard_map/all_gather | solution.py:97
  12.6 258.1 %all-gather.8.cloned.1.call-start = ((), (), s32[]{:S(2)}) async-start(), calls=%async_computation.5 | async-start | bytes 11943936 | tf_op jit(solution)/shard_map/all_gather | solution.py:99
  68.2 738.9 %reduce-scatter.6.cloned.1.call-start = ((), (), s32[]{:S(2)}) async-start(), calls=%async_computation.7 | async-start | bytes 7962624 | tf_op jit(solution)/shard_map/reduce_scatter | solution.py:203
  157.5 22.2 %collective-permute-start.31 = (bf16[128,2048]{1,0:T(8,128)(2,1)S(1)}, bf16[128,2048]{1,0:T(8,128)(2,1)S(1)}, u32[]{:S(2)}, u32[]{:S(2)}) collective-permute-start(bf16[128,2048]{1,0:T(8,128)(2,1)S(1)} %get-tuple-element.153), channel_id=1, source_target_pairs={{0,1},{1,2},{4,5},{5,6},{8,9},{9,10},{12,13},{13,14},{16,17},{17,1... | collective-permute-start | bytes 1572872 | tf_op jit(solution)/shard_map/ppermute | solution.py:66
  168.7 22.2 %collective-permute-start.13 = (bf16[128,2048]{1,0:T(8,128)(2,1)S(1)}, bf16[128,2048]{1,0:T(8,128)(2,1)S(1)}, u32[]{:S(2)}, u32[]{:S(2)}) collective-permute-start(bf16[128,2048]{1,0:T(8,128)(2,1)S(1)} %get-tuple-element.147), channel_id=1, source_target_pairs={{0,1},{1,2},{4,5},{5,6},{8,9},{9,10},{12,13},{13,14},{16,17},{17,1... | collective-permute-start | bytes 1572872 | tf_op jit(solution)/shard_map/ppermute | solution.py:66
  174.0 23.0 %collective-permute-start.49 = (bf16[128,2048]{1,0:T(8,128)(2,1)S(1)}, bf16[128,2048]{1,0:T(8,128)(2,1)S(1)}, u32[]{:S(2)}, u32[]{:S(2)}) collective-permute-start(bf16[128,2048]{1,0:T(8,128)(2,1)S(1)} %get-tuple-element.167), channel_id=1, source_target_pairs={{1,0},{2,1},{3,2},{5,4},{6,5},{7,6},{9,8},{10,9},{11,10},{13,12},{... | collective-permute-start | bytes 1572872 | tf_op jit(solution)/shard_map/ppermute | solution.py:53
  180.1 25.1 %collective-permute-start.32 = (bf16[128,2048]{1,0:T(8,128)(2,1)S(1)}, bf16[128,2048]{1,0:T(8,128)(2,1)S(1)}, u32[]{:S(2)}, u32[]{:S(2)}) collective-permute-start(bf16[128,2048]{1,0:T(8,128)(2,1)S(1)} %get-tuple-element.151), channel_id=1, source_target_pairs={{0,1},{1,2},{2,3},{4,5},{5,6},{6,7},{8,9},{9,10},{10,11},{12,13},{... | collective-permute-start | bytes 1572872 | tf_op jit(solution)/shard_map/ppermute | solution.py:66
  184.5 22.0 %collective-permute-start.35 = (bf16[128,2048]{1,0:T(8,128)(2,1)S(1)}, bf16[128,2048]{1,0:T(8,128)(2,1)S(1)}, u32[]{:S(2)}, u32[]{:S(2)}) collective-permute-start(bf16[128,2048]{1,0:T(8,128)(2,1)S(1)} %get-tuple-element.152), channel_id=1, source_target_pairs={{1,0},{2,1},{3,2},{5,4},{6,5},{7,6},{9,8},{10,9},{11,10},{13,12},{... | collective-permute-start | bytes 1572872 | tf_op jit(solution)/shard_map/ppermute | solution.py:67
  191.3 22.1 %collective-permute-start.14 = (bf16[128,2048]{1,0:T(8,128)(2,1)S(1)}, bf16[128,2048]{1,0:T(8,128)(2,1)S(1)}, u32[]{:S(2)}, u32[]{:S(2)}) collective-permute-start(bf16[128,2048]{1,0:T(8,128)(2,1)S(1)} %get-tuple-element.145), channel_id=1, source_target_pairs={{0,1},{1,2},{2,3},{4,5},{5,6},{6,7},{8,9},{9,10},{10,11},{12,13},{... | collective-permute-start | bytes 1572872 | tf_op jit(solution)/shard_map/ppermute | solution.py:66
  197.0 22.1 %collective-permute-start.48 = (bf16[128,2048]{1,0:T(8,128)(2,1)S(1)}, bf16[128,2048]{1,0:T(8,128)(2,1)S(1)}, u32[]{:S(2)}, u32[]{:S(2)}) collective-permute-start(bf16[128,2048]{1,0:T(8,128)(2,1)S(1)} %get-tuple-element.167), channel_id=1, source_target_pairs={{0,1},{1,2},{2,3},{4,5},{5,6},{6,7},{8,9},{9,10},{10,11},{12,13},{... | collective-permute-start | bytes 1572872 | tf_op jit(solution)/shard_map/ppermute | solution.py:52
  219.8 28.9 %collective-permute-start.51 = (bf16[128,2048]{1,0:T(8,128)(2,1)S(1)}, bf16[128,2048]{1,0:T(8,128)(2,1)S(1)}, u32[]{:S(2)}, u32[]{:S(2)}) collective-permute-start(bf16[128,2048]{1,0:T(8,128)(2,1)S(1)} %collective-permute-done.50), channel_id=1, source_target_pairs={{1,0},{5,4},{9,8},{13,12},{17,16},{21,20},{25,24},{29,28}} | collective-permute-start | bytes 1572872 | tf_op jit(solution)/shard_map/ppermute | solution.py:53
  221.1 28.6 %collective-permute-start.18 = (bf16[128,2048]{1,0:T(8,128)(2,1)S(1)}, bf16[128,2048]{1,0:T(8,128)(2,1)S(1)}, u32[]{:S(2)}, u32[]{:S(2)}) collective-permute-start(bf16[128,2048]{1,0:T(8,128)(2,1)S(1)} %get-tuple-element.72), channel_id=1, source_target_pairs={{0,1},{1,2},{2,3},{4,5},{5,6},{6,7},{8,9},{9,10},{10,11},{12,13},{... | collective-permute-start | bytes 1572872 | tf_op jit(solution)/shard_map/ppermute | solution.py:52
  300.3 26.8 %collective-permute-start.55 = (bf16[128,2048]{1,0:T(8,128)(2,1)S(1)}, bf16[128,2048]{1,0:T(8,128)(2,1)S(1)}, u32[]{:S(2)}, u32[]{:S(2)}) collective-permute-start(bf16[128,2048]{1,0:T(8,128)(2,1)S(1)} %get-tuple-element.129), channel_id=1, source_target_pairs={{0,1},{1,2},{4,5},{5,6},{8,9},{9,10},{12,13},{13,14},{16,17},{17,1... | collective-permute-start | bytes 1572872 | tf_op jit(solution)/shard_map/ppermute | solution.py:66
  304.7 22.4 %collective-permute-start.58 = (bf16[128,2048]{1,0:T(8,128)(2,1)S(1)}, bf16[128,2048]{1,0:T(8,128)(2,1)S(1)}, u32[]{:S(2)}, u32[]{:S(2)}) collective-permute-start(bf16[128,2048]{1,0:T(8,128)(2,1)S(1)} %get-tuple-element.130), channel_id=1, source_target_pairs={{2,1},{3,2},{6,5},{7,6},{10,9},{11,10},{14,13},{15,14},{18,17},{19... | collective-permute-start | bytes 1572872 | tf_op jit(solution)/shard_map/ppermute | solution.py:67
  309.1 31.6 %collective-permute-start.25 = (bf16[128,2048]{1,0:T(8,128)(2,1)S(1)}, bf16[128,2048]{1,0:T(8,128)(2,1)S(1)}, u32[]{:S(2)}, u32[]{:S(2)}) collective-permute-start(bf16[128,2048]{1,0:T(8,128)(2,1)S(1)} %get-tuple-element.135), channel_id=1, source_target_pairs={{0,1},{1,2},{4,5},{5,6},{8,9},{9,10},{12,13},{13,14},{16,17},{17,1... | collective-permute-start | bytes 1572872 | tf_op jit(solution)/shard_map/ppermute | solution.py:66
  327.6 25.3 %collective-permute-start.56 = (bf16[128,2048]{1,0:T(8,128)(2,1)S(1)}, bf16[128,2048]{1,0:T(8,128)(2,1)S(1)}, u32[]{:S(2)}, u32[]{:S(2)}) collective-permute-start(bf16[128,2048]{1,0:T(8,128)(2,1)S(1)} %get-tuple-element.127), channel_id=1, source_target_pairs={{0,1},{1,2},{2,3},{4,5},{5,6},{6,7},{8,9},{9,10},{10,11},{12,13},{... | collective-permute-start | bytes 1572872 | tf_op jit(solution)/shard_map/ppermute | solution.py:66
  376.2 26.6 %collective-permute-start.61 = (bf16[128,2048]{1,0:T(8,128)(2,1)S(1)}, bf16[128,2048]{1,0:T(8,128)(2,1)S(1)}, u32[]{:S(2)}, u32[]{:S(2)}) collective-permute-start(bf16[128,2048]{1,0:T(8,128)(2,1)S(1)} %get-tuple-element.89), channel_id=1, source_target_pairs={{1,0},{2,1},{3,2},{5,4},{6,5},{7,6},{9,8},{10,9},{11,10},{13,12},{... | collective-permute-start | bytes 1572872 | tf_op jit(solution)/shard_map/ppermute | solution.py:53
  377.5 27.4 %collective-permute-start.66 = (bf16[128,2048]{1,0:T(8,128)(2,1)S(1)}, bf16[128,2048]{1,0:T(8,128)(2,1)S(1)}, u32[]{:S(2)}, u32[]{:S(2)}) collective-permute-start(bf16[128,2048]{1,0:T(8,128)(2,1)S(1)} %get-tuple-element.164), channel_id=1, source_target_pairs={{0,1},{1,2},{2,3},{4,5},{5,6},{6,7},{8,9},{9,10},{10,11},{12,13},{... | collective-permute-start | bytes 1572872 | tf_op jit(solution)/shard_map/ppermute | solution.py:52
  382.7 31.3 %collective-permute-start.37 = (bf16[128,2048]{1,0:T(8,128)(2,1)S(1)}, bf16[128,2048]{1,0:T(8,128)(2,1)S(1)}, u32[]{:S(2)}, u32[]{:S(2)}) collective-permute-start(bf16[128,2048]{1,0:T(8,128)(2,1)S(1)} %get-tuple-element.174), channel_id=1, source_target_pairs={{1,0},{2,1},{3,2},{5,4},{6,5},{7,6},{9,8},{10,9},{11,10},{13,12},{... | collective-permute-start | bytes 1572872 | tf_op jit(solution)/shard_map/ppermute | solution.py:53
  384.0 31.3 %collective-permute-start.36 = (bf16[128,2048]{1,0:T(8,128)(2,1)S(1)}, bf16[128,2048]{1,0:T(8,128)(2,1)S(1)}, u32[]{:S(2)}, u32[]{:S(2)}) collective-permute-start(bf16[128,2048]{1,0:T(8,128)(2,1)S(1)} %get-tuple-element.174), channel_id=1, source_target_pairs={{0,1},{1,2},{2,3},{4,5},{5,6},{6,7},{8,9},{9,10},{10,11},{12,13},{... | collective-permute-start | bytes 1572872 | tf_op jit(solution)/shard_map/ppermute | solution.py:52
  391.6 33.7 %collective-permute-start.68 = (bf16[128,2048]{1,0:T(8,128)(2,1)S(1)}, bf16[128,2048]{1,0:T(8,128)(2,1)S(1)}, u32[]{:S(2)}, u32[]{:S(2)}) collective-permute-start(bf16[128,2048]{1,0:T(8,128)(2,1)S(1)} %collective-permute-done.67), channel_id=1, source_target_pairs={{1,0},{2,1},{5,4},{6,5},{9,8},{10,9},{13,12},{14,13},{17,16},{18,1... | collective-permute-start | bytes 1572872 | tf_op jit(solution)/shard_map/ppermute | solution.py:53
  402.9 23.8 %collective-permute-start.60 = (bf16[128,2048]{1,0:T(8,128)(2,1)S(1)}, bf16[128,2048]{1,0:T(8,128)(2,1)S(1)}, u32[]{:S(2)}, u32[]{:S(2)}) collective-permute-start(bf16[128,2048]{1,0:T(8,128)(2,1)S(1)} %get-tuple-element.89), channel_id=1, source_target_pairs={{0,1},{1,2},{2,3},{4,5},{5,6},{6,7},{8,9},{9,10},{10,11},{12,13},{... | collective-permute-start | bytes 1572872 | tf_op jit(solution)/shard_map/ppermute | solution.py:52
  404.9 23.0 %collective-permute-start.70 = (bf16[128,2048]{1,0:T(8,128)(2,1)S(1)}, bf16[128,2048]{1,0:T(8,128)(2,1)S(1)}, u32[]{:S(2)}, u32[]{:S(2)}) collective-permute-start(bf16[128,2048]{1,0:T(8,128)(2,1)S(1)} %collective-permute-done.66), channel_id=1, source_target_pairs={{1,2},{2,3},{5,6},{6,7},{9,10},{10,11},{13,14},{14,15},{17,18},{18... | collective-permute-start | bytes 1572872 | tf_op jit(solution)/shard_map/ppermute | solution.py:52
  414.1 22.2 %collective-permute-start.38 = (bf16[128,2048]{1,0:T(8,128)(2,1)S(1)}, bf16[128,2048]{1,0:T(8,128)(2,1)S(1)}, u32[]{:S(2)}, u32[]{:S(2)}) collective-permute-start(bf16[128,2048]{1,0:T(8,128)(2,1)S(1)} %collective-permute-done.37), channel_id=1, source_target_pairs={{1,0},{2,1},{5,4},{6,5},{9,8},{10,9},{13,12},{14,13},{17,16},{18,1... | collective-permute-start | bytes 1572872 | tf_op jit(solution)/shard_map/ppermute | solution.py:53
  415.4 21.6 %collective-permute-start.40 = (bf16[128,2048]{1,0:T(8,128)(2,1)S(1)}, bf16[128,2048]{1,0:T(8,128)(2,1)S(1)}, u32[]{:S(2)}, u32[]{:S(2)}) collective-permute-start(bf16[128,2048]{1,0:T(8,128)(2,1)S(1)} %collective-permute-done.36), channel_id=1, source_target_pairs={{1,2},{2,3},{5,6},{6,7},{9,10},{10,11},{13,14},{14,15},{17,18},{18... | collective-permute-start | bytes 1572872 | tf_op jit(solution)/shard_map/ppermute | solution.py:52
  426.6 59.2 %collective-permute-start.62 = (bf16[128,2048]{1,0:T(8,128)(2,1)S(1)}, bf16[128,2048]{1,0:T(8,128)(2,1)S(1)}, u32[]{:S(2)}, u32[]{:S(2)}) collective-permute-start(bf16[128,2048]{1,0:T(8,128)(2,1)S(1)} %collective-permute-done.61), channel_id=1, source_target_pairs={{1,0},{2,1},{5,4},{6,5},{9,8},{10,9},{13,12},{14,13},{17,16},{18,1... | collective-permute-start | bytes 1572872 | tf_op jit(solution)/shard_map/ppermute | solution.py:53
  427.9 58.6 %collective-permute-start.64 = (bf16[128,2048]{1,0:T(8,128)(2,1)S(1)}, bf16[128,2048]{1,0:T(8,128)(2,1)S(1)}, u32[]{:S(2)}, u32[]{:S(2)}) collective-permute-start(bf16[128,2048]{1,0:T(8,128)(2,1)S(1)} %collective-permute-done.60), channel_id=1, source_target_pairs={{1,2},{2,3},{5,6},{6,7},{9,10},{10,11},{13,14},{14,15},{17,18},{18... | collective-permute-start | bytes 1572872 | tf_op jit(solution)/shard_map/ppermute | solution.py:52
  488.7 39.8 %collective-permute-start.65 = (bf16[128,2048]{1,0:T(8,128)(2,1)S(1)}, bf16[128,2048]{1,0:T(8,128)(2,1)S(1)}, u32[]{:S(2)}, u32[]{:S(2)}) collective-permute-start(bf16[128,2048]{1,0:T(8,128)(2,1)S(1)} %collective-permute-done.64), channel_id=1, source_target_pairs={{2,3},{6,7},{10,11},{14,15},{18,19},{22,23},{26,27},{30,31}} | collective-permute-start | bytes 1572872 | tf_op jit(solution)/shard_map/ppermute | solution.py:52
  609.4 201.9 %reduce-scatter.4.cloned.1.call-start = ((), (), s32[]{:S(2)}) async-start(), calls=%async_computation.6 | async-start | bytes 8699904 | tf_op jit(solution)/shard_map/reduce_scatter | solution.py:215
  641.5 194.1 %reduce-scatter.8.cloned.1.call-start = ((), (), s32[]{:S(2)}) async-start(), calls=%async_computation.8 | async-start | bytes 11943936 | tf_op jit(solution)/shard_map/reduce_scatter | solution.py:190
  712.3 22.0 %collective-permute-start.85 = (bf16[128,2048]{1,0:T(8,128)(2,1)S(1)}, bf16[128,2048]{1,0:T(8,128)(2,1)S(1)}, u32[]{:S(2)}, u32[]{:S(2)}) collective-permute-start(bf16[128,2048]{1,0:T(8,128)(2,1)S(1)} %get-tuple-element.111), channel_id=1, source_target_pairs={{0,1},{1,2},{4,5},{5,6},{8,9},{9,10},{12,13},{13,14},{16,17},{17,1... | collective-permute-start | bytes 1572872 | tf_op jit(solution)/shard_map/ppermute | solution.py:66
  (165 other events, 2555.8 us)
Sparse Core Ops, SparseCore 0:
  12.0 71.3 all-gather.3
  85.3 34.4 all-gather.5
  121.6 65.7 all-gather.7
  609.6 67.5 reduce-scatter.5
  680.5 68.6 reduce-scatter.3
  752.5 83.0 reduce-scatter.7

commit v2 on v1

v2 whole, which is shorter than its diff:
```python
import functools

import jax
import jax.numpy as jnp
from jax import lax
from jax.experimental import pallas as pl
from jax.experimental.pallas import tpu as pltpu
from jax.sharding import PartitionSpec as P

H = 8
HK = 256
HV = 432
LEN = 1024
CHUNKS = 2
LANES = 128
VMEM_MOST = 66_000_000

epsilon = 1e-05
group_epsilon = 1.0
BF = jnp.bfloat16
F32 = jnp.float32


def layer_norm(values_in, offset):
    centre = jnp.mean(values_in, axis=-1, keepdims=True)
    centred = values_in - centre
    variance = jnp.mean(centred * centred, axis=-1, keepdims=True)
    scaling = lax.rsqrt(variance + offset)
    return (centred * scaling, scaling)


def norm_back(grad_hat, normed_hat, scaling):
    first_mean = jnp.mean(grad_hat, axis=-1, keepdims=True)
    second_mean = jnp.mean(grad_hat * normed_hat, axis=-1, keepdims=True)
    return scaling * (grad_hat - first_mean - normed_hat * second_mean)


def glu_act(gate_pre, up_pre):
    return jax.nn.gelu(gate_pre, approximate=True) * up_pre


def dot_nt(a, b):
    return lax.dot_general(a, b, (((1,), (1,)), ((), ())), preferred_element_type=F32)


def dot_nn(a, b):
    return lax.dot_general(a, b, (((1,), (0,)), ((), ())), preferred_element_type=F32)


def dot_tn(a, b):
    return lax.dot_general(a, b, (((0,), (0,)), ((), ())), preferred_element_type=F32)


MESH = pl.DeviceIdType.MESH


class Line:
    def __init__(self, n, send_sem, recv_sem):
        self.n, self.send_sem, self.recv_sem = n, send_sem, recv_sem
        self.place = lax.axis_index("mp")
        self.used = 0
        self.sent = []

    def enter(self):
        barrier = pltpu.get_barrier_semaphore()
        n, place = self.n, self.place

        @pl.when(place >= 1)
        def _():
            pl.semaphore_signal(barrier, inc=1, device_id={"mp": place - 1}, device_id_type=MESH)

        @pl.when(place <= n - 2)
        def _():
            pl.semaphore_signal(barrier, inc=1, device_id={"mp": place + 1}, device_id_type=MESH)

        pl.semaphore_wait(barrier, jnp.minimum(place, 1) + jnp.minimum(n - 1 - place, 1))

    def copy(self, src, dst, index, toward):
        return pltpu.make_async_remote_copy(
            src_ref=src,
            dst_ref=dst,
            send_sem=self.send_sem.at[index],
            recv_sem=self.recv_sem.at[index],
            device_id={"mp": self.place + toward},
            device_id_type=MESH,
        )

    def leave(self):
        for condition, copy in self.sent:
            pl.when(condition)(copy.wait_send)


class Gather:
    def __init__(self, line, slot):
        self.line, self.slot, self.step_no = line, slot, 0
        self.base = line.used
        line.used += 2 * (line.n - 1)
        n = line.n
        self.right = [
            line.copy(slot(s - 1), slot(s), self.base + s - 1, 1) for s in range(1, n)
        ]
        self.left = [
            line.copy(slot((n - s + 1) % n), slot(n - s), self.base + n - 2 + s, -1)
            for s in range(1, n)
        ]

    def arrive(self, s):
        n, place = self.line.n, self.line.place
        pl.when(place >= s)(self.right[s - 1].wait_recv)
        pl.when(place <= n - 1 - s)(self.left[s - 1].wait_recv)

    def step(self):
        self.step_no += 1
        s, n, place = self.step_no, self.line.n, self.line.place
        if s > 1:
            self.arrive(s - 1)
        if s < n:
            to_right = (place >= s - 1) & (place <= n - 2)
            to_left = (place <= n - s) & (place >= 1)
            pl.when(to_right)(self.right[s - 1].start)
            pl.when(to_left)(self.left[s - 1].start)
            self.line.sent += [(to_right, self.right[s - 1]), (to_left, self.left[s - 1])]


class Scatter:
    def __init__(self, line, slot, from_left, from_right, add):
        self.line, self.slot, self.add, self.step_no = line, slot, add, 0
        self.from_left, self.from_right = from_left, from_right
        self.base = line.used
        line.used += 2 * (line.n - 1)
        n = line.n
        self.right = [
            line.copy(slot(s), from_left(s), self.base + s - 1, 1) for s in range(1, n)
        ]
        self.left = [
            line.copy(slot(n - s), from_right(s), self.base + n - 2 + s, -1) for s in range(1, n)
        ]
        self.mine = []

    def step(self):
        self.step_no += 1
        s, n, place = self.step_no, self.line.n, self.line.place
        to_right, to_left = place <= s - 1, place >= n - s
        if s > 1:

            @pl.when(to_right & (place >= 1))
            def _():
                self.right[s - 2].wait_recv()
                self.add(self.slot(s), self.from_left(s - 1))

            @pl.when(to_left & (place <= n - 2))
            def _():
                self.left[s - 2].wait_recv()
                self.add(self.slot(n - s), self.from_right(s - 1))

        pl.when(to_right)(self.right[s - 1].start)
        pl.when(to_left)(self.left[s - 1].start)
        self.mine += [(to_right, self.right[s - 1]), (to_left, self.left[s - 1])]

    def finish(self):
        n, place = self.line.n, self.line.place

        @pl.when(place >= 1)
        def _():
            self.right[n - 2].wait_recv()

        @pl.when(place <= n - 2)
        def _():
            self.left[n - 2].wait_recv()

    def drain(self):
        for condition, copy in self.mine:
            pl.when(condition)(copy.wait_send)


ANY = pl.BlockSpec(memory_space=pl.ANY)
VM = pl.BlockSpec(memory_space=pltpu.VMEM)
BLOCK = 16


def blocks(count, step):
    def run(i, carry):
        step(lambda base=0: pl.ds(pl.multiple_of(base + i * BLOCK, BLOCK), BLOCK))
        return carry

    lax.fori_loop(0, count // BLOCK, run, 0)


def add_into(target, extra):
    def step(at):
        target[at(), :] = (target[at(), :].astype(F32) + extra[at(), :].astype(F32)).astype(BF)

    blocks(target.shape[0], step)


def product_tiles(target, left, right, tile):
    def step(j, carry):
        at = pl.ds(pl.multiple_of(j * tile, tile), tile)
        target[:, at] = dot_nn(left[...], right[:, at]).astype(BF)
        return carry

    lax.fori_loop(0, right.shape[1] // tile, step, 0)


def gather_kernel(n, own, out, send_sem, recv_sem, copy_sem):
    line = Line(n, send_sem, recv_sem)
    piece = own.shape[0] // CHUNKS
    per = n * piece
    line.enter()
    local, gathers = [], []
    for h in range(CHUNKS):
        mine = own.at[pl.ds(h * piece, piece)]
        keep = pltpu.make_async_copy(mine, out.at[pl.ds(h * per, piece)], copy_sem.at[h])
        keep.start()
        local.append(keep)

        def slot(k, h=h, mine=mine):
            return mine if k == 0 else out.at[pl.ds(h * per + k * piece, piece)]

        gathers.append(Gather(line, slot))
    for _ in range(n):
        for g in gathers:
            g.step()
    for keep in local:
        keep.wait()
    line.leave()


def gather_rows(own, n):
    rows, width = own.shape
    count = CHUNKS * 2 * (n - 1)
    return pl.pallas_call(
        functools.partial(gather_kernel, n),
        out_shape=jax.ShapeDtypeStruct((n * rows, width), own.dtype),
        in_specs=[VM],
        out_specs=ANY,
        scratch_shapes=[
            pltpu.SemaphoreType.DMA((count,)),
            pltpu.SemaphoreType.DMA((count,)),
            pltpu.SemaphoreType.DMA((CHUNKS,)),
        ],
        compiler_params=pltpu.CompilerParams(collective_id=0, has_side_effects=True),
        name="gather_rows",
    )(own)


def no_neighbour_zero(n, place, from_left, from_right):
    @pl.when(place == 0)
    def _():
        from_left[...] = jnp.zeros_like(from_left)

    @pl.when(place == n - 1)
    def _():
        from_right[...] = jnp.zeros_like(from_right)


def middle_kernel(
    n, gated, wo, wg, wd, own, cot, gain,
    rows_out, cot_out, mid_out, hidden_out, glu_out, outputs, d_middle, gain_out,
    gated_v, wo_v, wg_v, wd_v, own_v, cot_v, rows_v, hidden_v, glu_v, part, part_two,
    left_a, right_a, left_b, right_b, middle, stage, copy_sem, send_sem, recv_sem,
):
    line = Line(n, send_sem, recv_sem)
    place = line.place
    count, width = own.shape
    piece = count // CHUNKS
    per = n * piece
    wide = hidden_v.shape[1]
    copies = []

    def local(src, dst):
        c = pltpu.make_async_copy(src, dst, copy_sem.at[len(copies)])
        copies.append(c)
        c.start()
        return c

    def rows_at(ref, h, k=0, size=piece):
        return ref.at[pl.ds(h * per + k * piece, size)]

    load_cot = [
        local(cot.at[pl.ds(h * piece, piece)], rows_at(cot_v, h)) for h in range(CHUNKS)
    ]
    load_gated = local(gated, gated_v)
    load_wo = local(wo, wo_v)
    load_own = local(own, own_v)
    load_wg = local(wg, wg_v)
    load_wd = local(wd, wd_v)
    line.enter()
    for h in range(CHUNKS):
        no_neighbour_zero(n, place, left_a.at[h, n - 2], right_a.at[h, n - 2])
        no_neighbour_zero(n, place, left_b.at[h, n - 2], right_b.at[h, n - 2])
    gain_out[...] = jnp.zeros_like(gain_out)

    def scatter(buf, lefts, rights, h):
        return Scatter(
            line,
            lambda k: rows_at(buf, h, k),
            lambda s: lefts.at[h, s - 1],
            lambda s: rights.at[h, s - 1],
            add_into,
        )

    gather_cot = [Gather(line, functools.partial(rows_at, cot_v, h)) for h in range(CHUNKS)]
    gather_two = [Gather(line, functools.partial(rows_at, rows_v, h)) for h in range(CHUNKS)]

    def mid_slot(h, k):
        return stage.at[h] if k == 0 else rows_at(mid_out, h, k)

    gather_mid = [Gather(line, functools.partial(mid_slot, h)) for h in range(CHUNKS)]
    scatter_one = [scatter(part, left_a, right_a, h) for h in range(CHUNKS)]
    scatter_two = [scatter(part_two, left_b, right_b, h) for h in range(CHUNKS)]
    scatter_grad = [scatter(part, left_a, right_a, h) for h in range(CHUNKS)]

    def chunk(ref, h):
        return ref.at[pl.ds(h * per, per)]

    def out_product(h):
        product_tiles(chunk(part, h), chunk(gated_v, h), wo_v, 2 * LANES)

    def finish_one(h):
        scatter_one[h].finish()

        def step(at):
            src = at(h * per)
            mine = at(h * piece)
            total = (
                own_v[mine, :].astype(F32)
                + part[src, :].astype(F32)
                + left_a[h, n - 2, at(), :].astype(F32)
                + right_a[h, n - 2, at(), :].astype(F32)
            )
            middle[mine, :] = total
            hat, _ = layer_norm(total, epsilon)
            rows_v[src, :] = (hat * gain[...]).astype(BF)

        blocks(piece, step)

    def glu_tiles(h, first, last):
        def step(j, carry):
            pair = pl.ds(pl.multiple_of(j * 2 * LANES, 2 * LANES), 2 * LANES)
            at = pl.ds(pl.multiple_of(j * LANES, LANES), LANES)
            whole = pl.ds(h * per, per)
            both = dot_nt(rows_v[whole, :], wg_v[pair, :])
            d_hidden = dot_nt(cot_v[whole, :], wd_v[at, :])
            u, up = both[:, :LANES], both[:, LANES:]
            c = 0.7978845608028654
            t = jnp.tanh(c * (u + 0.044715 * (u * u * u)))
            half = 0.5 * (1.0 + t)
            act = u * half
            slope = half + 0.5 * u * (1.0 - t * t) * (c * (1.0 + 3 * 0.044715 * (u * u)))
            hidden_v[whole, at] = (act * up).astype(BF)
            glu_v[whole, pair] = jnp.concatenate(
                [(d_hidden * up * slope).astype(BF), (d_hidden * act).astype(BF)], axis=1
            )
            return carry

        lax.fori_loop(first, last, step, 0)

    def grad_product(h):
        product_tiles(chunk(part, h), chunk(glu_v, h), wg_v, 2 * LANES)

    def down_product(h):
        product_tiles(chunk(part_two, h), chunk(hidden_v, h), wd_v, 2 * LANES)

    def finish_grad(h):
        scatter_grad[h].finish()

        def step(at):
            src = at(h * per)
            mine = at(h * piece)
            grad = (
                part[src, :].astype(F32)
                + left_a[h, n - 2, at(), :].astype(F32)
                + right_a[h, n - 2, at(), :].astype(F32)
            )
            hat, scale = layer_norm(middle[mine, :], epsilon)
            gain_out[...] += jnp.sum((hat * grad).reshape(BLOCK // 8, 8, width), axis=0)
            d_mid = cot_v[src, :].astype(F32) + norm_back(grad * gain[...], hat, scale)
            d_middle[mine, :] = d_mid
            stage[h, at(), :] = d_mid.astype(BF)

        blocks(piece, step)
        local(stage.at[h], rows_at(mid_out, h))

    def finish_two(h):
        scatter_two[h].finish()

        def step(at):
            src = at(h * per)
            mine = at(h * piece)
            outputs[mine, :] = (
                middle[mine, :]
                + part_two[src, :].astype(F32)
                + left_b[h, n - 2, at(), :].astype(F32)
                + right_b[h, n - 2, at(), :].astype(F32)
            ).astype(BF)

        blocks(piece, step)

    assert CHUNKS == 2
    tiles = wide // LANES
    cut = tiles // 2
    cot_a, cot_b = gather_cot
    two_a, two_b = gather_two
    mid_a, mid_b = gather_mid
    one_a, one_b = scatter_one
    grad_a, grad_b = scatter_grad
    down_a, down_b = scatter_two

    load_cot[0].wait()
    load_cot[1].wait()
    cot_a.step()
    load_gated.wait()
    load_wo.wait()
    out_product(0)
    one_a.step()
    out_product(1)
    one_b.step()
    for i in range(n - 2):
        one_a.step()
        if i > 0:
            one_b.step()
        cot_a.step()
    load_own.wait()
    finish_one(0)
    two_a.step()
    one_b.step()
    cot_a.step()
    two_a.step()
    finish_one(1)
    two_b.step()
    for _ in range(n - 3):
        two_a.step()
        two_b.step()
    load_wg.wait()
    load_wd.wait()
    two_a.step()
    cot_b.step()
    glu_tiles(0, 0, cut)
    two_b.step()
    cot_b.step()
    glu_tiles(0, cut, tiles)
    for _ in range(n - 3):
        cot_b.step()
    one_a.drain()
    grad_product(0)
    grad_a.step()
    down_product(0)
    grad_a.step()
    two_b.step()
    cot_b.step()
    one_b.drain()
    down_a.step()
    glu_tiles(1, 0, cut)
    for _ in range(n - 3):
        grad_a.step()
    down_a.step()
    glu_tiles(1, cut, tiles)
    finish_grad(0)
    mid_a.step()
    grad_product(1)
    grad_b.step()
    mid_a.step()
    down_product(1)
    grad_b.step()
    for _ in range(n - 3):
        grad_b.step()
        mid_a.step()
        down_a.step()
    down_b.step()
    finish_grad(1)
    mid_b.step()
    mid_a.step()
    for c in range(CHUNKS):
        local(chunk(rows_v, c), chunk(rows_out, c))
        local(chunk(cot_v, c), chunk(cot_out, c))
        local(chunk(hidden_v, c), chunk(hidden_out, c))
        local(chunk(glu_v, c), chunk(glu_out, c))
    finish_two(0)
    for _ in range(n - 2):
        mid_b.step()
        down_b.step()
    mid_b.step()
    finish_two(1)
    for item in gather_cot + gather_two + gather_mid:
        assert item.step_no == n
    for item in scatter_one + scatter_two + scatter_grad:
        assert item.step_no == n - 1
    for group in (scatter_grad, scatter_two):
        for item in group:
            item.drain()
    for item in copies[2 + 5 :]:
        item.wait()
    line.leave()


def middle_call(gated, wo, wg, wd, own, cot, gain, n):
    rows, width = own.shape
    tokens, nv = gated.shape
    wide = wd.shape[0]
    piece = rows // CHUNKS
    sems = CHUNKS * 6 * 2 * (n - 1)
    hop = (CHUNKS, n - 1, piece, width)
    shape = jax.ShapeDtypeStruct
    return pl.pallas_call(
        functools.partial(middle_kernel, n),
        out_shape=(
            shape((tokens, width), BF),
            shape((tokens, width), BF),
            shape((tokens, width), BF),
            shape((tokens, wide), BF),
            shape((tokens, 2 * wide), BF),
            shape((rows, width), BF),
            shape((rows, width), F32),
            shape((8, width), F32),
        ),
        in_specs=[ANY] * 6 + [VM],
        out_specs=(ANY,) * 5 + (VM,) * 3,
        scratch_shapes=[
            pltpu.VMEM((tokens, nv), BF),
            pltpu.VMEM((nv, width), BF),
            pltpu.VMEM((2 * wide, width), BF),
            pltpu.VMEM((wide, width), BF),
            pltpu.VMEM((rows, width), BF),
            pltpu.VMEM((tokens, width), BF),
            pltpu.VMEM((tokens, width), BF),
            pltpu.VMEM((tokens, wide), BF),
            pltpu.VMEM((tokens, 2 * wide), BF),
            pltpu.VMEM((tokens, width), BF),
            pltpu.VMEM((tokens, width), BF),
            pltpu.VMEM(hop, BF),
            pltpu.VMEM(hop, BF),
            pltpu.VMEM(hop, BF),
            pltpu.VMEM(hop, BF),
            pltpu.VMEM((rows, width), F32),
            pltpu.VMEM((CHUNKS, piece, width), BF),
            pltpu.SemaphoreType.DMA((7 + 5 * CHUNKS,)),
            pltpu.SemaphoreType.DMA((sems,)),
            pltpu.SemaphoreType.DMA((sems,)),
        ],
        compiler_params=pltpu.CompilerParams(
            collective_id=1, has_side_effects=True, vmem_limit_bytes=VMEM_MOST
        ),
        name="middle",
    )(gated, wo, wg, wd, own, cot, gain)


def last_kernel(
    n, grads, weight, out, grads_v, weight_v, part, lefts, rights, copy_sem, send_sem, recv_sem
):
    line = Line(n, send_sem, recv_sem)
    count, width = out.shape
    piece = count // CHUNKS
    per = n * piece
    load = [
        pltpu.make_async_copy(
            grads.at[pl.ds(h * per, per)], grads_v.at[pl.ds(h * per, per)], copy_sem.at[h]
        )
        for h in range(CHUNKS)
    ]
    load_weight = pltpu.make_async_copy(weight, weight_v, copy_sem.at[CHUNKS])
    for item in load + [load_weight]:
        item.start()
    line.enter()
    for h in range(CHUNKS):
        no_neighbour_zero(n, line.place, lefts.at[h, n - 2], rights.at[h, n - 2])
    scatters = [
        Scatter(
            line,
            lambda k, h=h: part.at[pl.ds(h * per + k * piece, piece)],
            lambda s, h=h: lefts.at[h, s - 1],
            lambda s, h=h: rights.at[h, s - 1],
            add_into,
        )
        for h in range(CHUNKS)
    ]

    def finish(h):
        scatters[h].finish()

        def step(at):
            src = at(h * per)
            out[at(h * piece), :] = (
                part[src, :].astype(F32)
                + lefts[h, n - 2, at(), :].astype(F32)
                + rights[h, n - 2, at(), :].astype(F32)
            )

        blocks(piece, step)

    load_weight.wait()
    for h in range(CHUNKS):
        load[h].wait()
        rows = pl.ds(h * per, per)
        product_tiles(part.at[rows], grads_v.at[rows], weight_v, 2 * LANES)
        scatters[h].step()
    for _ in range(n - 2):
        for h in range(CHUNKS):
            scatters[h].step()
    for h in range(CHUNKS):
        finish(h)
    for h in range(CHUNKS):
        scatters[h].drain()


def last_call(grads, weight, n):
    tokens, deep = grads.shape
    width = weight.shape[1]
    rows = tokens // n
    sems = CHUNKS * 2 * (n - 1)
    hop = (CHUNKS, n - 1, rows // CHUNKS, width)
    return pl.pallas_call(
        functools.partial(last_kernel, n),
        out_shape=jax.ShapeDtypeStruct((rows, width), F32),
        in_specs=[ANY, ANY],
        out_specs=VM,
        scratch_shapes=[
            pltpu.VMEM((tokens, deep), BF),
            pltpu.VMEM((deep, width), BF),
            pltpu.VMEM((tokens, width), BF),
            pltpu.VMEM(hop, BF),
            pltpu.VMEM(hop, BF),
            pltpu.SemaphoreType.DMA((CHUNKS + 1,)),
            pltpu.SemaphoreType.DMA((sems,)),
            pltpu.SemaphoreType.DMA((sems,)),
        ],
        compiler_params=pltpu.CompilerParams(
            collective_id=2, has_side_effects=True, vmem_limit_bytes=VMEM_MOST
        ),
        name="last",
    )(grads, weight)


def pad_rows(array, count):
    return jnp.pad(array, ((0, count - array.shape[0]), (0, 0)))


def pad_columns(array, count):
    return jnp.pad(array, ((0, 0), (0, count - array.shape[1])))


def body(
    inputs,
    segments,
    first_norm_gain,
    w_query,
    w_key,
    w_value,
    w_gate,
    w_out,
    second_norm_gain,
    w_glu_gate,
    w_glu_up,
    w_down,
    cotangent,
):
    n = lax.axis_size("mp")
    place = lax.axis_index("mp")
    heads = H // n
    head_start = place * heads
    rows, width = inputs.shape
    shard = w_query.shape[0]
    piece = rows // CHUNKS
    nk, nv, nf = heads * HK, heads * HV, w_down.shape[0]
    n_one = 2 * nk + 2 * nv
    one_wide = -(-n_one // (2 * LANES)) * 2 * LANES
    v_wide, f_wide = -(-nv // LANES) * LANES, -(-nf // LANES) * LANES
    f_tiles = f_wide // LANES

    pack_one = pad_rows(
        jnp.concatenate([w_query.T, w_key.T, w_value.T, w_gate.T], axis=0), one_wide
    )
    weight_one = lax.all_gather(pack_one, "dp", axis=1, tiled=True)
    out_weight = lax.all_gather(pad_rows(w_out, v_wide), "dp", axis=1, tiled=True)
    glu_pack = jnp.stack(
        [
            pad_rows(w_glu_gate.T, f_wide).reshape(f_tiles, LANES, shard),
            pad_rows(w_glu_up.T, f_wide).reshape(f_tiles, LANES, shard),
        ],
        axis=1,
    ).reshape(2 * f_wide, shard)
    pack_two = jnp.concatenate([glu_pack, pad_rows(w_down, f_wide)], axis=0)
    weight_two = lax.all_gather(pack_two, "dp", axis=1, tiled=True)
    glu_weight, down_weight = weight_two[: 2 * f_wide], weight_two[2 * f_wide :]

    first_hat, first_scale = layer_norm(inputs.astype(F32), epsilon)
    rows_one = gather_rows((first_hat * first_norm_gain).astype(BF), n)
    tokens = rows_one.shape[0]

    slot_shard = lax.rem(place - jnp.arange(n) + n, n)
    places = (
        slot_shard[None, :, None] * rows
        + jnp.arange(CHUNKS)[:, None, None] * piece
        + jnp.arange(piece)[None, None, :]
    ).reshape(tokens)
    seg = segments.reshape(n, CHUNKS, piece)[::-1]
    seg = lax.dynamic_slice_in_dim(jnp.concatenate([seg, seg], axis=0), n - 1 - place, n, axis=0)
    seg = seg.transpose(1, 0, 2).reshape(tokens)

    query_key = dot_nt(rows_one, weight_one[: 2 * nk]).astype(BF)
    value = dot_nt(rows_one, weight_one[2 * nk : 2 * nk + nv]).astype(BF)
    gate_pre = dot_nt(rows_one, weight_one[2 * nk + nv : n_one])
    query = query_key[:, :nk].reshape(tokens, heads, HK)
    key = query_key[:, nk:].reshape(tokens, heads, HK)
    value = value.reshape(tokens, heads, HV)

    distance = places[:, None] - places[None, :]
    allowed = (distance >= 0) & (seg[:, None] == seg[None, :])
    log_gamma = jnp.log1p(-jnp.exp2(-5.0 - (head_start + jnp.arange(heads)).astype(F32)))
    exponent = jnp.where(
        allowed[None], distance[None].astype(F32) * log_gamma[:, None, None], 0.0
    )
    mask = jnp.where(allowed[None], jnp.exp(exponent), 0.0) * HK ** (-0.5)

    scores = (jnp.einsum("thk,shk->hts", query, key, preferred_element_type=F32) * mask).astype(BF)
    retained = jnp.einsum("hts,shv->thv", scores, value, preferred_element_type=F32)
    normalized, scale_group = layer_norm(retained, group_epsilon)
    normal_flat = normalized.reshape(tokens, nv)
    swish = jax.nn.silu(gate_pre)
    gated = pad_columns((swish * normal_flat).astype(BF), v_wide)

    rows_two, cot_rows, mid_rows, hidden, d_glu, outputs, middle_grad, second_gain = middle_call(
        gated, out_weight, glu_weight, down_weight, inputs, cotangent, second_norm_gain[None], n
    )

    grads_two = jnp.concatenate([dot_tn(d_glu, rows_two), dot_tn(hidden, cot_rows)], axis=0).astype(BF)
    summed_two = lax.psum_scatter(grads_two, "dp", scatter_dimension=1, tiled=True).astype(F32)
    glu_sum = summed_two[: 2 * f_wide].reshape(f_tiles, 2, LANES, shard)

    d_gated = dot_nt(mid_rows, out_weight[:nv])
    sigmoid_gate = jax.nn.sigmoid(gate_pre)
    d_gate_pre = (
        d_gated * normal_flat * (sigmoid_gate + gate_pre * sigmoid_gate * (1.0 - sigmoid_gate))
    ).astype(BF)
    d_normalized = (d_gated * swish).reshape(tokens, heads, HV)
    d_retained = norm_back(d_normalized, normalized, scale_group).astype(BF)
    grads_out = jnp.concatenate(
        [dot_tn(gated[:, :nv], mid_rows).astype(BF), dot_tn(d_gate_pre, rows_one).astype(BF)], axis=0
    )
    summed_out = lax.psum_scatter(grads_out, "dp", scatter_dimension=1, tiled=True).astype(F32)

    d_value = jnp.einsum("hts,thv->shv", scores, d_retained, preferred_element_type=F32).astype(BF)
    d_scores = (
        jnp.einsum("thv,shv->hts", d_retained, value, preferred_element_type=F32) * mask
    ).astype(BF)
    d_query = jnp.einsum("hts,shk->thk", d_scores, key, preferred_element_type=F32).astype(BF)
    d_key = jnp.einsum("hts,thk->shk", d_scores, query, preferred_element_type=F32).astype(BF)
    d_qkv = jnp.concatenate(
        [d_query.reshape(tokens, nk), d_key.reshape(tokens, nk), d_value.reshape(tokens, nv)], axis=1
    )
    grads_one = dot_tn(d_qkv, rows_one).astype(BF)
    summed_one = lax.psum_scatter(grads_one, "dp", scatter_dimension=1, tiled=True).astype(F32)

    d_one = pad_columns(jnp.concatenate([d_qkv, d_gate_pre], axis=1), one_wide)
    first_grad = last_call(d_one, weight_one, n)
    first_gain = jnp.sum(first_hat * first_grad, axis=0)
    input_gradient = middle_grad + norm_back(first_grad * first_norm_gain, first_hat, first_scale)

    gains = lax.psum(jnp.stack([first_gain, jnp.sum(second_gain, axis=0)]), ("dp", "mp"))
    return (
        outputs,
        input_gradient,
        gains[0],
        summed_one[:nk].T,
        summed_one[nk : 2 * nk].T,
        summed_one[2 * nk :].T,
        summed_out[nv:].T,
        summed_out[:nv],
        gains[1],
        glu_sum[:, 0].reshape(f_wide, shard)[:nf].T,
        glu_sum[:, 1].reshape(f_wide, shard)[:nf].T,
        summed_two[2 * f_wide : 2 * f_wide + nf],
    )


def solution(mesh):
    split = P(("dp", "mp"), None)
    wide, tall = P("dp", "mp"), P("mp", "dp")
    return jax.shard_map(
        body,
        mesh=mesh,
        in_specs=(
            split, P("dp", None), P(), wide, wide, wide, wide, tall, P(), wide, wide, tall, split,
        ),
        out_specs=(
            split, split, P(), wide, wide, wide, wide, tall, P(), wide, wide, tall,
        ),
        check_vma=False,
    )
```

time: 856 us -> 824 us (0.963)
  Pallas kernels: 0 us -> 503 us
  waiting for transfers between devices: 283 us -> 49.3 us
  starting transfers between devices: 234 us -> 0.65 us
  matrix products: 159 us -> 89.6 us
  local copies, waits for them, and re-layouts: 25.8 us -> 72.1 us
  other arithmetic: 87.5 us -> 43.9 us
    pallas_call x0 -> x3, Pallas kernels: none -> 503 us  [the longest x1 355 us: middle_call(): pl.pallas_call(functools.partial(middle_kernel, n), out_shape=(shape((tok...]
    ppermute x96 -> x0, waiting for transfers between devices: 262 us -> none  [the longest x24 155 us: line_gather(): l = lax.ppermute(l, 'mp', [(i, i - 1) for i in range(1, n - step + 1)])]
    ppermute x96 -> x0, starting transfers between devices: 233 us -> none  [the longest x24 113 us: line_scatter(): r = lax.ppermute(send_r, 'mp', [(i, i + 1) for i in range(step)])]
    all_gather x1, waiting for transfers between devices: 0.01 us -> 48.1 us  [body(): weight_one = lax.all_gather(pack_one, 'dp', axis=1, tiled=True)]
    dot_general x8 -> x0, matrix products: 43.3 us -> none  [dot_nn(): lax.dot_general(a, b, (((1,), (0,)), ((), ())), preferred_element_type=F32)]
    unnamed x27 -> x0, other arithmetic: 24.3 us -> none
    reduce_scatter x1, waiting for transfers between devices: 19.8 us -> 1.07 us  [body(): lax.psum_scatter(grads_two, 'dp', scatter_dimension=1, tiled=True)]
    dot_general x8 -> x4, matrix products: 48.2 us -> 34.6 us  [dot_nt(): lax.dot_general(a, b, (((1,), (1,)), ((), ())), preferred_element_type=F32)]
  transfers between devices with their start and end apart: 102 -> 6, of which waited for: 44 -> 2; matrix products, arithmetic and copies ran while one was open for 24% -> 19% of each run, Pallas kernels for 0% -> 18%
where the time goes in v2:
time: 824 us; the launch traced here: 816 us
  Pallas kernels  503 us (61%)
  matrix products  89.6 us (11%)
  local copies, waits for them, and re-layouts  72.1 us (9%)
  waiting for transfers between devices  49.3 us (6%)
  other arithmetic  43.9 us (5%)
  blocking collectives  41.8 us (5%)
  between operations  15.1 us (2%)
    pallas_call x1, Pallas kernels, middle_call(): pl.pallas_call(functools.partial(middle_kernel, n), out_shape=(shape((tok...  355 us
    pallas_call x1, Pallas kernels, last_call(): pl.pallas_call(functools.partial(last_kernel, n), out_shape=jax.ShapeDtyp...  74.4 us
    pallas_call x1, Pallas kernels, gather_rows(): pl.pallas_call(functools.partial(gather_kernel, n), out_shape=jax.ShapeDt...  74 us
    all_gather x1, waiting for transfers between devices, body(): weight_one = lax.all_gather(pack_one, 'dp', axis=1, tiled=True)  48.1 us
    psum x1, blocking collectives, body(): lax.psum(jnp.stack([first_gain, jnp.sum(second_gain, axis=0)]), ('dp', 'm...  41.8 us
    dot_general x5, matrix products, dot_tn(): lax.dot_general(a, b, (((0,), (0,)), ((), ())), preferred_element_type=F32)  40.2 us
    dot_general x4, matrix products, dot_nt(): lax.dot_general(a, b, (((1,), (1,)), ((), ())), preferred_element_type=F32)  34.6 us
    unnamed x103, local copies, waits for them, and re-layouts  17.1 us
  transfers between devices with their start and end apart: 6, of which 2 were waited for; matrix products, arithmetic and copies ran while one was open for 19% of the time, Pallas kernels for 18%

profile of v2, /device:TPU:0, one launch (start us, length us, event | category | flops | bytes accessed | tf_op | source)
XLA Modules:
  0.0 815.9 jit_solution(9008175263069328300)
XLA Ops:
  15.7 74.0 %gather_rows.1 = bf16[1024,2048]{1,0:T(8,128)(2,1)} custom-call(bf16[256,2048]{1,0:T(8,128)(2,1)} %fusion.27.own), custom_call_target="tpu_custom_call" | custom-call | tf_op jit(solution)/shard_map/gather_rows/pallas_call | solution.py:232
  91.0 2.3 subtract_convert_fusion
  93.3 4.5 slice.91.wd
  97.8 7.5 slice.90.wg
  105.3 48.1 %all-gather.4.cloned.1.call-done.weight = bf16[2816,2048]{1,0:T(8,128)(2,1)} async-done(((bf16[2816,256]{1,0:T(8,128)(2,1)}), bf16[2816,2048]{1,0:T(8,128)(2,1)}) %all-gather.4.cloned.1.call-update) | async-done | bytes 11534352 | tf_op jit(solution)/shard_map/all_gather | solution.py:673
  153.4 8.0 fusion.34
  161.7 2.9 copy-done.10
  164.6 3.7 multiply_convert_fusion.1
  168.3 7.4 fusion.37
  175.7 2.0 bitcast_reduce_fusion
  179.5 3.4 copy.73
  182.9 11.0 %multiply_convert_fusion.3 = (bf16[1024,864]{1,0:T(8,128)(2,1)S(1)}, f32[1024,864]{1,0:T(8,128)}) fusion(f32[1024,864]{1,0:T(8,128)} %copy.73, bf16[1024,2048]{1,0:T(8,128)(2,1)} %gather_rows.1, bf16[2816,2048]{1,0:T(8,128)(2,1)} %all-gather.4.cloned.1.call-done.weight), kind=kOutput, calls=%fused_computation.18 | convolution fusion | flops 3629187072 | bytes 16711680 | tf_op jit(solution)/shard_map/dot_general | solution.py:43
  196.5 355.1 %middle.1 = (bf16[1024,2048]{1,0:T(8,128)(2,1)}, bf16[1024,2048]{1,0:T(8,128)(2,1)}, bf16[1024,2048]{1,0:T(8,128)(2,1)}, bf16[1024,896]{1,0:T(8,128)(2,1)}, bf16...) custom-call(bf16[1024,896]{1,0:T(8,128)(2,1)} %pad.26.gated, ...), custom_call_target="tpu_custom_call" | custom-call | tf_op jit(solution)/shard_map/middle/pallas_call | solution.py:505
  551.7 6.8 convolution_convert_fusion.4
  558.5 8.3 %multiply_convert_fusion.2 = (bf16[1024,864]{1,0:T(8,128)(2,1)S(1)}, f32[1024,864]{1,0:T(8,128)}) fusion(f32[1024,864]{1,0:T(8,128)S(1)} %copy-done.12, f32[1024,864]{1,0:T(8,128)} %get-tuple-element.82, bf16[1024,2048]{1,0:T(8,128)(2,1)S(1)} %copy-done.40, bf16[896,2048]{1,0:T(8,128)(2,1)S(1)} %copy-done.13), kind=kOutput, calls=%fused_computation.17 | convolution fusion | flops 3633610752 | bytes 20250624 | tf_op jit(solution)/shard_map/dot_general | solution.py:43
  568.0 5.3 convolution_convert_fusion.3
  573.4 6.1 pad_maximum_fusion.1
  579.5 5.4 copy.77
  585.0 3.8 fusion.49
  593.3 4.4 multiply_convert_fusion
  605.2 13.4 %convolution_convert_fusion.1 = bf16[1888,2048]{1,0:T(8,128)(2,1)} fusion(bf16[1024,2048]{1,0:T(8,128)(2,1)S(1)} %copy-done.9, bf16[1024,864]{0,1:T(8,128)(2,1)S(1)} %bitcast.97, bf16[1024,512]{0,1:T(8,128)(2,1)S(1)} %bitcast.99, bf16[1024,512]{0,1:T(8,128)(2,1)S(1)} %bitcast.101), kind=kOutput, calls=%fused_computation.5 | convolution fusion | flops 7934312448 | bytes 15794176 | tf_op jit(solution)/shard_map/dot_general | solution.py:51
  620.1 6.4 convolution_convert_fusion.2
  626.5 8.3 %convolution_convert_fusion = bf16[1792,2048]{1,0:T(8,128)(2,1)S(1)} fusion(bf16[1024,1792]{1,0:T(8,128)(2,1)S(1)} %copy-done.41, bf16[1024,2048]{1,0:T(8,128)(2,1)S(1)} %copy-done.39), kind=kOutput, calls=%fused_computation.4 | convolution fusion | flops 7519862784 | bytes 15204352 | tf_op jit(solution)/shard_map/dot_general | solution.py:51
  634.8 13.8 %pad_maximum_fusion = bf16[2688,2048]{1,0:T(8,128)(2,1)} fusion(bf16[896,2048]{1,0:T(8,128)(2,1)S(1)} %convolution_convert_fusion.2, bf16[1792,2048]{1,0:T(8,128)(2,1)S(1)} %convolution_convert_fusion), kind=kLoop, calls=%fused_computation | loop fusion | flops 22020096 | bytes 22020096 | tf_op jit(solution)/shard_map/concatenate | solution.py:726
  649.2 2.3 copy.92
  651.5 3.1 copy.83
  654.7 9.7 %concatenate.26 = bf16[1024,2752]{1,0:T(8,128)(2,1)} concatenate(bf16[1024,512]{1,0:T(8,128)(2,1)} %copy.92, bf16[1024,512]{1,0:T(8,128)(2,1)S(1)} %copy.93, bf16[1024,864]{1,0:T(8,128)(2,1)S(1)} %copy.83, bf16[1024,864]{1,0:T(8,128)(2,1)} %copy-done.15), dimensions={1} | concatenate | bytes 11272192 | tf_op jit(solution)/shard_map/concatenate | solution.py:754
  664.4 5.6 pad.31.grads
  670.1 74.4 %last.1 = f32[256,2048]{1,0:T(8,128)} custom-call(bf16[1024,2816]{1,0:T(8,128)(2,1)} %pad.31.grads, bf16[2816,2048]{1,0:T(8,128)(2,1)} %all-gather.4.cloned.1.call-done.weight), custom_call_target="tpu_custom_call" | custom-call | tf_op jit(solution)/shard_map/last/pallas_call | solution.py:612
  744.5 3.6 fusion.32
  748.1 41.8 %psum.7 = f32[2,2048]{1,0:T(2,128)S(1)} all-reduce(f32[2,2048]{1,0:T(2,128)S(1)} %pad_maximum_fusion.3), channel_id=1, replica_groups=mesh['dp'=8,'mp'=4] {'dp','mp'}, use_global_device_ids=true, to_apply=%region_10.11 | all-reduce | flops 4096 | bytes 32768 | tf_op jit(solution)/shard_map/psum | solution.py:759
  790.5 3.7 fusion.31
  (166 shorter events, 44.9 us)
Async XLA Ops:
  7.2 86.1 %all-gather.8.cloned.1.call-start = ((), (), s32[]{:S(2)}) async-start(), calls=%async_computation.5 | async-start | bytes 12386304 | tf_op jit(solution)/shard_map/all_gather | solution.py:683
  10.8 142.6 %all-gather.4.cloned.1.call-start = ((), (), s32[]{:S(2)}) async-start(), calls=%async_computation.3 | async-start | bytes 12976128 | tf_op jit(solution)/shard_map/all_gather | solution.py:673
  12.4 184.1 %all-gather.6.cloned.1.call-start = ((), (), s32[]{:S(2)}) async-start(), calls=%async_computation.4 | async-start | bytes 4128768 | tf_op jit(solution)/shard_map/all_gather | solution.py:674
  13.3 780.9 %reduce-scatter.6.cloned.1.call-start = ((), (), s32[]{:S(2)}) async-start(), calls=%async_computation.7 | async-start | bytes 7962624 | tf_op jit(solution)/shard_map/reduce_scatter | solution.py:740
  13.4 148.2 %copy-start.45 = (f32[2]{0:T(128)}, f32[2]{0:T(128)S(1)}, u32[]{:S(2)}) copy-start(f32[2]{0:T(128)S(1)} %negate_log-plus-one_fusion) | copy-start | bytes 28
  13.7 76.0 %copy-start.34 = (f32[256]{0:T(256)}, f32[256]{0:T(256)S(1)}, u32[]{:S(2)}) copy-start(f32[256]{0:T(256)S(1)} %broadcast_multiply_fusion.5) | copy-start | bytes 3076
  14.1 75.6 %copy-start.36 = (f32[256]{0:T(256)}, f32[256]{0:T(256)S(1)}, u32[]{:S(2)}) copy-start(f32[256]{0:T(256)S(1)} %add_rsqrt_fusion.1) | copy-start | bytes 3076
  91.0 70.7 %copy-start.18 = (pred[1024,1024]{1,0:T(8,128)(4,1)}, pred[1024,1024]{1,0:T(8,128)(4,1)S(1)}, u32[]{:S(2)}) copy-start(pred[1024,1024]{1,0:T(8,128)(4,1)S(1)} %fusion.2) | copy-start | bytes 3145732
  161.6 6.6 copy-start.21
  161.6 6.6 copy-start.23
  164.6 3.7 copy-start.7
  168.3 7.4 copy-start.47
  551.6 6.8 copy-start.12
  551.7 6.8 copy-start.13
  551.7 6.8 copy-start.40
  558.5 9.6 %copy-start.8 = (bf16[1024,2048]{1,0:T(8,128)(2,1)S(1)}, bf16[1024,2048]{1,0:T(8,128)(2,1)}, u32[]{:S(2)}) copy-start(bf16[1024,2048]{1,0:T(8,128)(2,1)} %gather_rows.1) | copy-start | bytes 12582916
  579.5 219.0 %reduce-scatter.4.cloned.1.call-start = ((), (), s32[]{:S(2)}) async-start(), calls=%async_computation.6 | async-start | bytes 8699904 | tf_op jit(solution)/shard_map/reduce_scatter | solution.py:752
  579.5 5.4 copy-start.1
  584.9 4.4 copy-start.4
  589.3 4.0 copy-start.44
  589.3 4.0 copy-start.46
  593.3 4.4 copy-start.24
  601.2 4.0 copy-start.9
  618.7 185.3 %reduce-scatter.8.cloned.1.call-start = ((), (), s32[]{:S(2)}) async-start(), calls=%async_computation.8 | async-start | bytes 12386304 | tf_op jit(solution)/shard_map/reduce_scatter | solution.py:727
  620.1 6.4 copy-start.39
  620.1 6.4 copy-start.41
  664.4 5.7 copy-start.33
  670.0 74.4 %copy-start.32 = (f32[2048]{0:T(1024)S(1)}, f32[2048]{0:T(1024)}, u32[]{:S(2)}) copy-start(f32[2048]{0:T(1024)} %param.15) | copy-start | bytes 24580
  670.1 74.4 %copy-start.35 = (f32[256]{0:T(256)S(1)}, f32[256]{0:T(256)}, u32[]{:S(2)}) copy-start(f32[256]{0:T(256)} %copy-done.34) | copy-start | bytes 3076
  670.1 74.4 %copy-start.37 = (f32[256]{0:T(256)S(1)}, f32[256]{0:T(256)}, u32[]{:S(2)}) copy-start(f32[256]{0:T(256)} %copy-done.36) | copy-start | bytes 3076
  744.5 46.1 %copy-start.3 = (bf16[256,2048]{1,0:T(8,128)(2,1)S(1)}, bf16[256,2048]{1,0:T(8,128)(2,1)}, u32[]{:S(2)}) copy-start(bf16[256,2048]{1,0:T(8,128)(2,1)} %own.1) | copy-start | bytes 3145732
  744.5 46.1 %copy-start.5 = (f32[256,2048]{1,0:T(8,128)S(1)}, f32[256,2048]{1,0:T(8,128)}, u32[]{:S(2)}) copy-start(f32[256,2048]{1,0:T(8,128)} %last.1) | copy-start | bytes 6291460
  (23 other events, 49.6 us)
Sparse Core Ops, SparseCore 0:
  10.9 70.1 all-gather.7
  83.6 69.7 all-gather.3
  155.9 35.0 all-gather.5
  579.6 63.5 reduce-scatter.5
  646.5 68.6 reduce-scatter.3
  718.6 85.2 reduce-scatter.7

commit v3 on v2

--- a/solution.py
+++ b/solution.py
@@ -11,7 +11,7 @@
 HK = 256
 HV = 432
 LEN = 1024
-CHUNKS = 2
+CHUNKS = 4
 LANES = 128
 VMEM_MOST = 66_000_000
 
@@ -254,8 +254,58 @@
         from_right[...] = jnp.zeros_like(from_right)
 
 
+(COT, OUT, ONE, END_ONE, TWO, GLU, GRAD, GRAD_SUM, END_GRAD, MID, DOWN, DOWN_SUM, END_DOWN) = range(13)
+
+DUE = {
+    OUT: (-2.23, 1.66, 0), ONE: (-1.99, 1.12, 1.03), END_ONE: (1.46, 1.37, 0), TWO: (0.73, 1.15, 0.94),
+    COT: (0.35, 1.39, 1.02), GLU: (1.14, -1.37, 1.55), GRAD: (3.09, 2.02, 0),
+    GRAD_SUM: (3.48, 1.71, 0.74), END_GRAD: (7.02, -2.12, 0), MID: (5.68, 0.86, 1.11),
+    DOWN: (1.3, 0.36, 0), DOWN_SUM: (1.87, 1.35, 0.95), END_DOWN: (7.9, 2.17, 0),
+}
+TUNED = {
+    (4, 4): [
+        0, 4, 8, 0, 5, 8, 1, 0, 8, 9, 6, 1, 12, 9, 16, 9, 10, 16, 0, 3,
+        10, 16, 7, 11, 1, 13, 17, 16, 20, 10, 20, 11, 1, 17, 40, 14, 2, 11, 18, 24,
+        17, 2, 28, 44, 15, 19, 17, 21, 2, 18, 28, 44, 21, 41, 18, 19, 3, 2, 45, 28,
+        25, 29, 18, 45, 22, 3, 29, 22, 42, 29, 32, 19, 46, 26, 36, 46, 3, 33, 19, 44,
+        30, 23, 36, 23, 37, 45, 30, 46, 30, 37, 43, 27, 31, 47, 36, 34, 38, 36, 31, 47,
+        50, 37, 37, 38, 31, 48, 47, 35, 38, 39, 49, 39, 38, 39, 51, 39,
+    ],
+}
+
+
+def middle_order(n):
+    if (n, CHUNKS) in TUNED:
+        return [divmod(code, CHUNKS) for code in TUNED[n, CHUNKS]]
+    count = {k: 1 for k in DUE}
+    count.update({COT: n, TWO: n, MID: n, ONE: n - 1, GRAD_SUM: n - 1, DOWN_SUM: n - 1, GLU: 2})
+    needs = {
+        ONE: [OUT], END_ONE: [ONE], TWO: [END_ONE], GLU: [TWO, COT], GRAD: [GLU], GRAD_SUM: [GRAD],
+        END_GRAD: [GRAD_SUM], MID: [END_GRAD], DOWN: [GLU], DOWN_SUM: [DOWN], END_DOWN: [DOWN_SUM],
+    }
+    todo = sorted(
+        (first + h * later + s * 3 / (n - 1) * each, k, h, s)
+        for k, (first, later, each) in DUE.items()
+        for h in range(CHUNKS)
+        for s in range(count[k])
+    )
+    taken, order = {}, []
+    while todo:
+        for item in todo:
+            _, k, h, s = item
+            ready = taken.get((k, h), 0) == s and all(
+                taken.get((need, h), 0) == count[need] for need in needs.get(k, [])
+            )
+            if ready:
+                break
+        todo.remove(item)
+        taken[k, h] = s + 1
+        order.append((k, h))
+    return order
+
+
 def middle_kernel(
-    n, gated, wo, wg, wd, own, cot, gain,
+    n, gated, weights, own, cot, gain,
     rows_out, cot_out, mid_out, hidden_out, glu_out, outputs, d_middle, gain_out,
     gated_v, wo_v, wg_v, wd_v, own_v, cot_v, rows_v, hidden_v, glu_v, part, part_two,
     left_a, right_a, left_b, right_b, middle, stage, copy_sem, send_sem, recv_sem,
@@ -281,10 +331,10 @@
         local(cot.at[pl.ds(h * piece, piece)], rows_at(cot_v, h)) for h in range(CHUNKS)
     ]
     load_gated = local(gated, gated_v)
-    load_wo = local(wo, wo_v)
+    load_wo = local(weights.at[pl.ds(3 * wide, wo_v.shape[0])], wo_v)
     load_own = local(own, own_v)
-    load_wg = local(wg, wg_v)
-    load_wd = local(wd, wd_v)
+    load_wg = local(weights.at[pl.ds(0, 2 * wide)], wg_v)
+    load_wd = local(weights.at[pl.ds(2 * wide, wide)], wd_v)
     line.enter()
     for h in range(CHUNKS):
         no_neighbour_zero(n, place, left_a.at[h, n - 2], right_a.at[h, n - 2])
@@ -397,91 +447,62 @@
 
         blocks(piece, step)
 
-    assert CHUNKS == 2
     tiles = wide // LANES
     cut = tiles // 2
-    cot_a, cot_b = gather_cot
-    two_a, two_b = gather_two
-    mid_a, mid_b = gather_mid
-    one_a, one_b = scatter_one
-    grad_a, grad_b = scatter_grad
-    down_a, down_b = scatter_two
-
-    load_cot[0].wait()
-    load_cot[1].wait()
-    cot_a.step()
-    load_gated.wait()
-    load_wo.wait()
-    out_product(0)
-    one_a.step()
-    out_product(1)
-    one_b.step()
-    for i in range(n - 2):
-        one_a.step()
-        if i > 0:
-            one_b.step()
-        cot_a.step()
-    load_own.wait()
-    finish_one(0)
-    two_a.step()
-    one_b.step()
-    cot_a.step()
-    two_a.step()
-    finish_one(1)
-    two_b.step()
-    for _ in range(n - 3):
-        two_a.step()
-        two_b.step()
-    load_wg.wait()
-    load_wd.wait()
-    two_a.step()
-    cot_b.step()
-    glu_tiles(0, 0, cut)
-    two_b.step()
-    cot_b.step()
-    glu_tiles(0, cut, tiles)
-    for _ in range(n - 3):
-        cot_b.step()
-    one_a.drain()
-    grad_product(0)
-    grad_a.step()
-    down_product(0)
-    grad_a.step()
-    two_b.step()
-    cot_b.step()
-    one_b.drain()
-    down_a.step()
-    glu_tiles(1, 0, cut)
-    for _ in range(n - 3):
-        grad_a.step()
-    down_a.step()
-    glu_tiles(1, cut, tiles)
-    finish_grad(0)
-    mid_a.step()
-    grad_product(1)
-    grad_b.step()
-    mid_a.step()
-    down_product(1)
-    grad_b.step()
-    for _ in range(n - 3):
-        grad_b.step()
-        mid_a.step()
-        down_a.step()
-    down_b.step()
-    finish_grad(1)
-    mid_b.step()
-    mid_a.step()
+
+    def wait_for(items):
+        for item in items:
+            item.wait()
+        items.clear()
+
+    first_loads, own_load = [load_gated, load_wo], [load_own]
+    later_loads = [load_wg, load_wd]
+
+    def out_action(h):
+        wait_for(first_loads)
+        out_product(h)
+
+    def finish_one_action(h):
+        wait_for(own_load)
+        finish_one(h)
+
+    def glu_action(h):
+        wait_for(later_loads)
+        if h in begun:
+            glu_tiles(h, cut, tiles)
+        else:
+            begun.add(h)
+            glu_tiles(h, 0, cut)
+
+    def grad_action(h):
+        scatter_one[h].drain()
+        grad_product(h)
+
+    begun = set()
+    actions = {
+        COT: lambda h: gather_cot[h].step(),
+        OUT: out_action,
+        ONE: lambda h: scatter_one[h].step(),
+        END_ONE: finish_one_action,
+        TWO: lambda h: gather_two[h].step(),
+        GLU: glu_action,
+        GRAD: grad_action,
+        GRAD_SUM: lambda h: scatter_grad[h].step(),
+        END_GRAD: finish_grad,
+        MID: lambda h: gather_mid[h].step(),
+        DOWN: down_product,
+        DOWN_SUM: lambda h: scatter_two[h].step(),
+        END_DOWN: finish_two,
+    }
+    for item in load_cot:
+        item.wait()
+    for kind, h in middle_order(n):
+        actions[kind](h)
     for c in range(CHUNKS):
         local(chunk(rows_v, c), chunk(rows_out, c))
         local(chunk(cot_v, c), chunk(cot_out, c))
         local(chunk(hidden_v, c), chunk(hidden_out, c))
         local(chunk(glu_v, c), chunk(glu_out, c))
-    finish_two(0)
-    for _ in range(n - 2):
-        mid_b.step()
-        down_b.step()
-    mid_b.step()
-    finish_two(1)
     for item in gather_cot + gather_two + gather_mid:
         assert item.step_no == n
     for item in scatter_one + scatter_two + scatter_grad:
@@ -489,15 +510,15 @@
     for group in (scatter_grad, scatter_two):
         for item in group:
             item.drain()
-    for item in copies[2 + 5 :]:
+    for item in copies[CHUNKS + 5 :]:
         item.wait()
     line.leave()
 
 
-def middle_call(gated, wo, wg, wd, own, cot, gain, n):
+def middle_call(gated, weights, own, cot, gain, n):
     rows, width = own.shape
     tokens, nv = gated.shape
-    wide = wd.shape[0]
+    wide = (weights.shape[0] - nv) // 3
     piece = rows // CHUNKS
     sems = CHUNKS * 6 * 2 * (n - 1)
     hop = (CHUNKS, n - 1, piece, width)
@@ -514,7 +535,7 @@
             shape((rows, width), F32),
             shape((8, width), F32),
         ),
-        in_specs=[ANY] * 6 + [VM],
+        in_specs=[ANY] * 4 + [VM],
         out_specs=(ANY,) * 5 + (VM,) * 3,
         scratch_shapes=[
             pltpu.VMEM((tokens, nv), BF),
@@ -534,7 +555,7 @@
             pltpu.VMEM(hop, BF),
             pltpu.VMEM((rows, width), F32),
             pltpu.VMEM((CHUNKS, piece, width), BF),
-            pltpu.SemaphoreType.DMA((7 + 5 * CHUNKS,)),
+            pltpu.SemaphoreType.DMA((5 + 6 * CHUNKS,)),
             pltpu.SemaphoreType.DMA((sems,)),
             pltpu.SemaphoreType.DMA((sems,)),
         ],
@@ -542,7 +563,63 @@
             collective_id=1, has_side_effects=True, vmem_limit_bytes=VMEM_MOST
         ),
         name="middle",
-    )(gated, wo, wg, wd, own, cot, gain)
+    )(gated, weights, own, cot, gain)
+
+
+def gains_kernel(n, m, mine, total, first, second, send_sem, recv_sem):
+    barrier = pltpu.get_barrier_semaphore()
+    groups = (("dp", m, first), ("mp", n, second))
+    for axis, size, _ in groups:
+        me = lax.axis_index(axis)
+        for k in range(1, size):
+            peer = lax.rem(me + k, size)
+            pl.semaphore_signal(barrier, inc=1, device_id={axis: peer}, device_id_type=MESH)
+    pl.semaphore_wait(barrier, n + m - 2)
+    source = mine
+    for base, (axis, size, held) in zip((0, m), groups):
+        me = lax.axis_index(axis)
+        held[me] = source[...]
+
+        def copy(k, slot):
+            return pltpu.make_async_remote_copy(
+                src_ref=source,
+                dst_ref=held.at[slot],
+                send_sem=send_sem.at[base + k],
+                recv_sem=recv_sem.at[base + k],
+                device_id={axis: lax.rem(me + k, size)},
+                device_id_type=MESH,
+            )
+
+        sent = [copy(k, me) for k in range(1, size)]
+        for c in sent:
+            c.start()
+        for k in range(1, size):
+            copy(k, lax.rem(me - k + size, size)).wait_recv()
+        value = held[0]
+        for k in range(1, size):
+            value = value + held[k]
+        for c in sent:
+            c.wait_send()
+        total[...] = value
+        source = total
+
+
+def sum_gains(values, n, m):
+    flat = values.reshape(-1, LANES)
+    return pl.pallas_call(
+        functools.partial(gains_kernel, n, m),
+        out_shape=jax.ShapeDtypeStruct(flat.shape, F32),
+        in_specs=[VM],
+        out_specs=VM,
+        scratch_shapes=[
+            pltpu.VMEM((m,) + flat.shape, F32),
+            pltpu.VMEM((n,) + flat.shape, F32),
+            pltpu.SemaphoreType.DMA((n + m,)),
+            pltpu.SemaphoreType.DMA((n + m,)),
+        ],
+        compiler_params=pltpu.CompilerParams(collective_id=3, has_side_effects=True),
+        name="sum_gains",
+    )(flat).reshape(values.shape)
 
 
 def last_kernel(
@@ -671,7 +748,6 @@
         jnp.concatenate([w_query.T, w_key.T, w_value.T, w_gate.T], axis=0), one_wide
     )
     weight_one = lax.all_gather(pack_one, "dp", axis=1, tiled=True)
-    out_weight = lax.all_gather(pad_rows(w_out, v_wide), "dp", axis=1, tiled=True)
     glu_pack = jnp.stack(
         [
             pad_rows(w_glu_gate.T, f_wide).reshape(f_tiles, LANES, shard),
@@ -679,9 +755,10 @@
         ],
         axis=1,
     ).reshape(2 * f_wide, shard)
-    pack_two = jnp.concatenate([glu_pack, pad_rows(w_down, f_wide)], axis=0)
+    pack_two = jnp.concatenate([glu_pack, pad_rows(w_down, f_wide), pad_rows(w_out, v_wide)], axis=0)
+    pack_two, weight_one = lax.optimization_barrier((pack_two, weight_one))
     weight_two = lax.all_gather(pack_two, "dp", axis=1, tiled=True)
-    glu_weight, down_weight = weight_two[: 2 * f_wide], weight_two[2 * f_wide :]
+    out_weight = weight_two[3 * f_wide :]
 
     first_hat, first_scale = layer_norm(inputs.astype(F32), epsilon)
     rows_one = gather_rows((first_hat * first_norm_gain).astype(BF), n)
@@ -720,7 +797,7 @@
     gated = pad_columns((swish * normal_flat).astype(BF), v_wide)
 
     rows_two, cot_rows, mid_rows, hidden, d_glu, outputs, middle_grad, second_gain = middle_call(
-        gated, out_weight, glu_weight, down_weight, inputs, cotangent, second_norm_gain[None], n
+        gated, weight_two, inputs, cotangent, second_norm_gain[None], n
     )
 
     grads_two = jnp.concatenate([dot_tn(d_glu, rows_two), dot_tn(hidden, cot_rows)], axis=0).astype(BF)
@@ -756,7 +833,9 @@
     first_gain = jnp.sum(first_hat * first_grad, axis=0)
     input_gradient = middle_grad + norm_back(first_grad * first_norm_gain, first_hat, first_scale)
 
-    gains = lax.psum(jnp.stack([first_gain, jnp.sum(second_gain, axis=0)]), ("dp", "mp"))
+    gains = sum_gains(
+        jnp.stack([first_gain, jnp.sum(second_gain, axis=0)]), n, lax.axis_size("dp")
+    )
     return (
         outputs,
         input_gradient,

time: 824 us -> 779 us (0.945)
  waiting for transfers between devices: 49.3 us -> 95.6 us
  blocking collectives: 41.8 us -> 0 us
  Pallas kernels: 503 us -> 462 us
  local copies, waits for them, and re-layouts: 72.1 us -> 62.1 us
    pallas_call x1, Pallas kernels: 355 us -> 297 us  [middle_call(): pl.pallas_call(functools.partial(middle_kernel, n), out_shape=(shape((tok...]
    psum x1 -> x0, blocking collectives: 41.8 us -> none  [body(): lax.psum(jnp.stack([first_gain, jnp.sum(second_gain, axis=0)]), ('dp', 'm...]
    reduce_scatter x1, waiting for transfers between devices: 1.07 us -> 24.6 us  [body(): lax.psum_scatter(grads_two, 'dp', scatter_dimension=1, tiled=True)]
    all_gather x1, waiting for transfers between devices: 48.1 us -> 70.9 us  [body(): weight_one = lax.all_gather(pack_one, 'dp', axis=1, tiled=True)]
    pallas_call x0 -> x1, Pallas kernels: none -> 13.2 us  [sum_gains(): pl.pallas_call(functools.partial(gains_kernel, n, m), out_shape=jax.Shape...]
    slice x3 -> x0, local copies, waits for them, and re-layouts: 12.6 us -> none  [the longest x2 12 us: body(): glu_weight, down_weight = (weight_two[:2 * f_wide], weight_two[2 * f_wide:])]
    unnamed x103 -> x100, local copies, waits for them, and re-layouts: 17.1 us -> 19.4 us
  transfers between devices with their start and end apart: 6 -> 5, of which waited for: 2 -> 2; matrix products, arithmetic and copies ran while one was open for 19% -> 19% of each run, Pallas kernels for 18% -> 22%
where the time goes in v3:
time: 779 us; the launch traced here: 768 us
  Pallas kernels  462 us (59%)
  waiting for transfers between devices  95.6 us (12%)
  matrix products  90 us (12%)
  local copies, waits for them, and re-layouts  62.1 us (8%)
  other arithmetic  43.3 us (6%)
  between operations  14.8 us (2%)
    pallas_call x1, Pallas kernels, middle_call(): pl.pallas_call(functools.partial(middle_kernel, n), out_shape=(shape((tok...  297 us
    pallas_call x1, Pallas kernels, last_call(): pl.pallas_call(functools.partial(last_kernel, n), out_shape=jax.ShapeDtyp...  79.3 us
    pallas_call x1, Pallas kernels, gather_rows(): pl.pallas_call(functools.partial(gather_kernel, n), out_shape=jax.ShapeDt...  73 us
    all_gather x1, waiting for transfers between devices, body(): weight_one = lax.all_gather(pack_one, 'dp', axis=1, tiled=True)  70.9 us
    dot_general x5, matrix products, dot_tn(): lax.dot_general(a, b, (((0,), (0,)), ((), ())), preferred_element_type=F32)  40.2 us
    dot_general x4, matrix products, dot_nt(): lax.dot_general(a, b, (((1,), (1,)), ((), ())), preferred_element_type=F32)  35.3 us
    reduce_scatter x1, waiting for transfers between devices, body(): lax.psum_scatter(grads_two, 'dp', scatter_dimension=1, tiled=True)  24.6 us
    unnamed x100, local copies, waits for them, and re-layouts  19.4 us
  transfers between devices with their start and end apart: 5, of which 2 were waited for; matrix products, arithmetic and copies ran while one was open for 19% of the time, Pallas kernels for 22%

profile of v3, /device:TPU:0, one launch (start us, length us, event | category | flops | bytes accessed | tf_op | source)
XLA Modules:
  0.0 768.5 jit_solution(10162132146279256264)
XLA Ops:
  9.5 2.4 fusion.46
  13.7 70.9 %all-gather.3.cloned.1.call-done.weight = bf16[2816,2048]{1,0:T(8,128)(2,1)} async-done(((bf16[2816,256]{1,0:T(8,128)(2,1)}), bf16[2816,2048]{1,0:T(8,128)(2,1)}) %all-gather.3.cloned.1.call-update) | async-done | bytes 11534352 | tf_op jit(solution)/shard_map/all_gather | solution.py:750
  89.1 73.0 %gather_rows.1 = bf16[1024,2048]{1,0:T(8,128)(2,1)} custom-call(bf16[256,2048]{1,0:T(8,128)(2,1)} %fusion.29.own), custom_call_target="tpu_custom_call" | custom-call | tf_op jit(solution)/shard_map/gather_rows/pallas_call | solution.py:232
  163.8 2.0 copy-done.7
  165.8 7.6 fusion.36
  173.7 3.4 multiply_convert_fusion.1
  177.1 7.4 fusion.41
  184.5 2.0 bitcast_reduce_fusion
  188.3 3.6 copy.75
  191.9 10.9 %multiply_convert_fusion.3 = (bf16[1024,864]{1,0:T(8,128)(2,1)S(1)}, f32[1024,864]{1,0:T(8,128)}) fusion(f32[1024,864]{1,0:T(8,128)} %copy.75, bf16[1024,2048]{1,0:T(8,128)(2,1)} %gather_rows.1, bf16[2816,2048]{1,0:T(8,128)(2,1)} %all-gather.3.cloned.1.call-done.weight), kind=kOutput, calls=%fused_computation.21 | convolution fusion | flops 3629187072 | bytes 16711680 | tf_op jit(solution)/shard_map/dot_general | solution.py:43
  205.5 296.8 %middle.1 = (bf16[1024,2048]{1,0:T(8,128)(2,1)}, bf16[1024,2048]{1,0:T(8,128)(2,1)}, bf16[1024,2048]{1,0:T(8,128)(2,1)}, bf16[1024,896]{1,0:T(8,128)(2,1)}, bf16...) custom-call(bf16[1024,896]{1,0:T(8,128)(2,1)} %pad.30.gated, ...), custom_call_target="tpu_custom_call" | custom-call | tf_op jit(solution)/shard_map/middle/pallas_call | solution.py:526
  502.3 6.8 convolution_convert_fusion.4
  509.1 9.4 %multiply_convert_fusion.2 = (bf16[1024,864]{1,0:T(8,128)(2,1)S(1)}, f32[1024,864]{1,0:T(8,128)}) fusion(f32[1024,864]{1,0:T(8,128)S(1)} %copy-done.12, f32[1024,864]{1,0:T(8,128)S(1)} %copy-done.46, bf16[1024,2048]{1,0:T(8,128)(2,1)S(1)} %copy-done.37, bf16[3584,2048]{1,0:T(8,128)(2,1)} %all-gather.5.cloned.1.call-done.weights), kind=kOutput, calls=%fused_computation.20 | convolution fusion | flops 3633610752 | bytes 20119552 | tf_op jit(solution)/shard_map/dot_general | solution.py:43
  519.7 5.4 convolution_convert_fusion.3
  525.2 6.1 pad_maximum_fusion.1
  531.3 5.7 copy.77
  537.0 3.8 fusion.53
  545.4 4.4 multiply_convert_fusion
  553.3 2.0 convolution_convert_fusion.5
  557.3 13.3 %convolution_convert_fusion.1 = bf16[1888,2048]{1,0:T(8,128)(2,1)} fusion(bf16[1024,2048]{1,0:T(8,128)(2,1)S(1)} %copy-done.9, bf16[1024,864]{0,1:T(8,128)(2,1)S(1)} %bitcast.96, bf16[1024,512]{0,1:T(8,128)(2,1)S(1)} %bitcast.98, bf16[1024,512]{0,1:T(8,128)(2,1)S(1)} %bitcast.100), kind=kOutput, calls=%fused_computation.5 | convolution fusion | flops 7934312448 | bytes 15794176 | tf_op jit(solution)/shard_map/dot_general | solution.py:51
  572.1 6.4 convolution_convert_fusion.2
  578.5 8.3 %convolution_convert_fusion = bf16[1792,2048]{1,0:T(8,128)(2,1)S(1)} fusion(bf16[1024,1792]{1,0:T(8,128)(2,1)S(1)} %copy-done.38, bf16[1024,2048]{1,0:T(8,128)(2,1)S(1)} %copy-done.36), kind=kOutput, calls=%fused_computation.4 | convolution fusion | flops 7519862784 | bytes 15204352 | tf_op jit(solution)/shard_map/dot_general | solution.py:51
  586.8 13.8 %pad_maximum_fusion = bf16[2688,2048]{1,0:T(8,128)(2,1)} fusion(bf16[896,2048]{1,0:T(8,128)(2,1)S(1)} %convolution_convert_fusion.2, bf16[1792,2048]{1,0:T(8,128)(2,1)S(1)} %convolution_convert_fusion), kind=kLoop, calls=%fused_computation | loop fusion | flops 22020096 | bytes 22020096 | tf_op jit(solution)/shard_map/concatenate | solution.py:803
  601.2 2.3 copy.92
  603.5 3.3 copy.83
  606.8 9.7 %concatenate.26 = bf16[1024,2752]{1,0:T(8,128)(2,1)} concatenate(bf16[1024,512]{1,0:T(8,128)(2,1)} %copy.92, bf16[1024,512]{1,0:T(8,128)(2,1)S(1)} %copy.93, bf16[1024,864]{1,0:T(8,128)(2,1)S(1)} %copy.83, bf16[1024,864]{1,0:T(8,128)(2,1)} %copy-done.14), dimensions={1} | concatenate | bytes 11272192 | tf_op jit(solution)/shard_map/concatenate | solution.py:831
  616.5 5.5 pad.31.grads
  621.9 79.3 %last.1 = f32[256,2048]{1,0:T(8,128)} custom-call(bf16[1024,2816]{1,0:T(8,128)(2,1)} %pad.31.grads, bf16[2816,2048]{1,0:T(8,128)(2,1)} %all-gather.3.cloned.1.call-done.weight), custom_call_target="tpu_custom_call" | custom-call | tf_op jit(solution)/shard_map/last/pallas_call | solution.py:689
  701.3 2.9 fusion.34
  704.9 13.2 %sum_gains.1 = f32[32,128]{1,0:T(8,128)} custom-call(f32[32,128]{1,0:T(8,128)} %reshape.293.mine), custom_call_target="tpu_custom_call" | custom-call | tf_op jit(solution)/shard_map/sum_gains/pallas_call | solution.py:609
  719.4 3.7 fusion.33
  731.8 24.6 %reduce-scatter.8.cloned.1.call-done = bf16[2688,256]{1,0:T(8,128)(2,1)} async-done(((bf16[2688,2048]{1,0:T(8,128)(2,1)}), bf16[2688,256]{1,0:T(8,128)(2,1)}) %reduce-scatter.8.cloned.1.call-update) | async-done | bytes 1376272 | tf_op jit(solution)/shard_map/reduce_scatter | solution.py:804
  (163 shorter events, 44.0 us)
Async XLA Ops:
  7.2 4.8 copy-start.24
  7.2 4.9 copy-start.25
  7.2 77.4 %all-gather.3.cloned.1.call-start = ((), (), s32[]{:S(2)}) async-start(), calls=%async_computation.3 | async-start | bytes 12976128 | tf_op jit(solution)/shard_map/all_gather | solution.py:750
  12.0 193.5 %all-gather.5.cloned.1.call-start = ((), (), s32[]{:S(2)}) async-start(), calls=%async_computation.4 | async-start | bytes 16515072 | tf_op jit(solution)/shard_map/all_gather | solution.py:760
  12.1 73.1 %copy-start.35 = (s32[1,1024]{1,0:T(1,128)S(1)}, s32[1,1024]{1,0:T(1,128)}, u32[]{:S(2)}) copy-start(s32[1,1024]{1,0:T(1,128)} %param.14) | copy-start | bytes 12292
  12.1 74.2 %copy-start.2 = (bf16[256,2048]{1,0:T(8,128)(2,1)S(1)}, bf16[256,2048]{1,0:T(8,128)(2,1)}, u32[]{:S(2)}) copy-start(bf16[256,2048]{1,0:T(8,128)(2,1)} %own.1) | copy-start | bytes 3145732
  12.2 75.5 %copy-start.28 = (f32[2048]{0:T(1024)S(1)}, f32[2048]{0:T(1024)}, u32[]{:S(2)}) copy-start(f32[2048]{0:T(1024)} %param.15) | copy-start | bytes 24580
  84.7 638.4 %reduce-scatter.6.cloned.1.call-start = ((), (), s32[]{:S(2)}) async-start(), calls=%async_computation.6 | async-start | bytes 7962624 | tf_op jit(solution)/shard_map/reduce_scatter | solution.py:817
  162.1 11.5 %copy-start.42 = (f32[2]{0:T(128)}, f32[2]{0:T(128)S(1)}, u32[]{:S(2)}) copy-start(f32[2]{0:T(128)S(1)} %negate_log-plus-one_fusion) | copy-start | bytes 28
  162.5 11.2 %copy-start.10 = (f32[1024,1024]{1,0:T(8,128)}, f32[1024,1024]{1,0:T(8,128)S(1)}, u32[]{:S(2)}) copy-start(f32[1024,1024]{1,0:T(8,128)S(1)} %subtract_convert_fusion) | copy-start | bytes 12582916
  165.8 7.9 %copy-start.17 = (pred[1024,1024]{1,0:T(8,128)(4,1)}, pred[1024,1024]{1,0:T(8,128)(4,1)S(1)}, u32[]{:S(2)}) copy-start(pred[1024,1024]{1,0:T(8,128)(4,1)S(1)} %fusion.2) | copy-start | bytes 3145732
  177.1 7.4 copy-start.44
  502.3 6.8 copy-start.12
  502.3 6.8 copy-start.37
  502.3 6.8 copy-start.46
  509.1 10.6 %copy-start.8 = (bf16[1024,2048]{1,0:T(8,128)(2,1)S(1)}, bf16[1024,2048]{1,0:T(8,128)(2,1)}, u32[]{:S(2)}) copy-start(bf16[1024,2048]{1,0:T(8,128)(2,1)} %gather_rows.1) | copy-start | bytes 12582916
  531.2 5.8 copy-start.1
  531.3 196.1 %reduce-scatter.4.cloned.1.call-start = ((), (), s32[]{:S(2)}) async-start(), calls=%async_computation.5 | async-start | bytes 8699904 | tf_op jit(solution)/shard_map/reduce_scatter | solution.py:829
  537.0 4.4 copy-start.4
  541.4 4.0 copy-start.41
  541.4 4.0 copy-start.43
  545.4 4.4 copy-start.23
  553.3 4.0 copy-start.9
  570.6 185.7 %reduce-scatter.8.cloned.1.call-start = ((), (), s32[]{:S(2)}) async-start(), calls=%async_computation.7 | async-start | bytes 12386304 | tf_op jit(solution)/shard_map/reduce_scatter | solution.py:804
  572.1 6.4 copy-start.36
  572.1 6.4 copy-start.38
  621.9 79.4 %copy-start.30 = (f32[8,2048]{1,0:T(8,128)S(1)}, f32[8,2048]{1,0:T(8,128)}, u32[]{:S(2)}) copy-start(f32[8,2048]{1,0:T(8,128)} %get-tuple-element.27) | copy-start | bytes 196612
  621.9 79.4 %copy-start.29 = (f32[2048]{0:T(1024)S(1)}, f32[2048]{0:T(1024)}, u32[]{:S(2)}) copy-start(f32[2048]{0:T(1024)} %param.15) | copy-start | bytes 24580
  621.9 79.4 %copy-start.32 = (f32[256]{0:T(256)S(1)}, f32[256]{0:T(256)}, u32[]{:S(2)}) copy-start(f32[256]{0:T(256)} %copy-done.31) | copy-start | bytes 3076
  621.9 79.4 %copy-start.34 = (f32[256]{0:T(256)S(1)}, f32[256]{0:T(256)}, u32[]{:S(2)}) copy-start(f32[256]{0:T(256)} %copy-done.33) | copy-start | bytes 3076
  701.3 18.2 %copy-start.3 = (bf16[256,2048]{1,0:T(8,128)(2,1)S(1)}, bf16[256,2048]{1,0:T(8,128)(2,1)}, u32[]{:S(2)}) copy-start(bf16[256,2048]{1,0:T(8,128)(2,1)} %own.1) | copy-start | bytes 3145732
  701.3 18.2 %copy-start.5 = (f32[256,2048]{1,0:T(8,128)S(1)}, f32[256,2048]{1,0:T(8,128)}, u32[]{:S(2)}) copy-start(f32[256,2048]{1,0:T(8,128)} %last.1) | copy-start | bytes 6291460
  (20 other events, 43.2 us)
Sparse Core Ops, SparseCore 0:
  12.1 72.5 all-gather.2
  86.5 83.7 all-gather.4
  531.4 63.9 reduce-scatter.5
  598.7 68.6 reduce-scatter.3
  670.8 85.5 reduce-scatter.7

commit v4 on v3

--- a/solution.py
+++ b/solution.py
@@ -61,7 +61,7 @@
         self.used = 0
         self.sent = []
 
-    def enter(self):
+    def enter(self, others=None):
         barrier = pltpu.get_barrier_semaphore()
         n, place = self.n, self.place
 
@@ -73,7 +73,13 @@
         def _():
             pl.semaphore_signal(barrier, inc=1, device_id={"mp": place + 1}, device_id_type=MESH)
 
-        pl.semaphore_wait(barrier, jnp.minimum(place, 1) + jnp.minimum(n - 1 - place, 1))
+        peers = jnp.minimum(place, 1) + jnp.minimum(n - 1 - place, 1)
+        if others is not None:
+            axis, indices = others
+            for index in indices:
+                pl.semaphore_signal(barrier, inc=1, device_id={axis: index}, device_id_type=MESH)
+            peers = peers + len(indices)
+        pl.semaphore_wait(barrier, peers)
 
     def copy(self, src, dst, index, toward):
         return pltpu.make_async_remote_copy(
@@ -202,46 +208,151 @@
     lax.fori_loop(0, right.shape[1] // tile, step, 0)
 
 
-def gather_kernel(n, own, out, send_sem, recv_sem, copy_sem):
+class Doubling:
+    def __init__(self, m, own, out, rows, bits, base, send_sem, recv_sem):
+        self.d = lax.axis_index("dp")
+        self.own, self.out, self.rows, self.bits, self.base = own, out, rows, bits, base
+        self.send_sem, self.recv_sem = send_sem, recv_sem
+        self.shard = own.shape[1]
+        self.done = 0
+        self.sent = []
+
+    def flip(self, d, bit):
+        return d + bit * (1 - 2 * (lax.div(d, bit) % 2))
+
+    def block(self, d):
+        return self.out.at[self.rows, pl.ds(pl.multiple_of(d * self.shard, self.shard), self.shard)]
+
+    def copies(self, level, landing):
+        owners = [self.d]
+        for bit in self.bits[:level]:
+            owners += [self.flip(d, bit) for d in owners]
+        bit = self.bits[level]
+        partner = self.flip(self.d, bit)
+        out = []
+        for i, d in enumerate(owners):
+            d = self.flip(d, bit) if landing else d
+            src = self.own.at[self.rows] if i == 0 and not landing else self.block(d)
+            index = self.base + (1 << level) - 1 + i
+            out.append(
+                pltpu.make_async_remote_copy(
+                    src_ref=src,
+                    dst_ref=self.block(d),
+                    send_sem=self.send_sem.at[index],
+                    recv_sem=self.recv_sem.at[index],
+                    device_id={"dp": partner},
+                    device_id_type=MESH,
+                )
+            )
+        return out
+
+    def step(self):
+        level = self.done
+        if level > 0:
+            for c in self.copies(level - 1, True):
+                c.wait_recv()
+        if level < len(self.bits):
+            out = self.copies(level, False)
+            for c in out:
+                c.start()
+            self.sent += out
+        self.done += 1
+
+    def leave(self):
+        for c in self.sent:
+            c.wait_send()
+
+
+def bits_of(m):
+    bits = [1 << b for b in range(m.bit_length() - 1)]
+    assert 1 << len(bits) == m
+    return bits
+
+
+PARTS = 2
+
+
+def gather_kernel(n, m, own, pack, out, weight, send_sem, recv_sem, copy_sem, wide_send, wide_recv):
     line = Line(n, send_sem, recv_sem)
     piece = own.shape[0] // CHUNKS
     per = n * piece
-    line.enter()
+    shard = pack.shape[1]
+    d = lax.axis_index("dp")
+    bits = bits_of(m)
+    outer = bits[1:]
+    height = pack.shape[0] // (2 * PARTS)
+    doubling = []
+    for i in range(2 * PARTS):
+        order = (outer if i % 2 == 0 else outer[::-1]) + bits[:1]
+        doubling.append(
+            Doubling(
+                m, pack, weight, pl.ds(i * height, height), order, i * (m - 1), wide_send, wide_recv
+            )
+        )
+    first = doubling[0]
+    line.enter(["dp", [first.flip(d, bit) for bit in bits]])
     local, gathers = [], []
+    columns = pl.ds(pl.multiple_of(d * shard, shard), shard)
+    keep = pltpu.make_async_copy(pack, weight.at[:, columns], copy_sem.at[CHUNKS])
     for h in range(CHUNKS):
         mine = own.at[pl.ds(h * piece, piece)]
-        keep = pltpu.make_async_copy(mine, out.at[pl.ds(h * per, piece)], copy_sem.at[h])
-        keep.start()
-        local.append(keep)
+        local.append(
+            pltpu.make_async_copy(mine, out.at[pl.ds(h * per, piece)], copy_sem.at[h])
+        )
 
         def slot(k, h=h, mine=mine):
             return mine if k == 0 else out.at[pl.ds(h * per + k * piece, piece)]
 
         gathers.append(Gather(line, slot))
-    for _ in range(n):
-        for g in gathers:
-            g.step()
-    for keep in local:
-        keep.wait()
+    local.append(keep)
+
+    def line_step(items):
+        for item in items:
+            item.step()
+
+    half = CHUNKS // 2
+    line_step(gathers)
+    line_step(doubling)
+    for item in local:
+        item.start()
+    for level in range(1, max(n, len(bits) + 1)):
+        for side in range(2):
+            if level <= len(bits):
+                line_step(doubling[side * PARTS : (side + 1) * PARTS])
+            if level < n:
+                line_step(gathers[side * half : (side + 1) * half])
+    for item in local:
+        item.wait()
+    for item in gathers:
+        assert item.step_no == n
+    for item in doubling:
+        assert item.done == len(bits) + 1
+        item.leave()
     line.leave()
 
 
-def gather_rows(own, n):
+def gather_rows(own, pack, n, m):
     rows, width = own.shape
     count = CHUNKS * 2 * (n - 1)
+    wide = 2 * PARTS * (m - 1)
     return pl.pallas_call(
-        functools.partial(gather_kernel, n),
-        out_shape=jax.ShapeDtypeStruct((n * rows, width), own.dtype),
-        in_specs=[VM],
-        out_specs=ANY,
+        functools.partial(gather_kernel, n, m),
+        out_shape=(
+            jax.ShapeDtypeStruct((n * rows, width), own.dtype),
+            jax.ShapeDtypeStruct((pack.shape[0], m * pack.shape[1]), pack.dtype),
+        ),
+        in_specs=[VM, VM],
+        out_specs=(ANY, ANY),
         scratch_shapes=[
             pltpu.SemaphoreType.DMA((count,)),
             pltpu.SemaphoreType.DMA((count,)),
-            pltpu.SemaphoreType.DMA((CHUNKS,)),
+            pltpu.SemaphoreType.DMA((CHUNKS + 1,)),
+            pltpu.SemaphoreType.DMA((wide,)),
+            pltpu.SemaphoreType.DMA((wide,)),
         ],
         compiler_params=pltpu.CompilerParams(collective_id=0, has_side_effects=True),
         name="gather_rows",
-    )(own)
+    )(own, pack)
 
 
 def no_neighbour_zero(n, place, from_left, from_right):
@@ -747,7 +858,6 @@
     pack_one = pad_rows(
         jnp.concatenate([w_query.T, w_key.T, w_value.T, w_gate.T], axis=0), one_wide
     )
-    weight_one = lax.all_gather(pack_one, "dp", axis=1, tiled=True)
     glu_pack = jnp.stack(
         [
             pad_rows(w_glu_gate.T, f_wide).reshape(f_tiles, LANES, shard),
@@ -756,12 +866,13 @@
         axis=1,
     ).reshape(2 * f_wide, shard)
     pack_two = jnp.concatenate([glu_pack, pad_rows(w_down, f_wide), pad_rows(w_out, v_wide)], axis=0)
-    pack_two, weight_one = lax.optimization_barrier((pack_two, weight_one))
     weight_two = lax.all_gather(pack_two, "dp", axis=1, tiled=True)
     out_weight = weight_two[3 * f_wide :]
 
     first_hat, first_scale = layer_norm(inputs.astype(F32), epsilon)
-    rows_one = gather_rows((first_hat * first_norm_gain).astype(BF), n)
+    rows_one, weight_one = gather_rows(
+        (first_hat * first_norm_gain).astype(BF), pack_one, n, lax.axis_size("dp")
+    )
     tokens = rows_one.shape[0]
 
     slot_shard = lax.rem(place - jnp.arange(n) + n, n)

time: 779 us -> 729 us (0.936)
  waiting for transfers between devices: 95.6 us -> 26.8 us
  Pallas kernels: 462 us -> 488 us
    all_gather x1 -> x0, waiting for transfers between devices: 70.9 us -> none  [body(): weight_one = lax.all_gather(pack_one, 'dp', axis=1, tiled=True)]
    pallas_call x1, Pallas kernels: 73 us -> 102 us  [gather_rows(): pl.pallas_call(functools.partial(gather_kernel, n, m), out_shape=(jax.Sha...]
    unnamed x100 -> x104, local copies, waits for them, and re-layouts: 19.4 us -> 14.5 us
  transfers between devices with their start and end apart: 5 -> 4, of which waited for: 2 -> 1; matrix products, arithmetic and copies ran while one was open for 19% -> 20% of each run, Pallas kernels for 22% -> 27%
where the time goes in v4:
time: 729 us; the launch traced here: 723 us
  Pallas kernels  488 us (67%)
  matrix products  90.6 us (12%)
  local copies, waits for them, and re-layouts  59.4 us (8%)
  other arithmetic  42.7 us (6%)
  waiting for transfers between devices  26.8 us (4%)
  between operations  14.8 us (2%)
    pallas_call x1, Pallas kernels, middle_call(): pl.pallas_call(functools.partial(middle_kernel, n), out_shape=(shape((tok...  295 us
    pallas_call x1, Pallas kernels, gather_rows(): pl.pallas_call(functools.partial(gather_kernel, n, m), out_shape=(jax.Sha...  102 us
    pallas_call x1, Pallas kernels, last_call(): pl.pallas_call(functools.partial(last_kernel, n), out_shape=jax.ShapeDtyp...  77.2 us
    dot_general x5, matrix products, dot_tn(): lax.dot_general(a, b, (((0,), (0,)), ((), ())), preferred_element_type=F32)  40.3 us
    dot_general x4, matrix products, dot_nt(): lax.dot_general(a, b, (((1,), (1,)), ((), ())), preferred_element_type=F32)  35.7 us
    reduce_scatter x1, waiting for transfers between devices, body(): lax.psum_scatter(grads_two, 'dp', scatter_dimension=1, tiled=True)  26.7 us
  transfers between devices with their start and end apart: 4, of which 1 were waited for; matrix products, arithmetic and copies ran while one was open for 20% of the time, Pallas kernels for 27%

profile of v4, /device:TPU:0, one launch (start us, length us, event | category | flops | bytes accessed | tf_op | source)
XLA Modules:
  0.0 722.6 jit_solution(14701656414508242688)
XLA Ops:
  16.3 101.9 %gather_rows.1 = (bf16[1024,2048]{1,0:T(8,128)(2,1)}, bf16[2816,2048]{1,0:T(8,128)(2,1)}) custom-call(bf16[256,2048]{1,0:T(8,128)(2,1)} %fusion.29.own, bf16[2816,256]{1,0:T(8,128)(2,1)} %fusion.46.pack), custom_call_target="tpu_custom_call" | custom-call | tf_op jit(solution)/shard_map/gather_rows/pallas_call | solution.py:338
  118.3 8.0 %fusion.36 = bf16[1024,1024]{0,1:T(8,128)(2,1)S(1)} fusion(bf16[1024,2048]{1,0:T(8,128)(2,1)} %get-tuple-element.22, bf16[2816,2048]{1,0:T(8,128)(2,1)} %get-tuple-element.23.weight), kind=kOutput, calls=%fused_computation.62 | convolution fusion | flops 4296015872 | bytes 10485760 | tf_op jit(solution)/shard_map/dot_general | solution.py:43
  126.8 1.5 fusion.2
  128.3 3.4 multiply_convert_fusion.1
  131.8 7.4 %fusion.41 = bf16[1024,864]{0,1:T(8,128)(2,1)S(1)} fusion(bf16[1024,2048]{1,0:T(8,128)(2,1)S(1)} %copy-done.35, bf16[2816,2048]{1,0:T(8,128)(2,1)} %get-tuple-element.23.weight), kind=kOutput, calls=%fused_computation.67 | convolution fusion | flops 3624763392 | bytes 9502720 | tf_op jit(solution)/shard_map/dot_general | solution.py:43
  139.2 2.1 bitcast_reduce_fusion
  143.1 3.7 copy.73
  146.8 10.9 %multiply_convert_fusion.3 = (bf16[1024,864]{1,0:T(8,128)(2,1)S(1)}, f32[1024,864]{1,0:T(8,128)}) fusion(f32[1024,864]{1,0:T(8,128)} %copy.73, bf16[1024,2048]{1,0:T(8,128)(2,1)} %get-tuple-element.22, bf16[2816,2048]{1,0:T(8,128)(2,1)} %get-tuple-element.23.weight), kind=kOutput, calls=%fused_computation.21 | convolution fusion | flops 3629187072 | bytes 16711680 | tf_op jit(solution)/shard_map/dot_general | solution.py:43
  160.4 295.1 %middle.1 = (bf16[1024,2048]{1,0:T(8,128)(2,1)}, bf16[1024,2048]{1,0:T(8,128)(2,1)}, bf16[1024,2048]{1,0:T(8,128)(2,1)}, bf16[1024,896]{1,0:T(8,128)(2,1)}, bf16...) custom-call(bf16[1024,896]{1,0:T(8,128)(2,1)} %pad.26.gated, ...), custom_call_target="tpu_custom_call" | custom-call | tf_op jit(solution)/shard_map/middle/pallas_call | solution.py:637
  455.5 6.8 convolution_convert_fusion.4
  462.3 9.4 %multiply_convert_fusion.2 = (bf16[1024,864]{1,0:T(8,128)(2,1)S(1)}, f32[1024,864]{1,0:T(8,128)}) fusion(f32[1024,864]{1,0:T(8,128)S(1)} %copy-done.9, f32[1024,864]{1,0:T(8,128)S(1)} %copy-done.48, bf16[1024,2048]{1,0:T(8,128)(2,1)S(1)} %copy-done.39, bf16[3584,2048]{1,0:T(8,128)(2,1)} %all-gather.2.cloned.1.call-done.weights), kind=kOutput, calls=%fused_computation.20 | convolution fusion | flops 3633610752 | bytes 20119552 | tf_op jit(solution)/shard_map/dot_general | solution.py:43
  472.9 5.4 convolution_convert_fusion.3
  478.4 6.1 pad_maximum_fusion.1
  484.5 5.7 copy.77
  490.2 3.7 fusion.53
  495.4 1.8 copy-done.8
  498.5 4.4 multiply_convert_fusion
  506.4 2.0 convolution_convert_fusion.5
  510.2 13.3 %convolution_convert_fusion.1 = bf16[1888,2048]{1,0:T(8,128)(2,1)} fusion(bf16[1024,2048]{1,0:T(8,128)(2,1)S(1)} %copy-done.37, bf16[1024,864]{0,1:T(8,128)(2,1)S(1)} %bitcast.96, bf16[1024,512]{0,1:T(8,128)(2,1)S(1)} %bitcast.98, bf16[1024,512]{0,1:T(8,128)(2,1)S(1)} %bitcast.100), kind=kOutput, calls=%fused_computation.5 | convolution fusion | flops 7934312448 | bytes 15794176 | tf_op jit(solution)/shard_map/dot_general | solution.py:51
  525.0 6.5 convolution_convert_fusion.2
  531.5 8.3 %convolution_convert_fusion = bf16[1792,2048]{1,0:T(8,128)(2,1)S(1)} fusion(bf16[1024,1792]{1,0:T(8,128)(2,1)S(1)} %copy-done.40, bf16[1024,2048]{1,0:T(8,128)(2,1)S(1)} %copy-done.38), kind=kOutput, calls=%fused_computation.4 | convolution fusion | flops 7519862784 | bytes 15204352 | tf_op jit(solution)/shard_map/dot_general | solution.py:51
  539.8 13.8 %pad_maximum_fusion = bf16[2688,2048]{1,0:T(8,128)(2,1)} fusion(bf16[896,2048]{1,0:T(8,128)(2,1)S(1)} %convolution_convert_fusion.2, bf16[1792,2048]{1,0:T(8,128)(2,1)S(1)} %convolution_convert_fusion), kind=kLoop, calls=%fused_computation | loop fusion | flops 22020096 | bytes 22020096 | tf_op jit(solution)/shard_map/concatenate | solution.py:914
  554.2 2.3 copy.92
  556.5 3.1 copy.83
  559.6 9.8 %concatenate.26 = bf16[1024,2752]{1,0:T(8,128)(2,1)} concatenate(bf16[1024,512]{1,0:T(8,128)(2,1)} %copy.92, bf16[1024,512]{1,0:T(8,128)(2,1)S(1)} %copy.93, bf16[1024,864]{1,0:T(8,128)(2,1)S(1)} %copy.83, bf16[1024,864]{1,0:T(8,128)(2,1)} %copy-done.11), dimensions={1} | concatenate | bytes 11272192 | tf_op jit(solution)/shard_map/concatenate | solution.py:942
  569.3 5.5 pad.31.grads
  574.9 77.2 %last.1 = f32[256,2048]{1,0:T(8,128)} custom-call(bf16[1024,2816]{1,0:T(8,128)(2,1)} %pad.31.grads, bf16[2816,2048]{1,0:T(8,128)(2,1)} %get-tuple-element.23.weight), custom_call_target="tpu_custom_call" | custom-call | tf_op jit(solution)/shard_map/last/pallas_call | solution.py:800
  652.1 3.1 fusion.34
  655.8 14.0 %sum_gains.1 = f32[32,128]{1,0:T(8,128)} custom-call(f32[32,128]{1,0:T(8,128)} %reshape.293.mine), custom_call_target="tpu_custom_call" | custom-call | tf_op jit(solution)/shard_map/sum_gains/pallas_call | solution.py:720
  671.2 3.9 fusion.33
  675.1 2.0 slice.88
  683.8 26.7 %reduce-scatter.8.cloned.1.call-done = bf16[2688,256]{1,0:T(8,128)(2,1)} async-done(((bf16[2688,2048]{1,0:T(8,128)(2,1)}), bf16[2688,256]{1,0:T(8,128)(2,1)}) %reduce-scatter.8.cloned.1.call-update) | async-done | bytes 1376272 | tf_op jit(solution)/shard_map/reduce_scatter | solution.py:915
  (164 shorter events, 39.2 us)
Async XLA Ops:
  7.2 153.2 %all-gather.2.cloned.1.call-start = ((), (), s32[]{:S(2)}) async-start(), calls=%async_computation.3 | async-start | bytes 16515072 | tf_op jit(solution)/shard_map/all_gather | solution.py:869
  9.6 4.2 copy-start.23
  9.6 4.2 copy-start.24
  11.1 3.9 copy-start.27
  11.1 664.0 %reduce-scatter.6.cloned.1.call-start = ((), (), s32[]{:S(2)}) async-start(), calls=%async_computation.5 | async-start | bytes 7962624 | tf_op jit(solution)/shard_map/reduce_scatter | solution.py:928
  13.3 104.9 %copy-start.30 = (f32[256]{0:T(256)}, f32[256]{0:T(256)S(1)}, u32[]{:S(2)}) copy-start(f32[256]{0:T(256)S(1)} %broadcast_multiply_fusion.5) | copy-start | bytes 3076
  13.7 104.5 %copy-start.32 = (f32[256]{0:T(256)}, f32[256]{0:T(256)S(1)}, u32[]{:S(2)}) copy-start(f32[256]{0:T(256)S(1)} %add_rsqrt_fusion.1) | copy-start | bytes 3076
  118.2 10.1 %copy-start.44 = (f32[2]{0:T(128)}, f32[2]{0:T(128)S(1)}, u32[]{:S(2)}) copy-start(f32[2]{0:T(128)S(1)} %negate_log-plus-one_fusion) | copy-start | bytes 28
  126.4 5.3 copy-start.17
  126.5 5.3 copy-start.19
  126.8 5.0 copy-start.7
  131.8 7.4 %copy-start.46 = (bf16[2,1024,1024]{2,1,0:T(8,128)(2,1)}, bf16[2,1024,1024]{2,1,0:T(8,128)(2,1)S(1)}, u32[]{:S(2)}) copy-start(bf16[2,1024,1024]{2,1,0:T(8,128)(2,1)S(1)} %multiply_convert_fusion.1) | copy-start | bytes 12582916
  455.5 6.8 copy-start.9
  455.5 6.8 copy-start.39
  455.5 6.8 copy-start.48
  462.3 10.6 %copy-start.36 = (bf16[1024,2048]{1,0:T(8,128)(2,1)S(1)}, bf16[1024,2048]{1,0:T(8,128)(2,1)}, u32[]{:S(2)}) copy-start(bf16[1024,2048]{1,0:T(8,128)(2,1)} %get-tuple-element.22) | copy-start | bytes 12582916
  484.4 5.7 copy-start.1
  484.5 194.9 %reduce-scatter.4.cloned.1.call-start = ((), (), s32[]{:S(2)}) async-start(), calls=%async_computation.4 | async-start | bytes 8699904 | tf_op jit(solution)/shard_map/reduce_scatter | solution.py:940
  490.2 4.2 copy-start.4
  494.4 4.1 copy-start.43
  494.4 4.1 copy-start.45
  498.5 4.4 copy-start.20
  506.4 3.8 copy-start.37
  523.5 187.0 %reduce-scatter.8.cloned.1.call-start = ((), (), s32[]{:S(2)}) async-start(), calls=%async_computation.6 | async-start | bytes 12386304 | tf_op jit(solution)/shard_map/reduce_scatter | solution.py:915
  525.0 6.5 copy-start.38
  525.0 6.5 copy-start.40
  574.9 77.2 %copy-start.29 = (f32[8,2048]{1,0:T(8,128)S(1)}, f32[8,2048]{1,0:T(8,128)}, u32[]{:S(2)}) copy-start(f32[8,2048]{1,0:T(8,128)} %get-tuple-element.27) | copy-start | bytes 196612
  574.9 77.2 %copy-start.28 = (f32[2048]{0:T(1024)S(1)}, f32[2048]{0:T(1024)}, u32[]{:S(2)}) copy-start(f32[2048]{0:T(1024)} %param.15) | copy-start | bytes 24580
  574.9 77.3 %copy-start.31 = (f32[256]{0:T(256)S(1)}, f32[256]{0:T(256)}, u32[]{:S(2)}) copy-start(f32[256]{0:T(256)} %copy-done.30) | copy-start | bytes 3076
  574.9 77.3 %copy-start.33 = (f32[256]{0:T(256)S(1)}, f32[256]{0:T(256)}, u32[]{:S(2)}) copy-start(f32[256]{0:T(256)} %copy-done.32) | copy-start | bytes 3076
  652.0 19.1 %copy-start.3 = (bf16[256,2048]{1,0:T(8,128)(2,1)S(1)}, bf16[256,2048]{1,0:T(8,128)(2,1)}, u32[]{:S(2)}) copy-start(bf16[256,2048]{1,0:T(8,128)(2,1)} %own.1) | copy-start | bytes 3145732
  652.1 19.1 %copy-start.5 = (f32[256,2048]{1,0:T(8,128)S(1)}, f32[256,2048]{1,0:T(8,128)}, u32[]{:S(2)}) copy-start(f32[256,2048]{1,0:T(8,128)} %last.1) | copy-start | bytes 6291460
  (21 other events, 50.2 us)
Sparse Core Ops, SparseCore 0:
  11.2 122.4 all-gather.1
  484.6 64.6 reduce-scatter.5
  552.8 68.6 reduce-scatter.3
  624.9 85.5 reduce-scatter.7

commit v5 on v4

--- a/solution.py
+++ b/solution.py
@@ -12,6 +12,7 @@
 HV = 432
 LEN = 1024
 CHUNKS = 4
+FRONT = CHUNKS // 2
 LANES = 128
 VMEM_MOST = 66_000_000
 
@@ -375,12 +376,11 @@
 }
 TUNED = {
     (4, 4): [
-        0, 4, 8, 0, 5, 8, 1, 0, 8, 9, 6, 1, 12, 9, 16, 9, 10, 16, 0, 3,
-        10, 16, 7, 11, 1, 13, 17, 16, 20, 10, 20, 11, 1, 17, 40, 14, 2, 11, 18, 24,
-        17, 2, 28, 44, 15, 19, 17, 21, 2, 18, 28, 44, 21, 41, 18, 19, 3, 2, 45, 28,
-        25, 29, 18, 45, 22, 3, 29, 22, 42, 29, 32, 19, 46, 26, 36, 46, 3, 33, 19, 44,
-        30, 23, 36, 23, 37, 45, 30, 46, 30, 37, 43, 27, 31, 47, 36, 34, 38, 36, 31, 47,
-        50, 37, 37, 38, 31, 48, 47, 35, 38, 39, 49, 39, 38, 39, 51, 39,
+        2, 4, 8, 8, 5, 2, 8, 6, 9, 10, 2, 9, 12, 16, 7, 9, 11, 16, 13, 10,
+        11, 16, 16, 17, 2, 20, 11, 10, 20, 17, 15, 19, 14, 24, 17, 18, 40, 28, 17, 21,
+        18, 28, 18, 3, 21, 28, 25, 19, 18, 29, 22, 29, 32, 3, 36, 44, 19, 22, 26, 36,
+        30, 41, 30, 3, 42, 44, 19, 3, 29, 30, 23, 44, 23, 36, 34, 33, 38, 37, 27, 31,
+        38, 31, 37, 38, 31, 45, 45, 35, 39, 36, 45, 39, 49, 48, 37, 43, 37, 39, 39, 38,
     ],
 }
 
@@ -399,13 +399,15 @@
         for k, (first, later, each) in DUE.items()
         for h in range(CHUNKS)
         for s in range(count[k])
+        if not (k == COT and h < FRONT or k in (DOWN_SUM, END_DOWN) and h >= FRONT)
     )
     taken, order = {}, []
     while todo:
         for item in todo:
             _, k, h, s = item
             ready = taken.get((k, h), 0) == s and all(
-                taken.get((need, h), 0) == count[need] for need in needs.get(k, [])
+                taken.get((need, h), 0) == count[need] or (need == COT and h < FRONT)
+                for need in needs.get(k, [])
             )
             if ready:
                 break
@@ -416,8 +418,9 @@
 
 
 def middle_kernel(
-    n, gated, weights, own, cot, gain,
-    rows_out, cot_out, mid_out, hidden_out, glu_out, outputs, d_middle, gain_out,
+    n, gated, weights, own, cot, cot_front, gain,
+    rows_out, cot_out, mid_out, hidden_out, glu_out, down_out, outputs, middle_out, d_middle,
+    gain_out,
     gated_v, wo_v, wg_v, wd_v, own_v, cot_v, rows_v, hidden_v, glu_v, part, part_two,
     left_a, right_a, left_b, right_b, middle, stage, copy_sem, send_sem, recv_sem,
 ):
@@ -439,8 +442,10 @@
         return ref.at[pl.ds(h * per + k * piece, size)]
 
     load_cot = [
-        local(cot.at[pl.ds(h * piece, piece)], rows_at(cot_v, h)) for h in range(CHUNKS)
+        local(cot.at[pl.ds(h * piece, piece)], rows_at(cot_v, h)) for h in range(FRONT, CHUNKS)
     ]
+    front = pl.ds(0, FRONT * per)
+    load_cot.append(local(cot_front, cot_v.at[front]))
     load_gated = local(gated, gated_v)
     load_wo = local(weights.at[pl.ds(3 * wide, wo_v.shape[0])], wo_v)
     load_own = local(own, own_v)
@@ -449,6 +454,7 @@
     line.enter()
     for h in range(CHUNKS):
         no_neighbour_zero(n, place, left_a.at[h, n - 2], right_a.at[h, n - 2])
+    for h in range(FRONT):
         no_neighbour_zero(n, place, left_b.at[h, n - 2], right_b.at[h, n - 2])
     gain_out[...] = jnp.zeros_like(gain_out)
 
@@ -461,7 +467,9 @@
             add_into,
         )
 
-    gather_cot = [Gather(line, functools.partial(rows_at, cot_v, h)) for h in range(CHUNKS)]
+    gather_cot = {
+        h: Gather(line, functools.partial(rows_at, cot_v, h)) for h in range(FRONT, CHUNKS)
+    }
     gather_two = [Gather(line, functools.partial(rows_at, rows_v, h)) for h in range(CHUNKS)]
 
     def mid_slot(h, k):
@@ -469,14 +477,24 @@
 
     gather_mid = [Gather(line, functools.partial(mid_slot, h)) for h in range(CHUNKS)]
     scatter_one = [scatter(part, left_a, right_a, h) for h in range(CHUNKS)]
-    scatter_two = [scatter(part_two, left_b, right_b, h) for h in range(CHUNKS)]
+    scatter_two = [scatter(part_two, left_b, right_b, h) for h in range(FRONT)]
     scatter_grad = [scatter(part, left_a, right_a, h) for h in range(CHUNKS)]
 
     def chunk(ref, h):
         return ref.at[pl.ds(h * per, per)]
 
     def out_product(h):
-        product_tiles(chunk(part, h), chunk(gated_v, h), wo_v, 2 * LANES)
+        heads, _, size = gated_v.shape
+        target, whole = chunk(part, h), pl.ds(h * per, per)
+
+        def step(j, carry):
+            at = pl.ds(pl.multiple_of(j * 2 * LANES, 2 * LANES), 2 * LANES)
+            target[:, at] = sum(
+                dot_nn(gated_v[i, whole, :], wo_v[pl.ds(i * size, size), at]) for i in range(heads)
+            ).astype(BF)
+            return carry
+
+        lax.fori_loop(0, width // (2 * LANES), step, 0)
 
     def finish_one(h):
         scatter_one[h].finish()
@@ -614,24 +632,28 @@
         local(chunk(cot_v, c), chunk(cot_out, c))
         local(chunk(hidden_v, c), chunk(hidden_out, c))
         local(chunk(glu_v, c), chunk(glu_out, c))
-    for item in gather_cot + gather_two + gather_mid:
+    local(part_two.at[pl.ds(FRONT * per, down_out.shape[0])], down_out)
+    local(middle.at[pl.ds(FRONT * piece, middle_out.shape[0])], middle_out)
+    for item in list(gather_cot.values()) + gather_two + gather_mid:
         assert item.step_no == n
     for item in scatter_one + scatter_two + scatter_grad:
         assert item.step_no == n - 1
     for group in (scatter_grad, scatter_two):
         for item in group:
             item.drain()
-    for item in copies[CHUNKS + 5 :]:
+    for item in copies[CHUNKS - FRONT + 6 :]:
         item.wait()
     line.leave()
 
 
-def middle_call(gated, weights, own, cot, gain, n):
+def middle_call(gated, weights, own, cot, cot_front, gain, n):
     rows, width = own.shape
-    tokens, nv = gated.shape
-    wide = (weights.shape[0] - nv) // 3
+    heads, tokens, size = gated.shape
+    nv = heads * size
+    wide = (weights.shape[0] - -(-nv // LANES) * LANES) // 3
     piece = rows // CHUNKS
-    sems = CHUNKS * 6 * 2 * (n - 1)
+    back = CHUNKS - FRONT
+    sems = CHUNKS * 5 * 2 * (n - 1)
     hop = (CHUNKS, n - 1, piece, width)
     shape = jax.ShapeDtypeStruct
     return pl.pallas_call(
@@ -642,14 +664,16 @@
             shape((tokens, width), BF),
             shape((tokens, wide), BF),
             shape((tokens, 2 * wide), BF),
-            shape((rows, width), BF),
+            shape((back * n * piece, width), BF),
+            shape((FRONT * piece, width), BF),
+            shape((back * piece, width), F32),
             shape((rows, width), F32),
             shape((8, width), F32),
         ),
-        in_specs=[ANY] * 4 + [VM],
-        out_specs=(ANY,) * 5 + (VM,) * 3,
+        in_specs=[ANY] * 5 + [VM],
+        out_specs=(ANY,) * 6 + (VM, ANY, VM, VM),
         scratch_shapes=[
-            pltpu.VMEM((tokens, nv), BF),
+            pltpu.VMEM((heads, tokens, size), BF),
             pltpu.VMEM((nv, width), BF),
             pltpu.VMEM((2 * wide, width), BF),
             pltpu.VMEM((wide, width), BF),
@@ -662,11 +686,11 @@
             pltpu.VMEM((tokens, width), BF),
             pltpu.VMEM(hop, BF),
             pltpu.VMEM(hop, BF),
-            pltpu.VMEM(hop, BF),
-            pltpu.VMEM(hop, BF),
+            pltpu.VMEM((FRONT,) + hop[1:], BF),
+            pltpu.VMEM((FRONT,) + hop[1:], BF),
             pltpu.VMEM((rows, width), F32),
             pltpu.VMEM((CHUNKS, piece, width), BF),
-            pltpu.SemaphoreType.DMA((5 + 6 * CHUNKS,)),
+            pltpu.SemaphoreType.DMA((8 + 6 * CHUNKS - FRONT,)),
             pltpu.SemaphoreType.DMA((sems,)),
             pltpu.SemaphoreType.DMA((sems,)),
         ],
@@ -674,7 +698,7 @@
             collective_id=1, has_side_effects=True, vmem_limit_bytes=VMEM_MOST
         ),
         name="middle",
-    )(gated, weights, own, cot, gain)
+    )(gated, weights, own, cot, cot_front, gain)
 
 
 def gains_kernel(n, m, mine, total, first, second, send_sem, recv_sem):
@@ -734,20 +758,22 @@
 
 
 def last_kernel(
-    n, grads, weight, out, grads_v, weight_v, part, lefts, rights, copy_sem, send_sem, recv_sem
+    n, d_qk, d_value, d_gate, weight, out,
+    qk_v, value_v, gate_v, weight_v, part, lefts, rights, copy_sem, send_sem, recv_sem
 ):
     line = Line(n, send_sem, recv_sem)
     count, width = out.shape
     piece = count // CHUNKS
     per = n * piece
+    heads, _, size = value_v.shape
+    wide = qk_v.shape[1]
     load = [
-        pltpu.make_async_copy(
-            grads.at[pl.ds(h * per, per)], grads_v.at[pl.ds(h * per, per)], copy_sem.at[h]
+        pltpu.make_async_copy(src, dst, copy_sem.at[i])
+        for i, (src, dst) in enumerate(
+            [(weight, weight_v), (d_qk, qk_v), (d_value, value_v), (d_gate, gate_v)]
         )
-        for h in range(CHUNKS)
     ]
-    load_weight = pltpu.make_async_copy(weight, weight_v, copy_sem.at[CHUNKS])
-    for item in load + [load_weight]:
+    for item in load:
         item.start()
     line.enter()
     for h in range(CHUNKS):
@@ -763,24 +789,38 @@
         for h in range(CHUNKS)
     ]
 
+    def product(h):
+        rows = pl.ds(h * per, per)
+
+        def step(j, carry):
+            at = pl.ds(pl.multiple_of(j * 2 * LANES, 2 * LANES), 2 * LANES)
+            total = dot_nn(qk_v[rows, :], weight_v[pl.ds(0, wide), at])
+            for i in range(heads):
+                base = wide + i * size
+                total += dot_nn(value_v[i, rows, :], weight_v[pl.ds(base, size), at])
+                base += heads * size
+                total += dot_nn(gate_v[i, rows, :], weight_v[pl.ds(base, size), at])
+            part[rows, at] = total.astype(BF)
+            return carry
+
+        lax.fori_loop(0, width // (2 * LANES), step, 0)
+
     def finish(h):
         scatters[h].finish()
 
         def step(at):
-            src = at(h * per)
             out[at(h * piece), :] = (
-                part[src, :].astype(F32)
+                part[at(h * per), :].astype(F32)
                 + lefts[h, n - 2, at(), :].astype(F32)
                 + rights[h, n - 2, at(), :].astype(F32)
             )
 
         blocks(piece, step)
 
-    load_weight.wait()
+    for item in load:
+        item.wait()
     for h in range(CHUNKS):
-        load[h].wait()
-        rows = pl.ds(h * per, per)
-        product_tiles(part.at[rows], grads_v.at[rows], weight_v, 2 * LANES)
+        product(h)
         scatters[h].step()
     for _ in range(n - 2):
         for h in range(CHUNKS):
@@ -791,8 +831,8 @@
         scatters[h].drain()
 
 
-def last_call(grads, weight, n):
-    tokens, deep = grads.shape
+def last_call(d_qk, d_value, d_gate, weight, n):
+    tokens = d_qk.shape[0]
     width = weight.shape[1]
     rows = tokens // n
     sems = CHUNKS * 2 * (n - 1)
@@ -800,15 +840,17 @@
     return pl.pallas_call(
         functools.partial(last_kernel, n),
         out_shape=jax.ShapeDtypeStruct((rows, width), F32),
-        in_specs=[ANY, ANY],
+        in_specs=[ANY] * 4,
         out_specs=VM,
         scratch_shapes=[
-            pltpu.VMEM((tokens, deep), BF),
-            pltpu.VMEM((deep, width), BF),
+            pltpu.VMEM(d_qk.shape, BF),
+            pltpu.VMEM(d_value.shape, BF),
+            pltpu.VMEM(d_gate.shape, BF),
+            pltpu.VMEM(weight.shape, BF),
             pltpu.VMEM((tokens, width), BF),
             pltpu.VMEM(hop, BF),
             pltpu.VMEM(hop, BF),
-            pltpu.SemaphoreType.DMA((CHUNKS + 1,)),
+            pltpu.SemaphoreType.DMA((4,)),
             pltpu.SemaphoreType.DMA((sems,)),
             pltpu.SemaphoreType.DMA((sems,)),
         ],
@@ -816,7 +858,332 @@
             collective_id=2, has_side_effects=True, vmem_limit_bytes=VMEM_MOST
         ),
         name="last",
-    )(grads, weight)
+    )(d_qk, d_value, d_gate, weight)
+
+
+TILE = 256
+
+
+def tiles_of(count, step):
+    def run(i, carry):
+        step(pl.ds(pl.multiple_of(i * TILE, TILE), TILE))
+        return carry
+
+    lax.fori_loop(0, count // TILE, run, 0)
+
+
+def in_order(units, steps):
+    taken = 0
+    for i, unit in enumerate(units):
+        unit()
+        upto = (i + 1) * len(steps) // len(units)
+        for step in steps[taken:upto]:
+            step()
+        taken = upto
+
+
+def forward_kernel(
+    n, rows, weight, cot, col, row,
+    query_o, key_o, value_o, gate_o, norm_o, scale_o, scores_o, gated_o, cot_o,
+    rows_v, weight_v, query_v, key_v, value_v, gate_v, norm_v, scale_v, scores_v, gated_v, cot_v,
+    copy_sem, send_sem, recv_sem,
+):
+    line = Line(n, send_sem, recv_sem)
+    heads, tokens, deep = query_v.shape
+    size = value_v.shape[2]
+    per = cot_v.shape[0] // FRONT
+    piece = per // n
+    copies = []
+
+    def local(src, dst):
+        c = pltpu.make_async_copy(src, dst, copy_sem.at[len(copies)])
+        copies.append(c)
+        c.start()
+        return c
+
+    load_cot = [
+        local(cot.at[pl.ds(h * piece, piece)], cot_v.at[pl.ds(h * per, piece)])
+        for h in range(FRONT)
+    ]
+    load_rows, load_weight = local(rows, rows_v), local(weight, weight_v)
+    line.enter()
+    gathers = [
+        Gather(line, lambda k, h=h: cot_v.at[pl.ds(h * per + k * piece, piece)])
+        for h in range(FRONT)
+    ]
+    for item in load_cot:
+        item.wait()
+    for g in gathers:
+        g.step()
+    load_rows.wait()
+    load_weight.wait()
+
+    def project(target, h, base, width):
+        def step(at):
+            target[h, at, :] = dot_nt(rows_v[at, :], weight_v[pl.ds(base, width), :]).astype(
+                target.dtype
+            )
+
+        return lambda: tiles_of(tokens, step)
+
+    def attend(h):
+        def step(at):
+            allowed = (col[at, 0:1] >= row[0:1, :]) & (col[at, 1:2] == row[1:2, :])
+            scores = dot_nt(query_v[h, at, :], key_v[h]) * col[at, 2 + h : 3 + h]
+            scores = jnp.where(allowed, scores * row[2 + h : 3 + h, :], 0.0).astype(BF)
+            scores_v[h, at, :] = scores
+            hat, scale = layer_norm(dot_nn(scores, value_v[h]), group_epsilon)
+            norm_v[h, at, :] = hat
+            scale_v[h, at, :] = scale
+            gate = gate_v[h, at, :]
+            gated_v[h, at, :] = (gate * jax.nn.sigmoid(gate) * hat).astype(BF)
+
+        return lambda: tiles_of(tokens, step)
+
+    values, gates = 2 * heads * deep, 2 * heads * deep + heads * size
+    units = []
+    for h in range(heads):
+        units += [
+            project(query_v, h, h * deep, deep),
+            project(key_v, h, (heads + h) * deep, deep),
+            project(value_v, h, values + h * size, size),
+            project(gate_v, h, gates + h * size, size),
+            attend(h),
+        ]
+    in_order(units, [g.step for _ in range(n - 1) for g in gathers])
+    count = len(copies)
+    for src, dst in (
+        (query_v, query_o), (key_v, key_o), (value_v, value_o), (gate_v, gate_o),
+        (norm_v, norm_o), (scale_v, scale_o), (scores_v, scores_o), (gated_v, gated_o),
+        (cot_v, cot_o),
+    ):
+        local(src, dst)
+    for item in copies[count:]:
+        item.wait()
+    line.leave()
+
+
+def forward_call(rows, weight, cot, col, row, n, heads):
+    tokens, width = rows.shape
+    shape = jax.ShapeDtypeStruct
+    outs = (
+        shape((heads, tokens, HK), BF),
+        shape((heads, tokens, HK), BF),
+        shape((heads, tokens, HV), BF),
+        shape((heads, tokens, HV), F32),
+        shape((heads, tokens, HV), F32),
+        shape((heads, tokens, 1), F32),
+        shape((heads, tokens, tokens), BF),
+        shape((heads, tokens, HV), BF),
+        shape((tokens * FRONT // CHUNKS, width), BF),
+    )
+    sems = FRONT * 2 * (n - 1)
+    return pl.pallas_call(
+        functools.partial(forward_kernel, n),
+        out_shape=outs,
+        in_specs=[ANY] * 3 + [VM] * 2,
+        out_specs=(ANY,) * len(outs),
+        scratch_shapes=[pltpu.VMEM(rows.shape, BF), pltpu.VMEM(weight.shape, BF)]
+        + [pltpu.VMEM(o.shape, o.dtype) for o in outs]
+        + [
+            pltpu.SemaphoreType.DMA((FRONT + 2 + len(outs),)),
+            pltpu.SemaphoreType.DMA((sems,)),
+            pltpu.SemaphoreType.DMA((sems,)),
+        ],
+        compiler_params=pltpu.CompilerParams(
+            collective_id=4, has_side_effects=True, vmem_limit_bytes=VMEM_MOST
+        ),
+        name="forward",
+    )(rows, weight, cot, col, row)
+
+
+def backward_kernel(
+    n, mid, weights, gate, norm, scale, scores, query, key, value, down, middle, col, row,
+    qk_o, value_o, gate_o, outputs,
+    mid_v, wo_v, gate_v, norm_v, scale_v, scores_v, query_v, key_v, value_v, part, middle_v,
+    d_qk, d_value, d_gate, d_kept, d_scores, lefts, rights, copy_sem, send_sem, recv_sem,
+):
+    line = Line(n, send_sem, recv_sem)
+    heads, tokens, deep = query_v.shape
+    size = value_v.shape[2]
+    back = CHUNKS - FRONT
+    per = part.shape[0] // back
+    piece = per // n
+    copies = []
+
+    def local(src, dst):
+        c = pltpu.make_async_copy(src, dst, copy_sem.at[len(copies)])
+        copies.append(c)
+        c.start()
+        return c
+
+    load_part = local(down, part)
+    loads = [
+        local(src, dst)
+        for src, dst in (
+            (mid, mid_v), (weights.at[pl.ds(weights.shape[0] - wo_v.shape[0], wo_v.shape[0])], wo_v),
+            (gate, gate_v), (norm, norm_v), (scale, scale_v), (value, value_v), (key, key_v),
+            (query, query_v), (scores, scores_v), (middle, middle_v),
+        )
+    ]
+    line.enter()
+    for h in range(back):
+        no_neighbour_zero(n, line.place, lefts.at[h, n - 2], rights.at[h, n - 2])
+    scatters = [
+        Scatter(
+            line,
+            lambda k, h=h: part.at[pl.ds(h * per + k * piece, piece)],
+            lambda s, h=h: lefts.at[h, s - 1],
+            lambda s, h=h: rights.at[h, s - 1],
+            add_into,
+        )
+        for h in range(back)
+    ]
+    load_part.wait()
+    for item in scatters:
+        item.step()
+    for item in loads:
+        item.wait()
+
+    def gates(h):
+        def step(at):
+            grad = dot_nt(mid_v[at, :], wo_v[pl.ds(h * size, size), :])
+            pre, hat = gate_v[h, at, :], norm_v[h, at, :]
+            s = jax.nn.sigmoid(pre)
+            d_gate[h, at, :] = (grad * hat * (s + pre * s * (1.0 - s))).astype(BF)
+            d_kept[h, at, :] = norm_back(grad * (pre * s), hat, scale_v[h, at, :]).astype(BF)
+
+        return lambda: tiles_of(tokens, step)
+
+    def by_row(h):
+        def step(at):
+            allowed = (col[at, 0:1] >= row[0:1, :]) & (col[at, 1:2] == row[1:2, :])
+            grad = dot_nt(d_kept[h, at, :], value_v[h]) * col[at, 2 + h : 3 + h]
+            grad = jnp.where(allowed, grad * row[2 + h : 3 + h, :], 0.0).astype(BF)
+            d_scores[at, :] = grad
+            d_qk[at, pl.ds(h * deep, deep)] = dot_nn(grad, key_v[h]).astype(BF)
+
+        return lambda: tiles_of(tokens, step)
+
+    def by_column(h):
+        def step(at):
+            d_value[h, at, :] = dot_tn(scores_v[h, :, at], d_kept[h]).astype(BF)
+            d_qk[at, pl.ds((heads + h) * deep, deep)] = dot_tn(d_scores[:, at], query_v[h]).astype(
+                BF
+            )
+
+        return lambda: tiles_of(tokens, step)
+
+    units = []
+    for h in range(heads):
+        units += [gates(h), by_row(h), by_column(h)]
+    in_order(units, [item.step for _ in range(n - 2) for item in scatters])
+    count = len(copies)
+    local(d_qk, qk_o)
+    local(d_value, value_o)
+    local(d_gate, gate_o)
+    for h in range(back):
+        scatters[h].finish()
+
+        def step(at):
+            outputs[at(h * piece), :] = (
+                middle_v[at(h * piece), :]
+                + part[at(h * per), :].astype(F32)
+                + lefts[h, n - 2, at(), :].astype(F32)
+                + rights[h, n - 2, at(), :].astype(F32)
+            ).astype(BF)
+
+        blocks(piece, step)
+    for item in copies[count:]:
+        item.wait()
+    for item in scatters:
+        item.drain()
+
+
+def backward_call(mid, weights, gate, norm, scale, scores, query, key, value, down, middle, col, row, n):
+    tokens, width = mid.shape
+    heads, _, size = value.shape
+    back = CHUNKS - FRONT
+    nv = heads * size
+    shape = jax.ShapeDtypeStruct
+    outs = (
+        shape((tokens, 2 * heads * HK), BF),
+        shape(value.shape, BF),
+        shape(value.shape, BF),
+        shape(middle.shape, BF),
+    )
+    ins = (gate, norm, scale, scores, query, key, value, down, middle)
+    hop = (back, n - 1, middle.shape[0] // back, width)
+    sems = back * 2 * (n - 1)
+    wo_rows = -(-nv // LANES) * LANES
+    return pl.pallas_call(
+        functools.partial(backward_kernel, n),
+        out_shape=outs,
+        in_specs=[ANY] * 11 + [VM] * 2,
+        out_specs=(ANY,) * 3 + (VM,),
+        scratch_shapes=[pltpu.VMEM(mid.shape, BF), pltpu.VMEM((wo_rows, width), BF)]
+        + [pltpu.VMEM(a.shape, a.dtype) for a in ins]
+        + [pltpu.VMEM(o.shape, o.dtype) for o in outs[:3]]
+        + [
+            pltpu.VMEM(value.shape, BF),
+            pltpu.VMEM((tokens, tokens), BF),
+            pltpu.VMEM(hop, BF),
+            pltpu.VMEM(hop, BF),
+            pltpu.SemaphoreType.DMA((14,)),
+            pltpu.SemaphoreType.DMA((sems,)),
+            pltpu.SemaphoreType.DMA((sems,)),
+        ],
+        compiler_params=pltpu.CompilerParams(
+            collective_id=5, has_side_effects=True, vmem_limit_bytes=VMEM_MOST
+        ),
+        name="backward",
+    )(mid, weights, *ins, col, row)
+
+
+def products_kernel(plan, arrays, *refs):
+    ins, out = refs[:arrays], refs[arrays]
+    held, result, copy_sem = refs[arrays + 1 : 2 * arrays + 1], refs[-2], refs[-1]
+    loads = [pltpu.make_async_copy(a, b, copy_sem.at[i]) for i, (a, b) in enumerate(zip(ins, held))]
+    for item in loads:
+        item.start()
+    waited, stores, base = set(), [], 0
+    for left, head, start, size, right in plan:
+        for i in (left, right):
+            if i not in waited:
+                loads[i].wait()
+                waited.add(i)
+        target = pl.ds(base, size)
+
+        def step(j, carry):
+            at = pl.ds(pl.multiple_of(j * 4 * LANES, 4 * LANES), 4 * LANES)
+            source = held[left][head] if head is not None else held[left][:, pl.ds(start, size)]
+            result[target, at] = dot_tn(source, held[right][:, at]).astype(BF)
+            return carry
+
+        lax.fori_loop(0, result.shape[1] // (4 * LANES), step, 0)
+        store = pltpu.make_async_copy(
+            result.at[target], out.at[target], copy_sem.at[arrays + len(stores)]
+        )
+        store.start()
+        stores.append(store)
+        base += size
+    for item in stores:
+        item.wait()
+
+
+def weight_products(plan, arrays, name):
+    rows = sum(p[3] for p in plan)
+    width = arrays[plan[0][4]].shape[1]
+    return pl.pallas_call(
+        functools.partial(products_kernel, plan, len(arrays)),
+        out_shape=jax.ShapeDtypeStruct((rows, width), BF),
+        in_specs=[ANY] * len(arrays),
+        out_specs=ANY,
+        scratch_shapes=[pltpu.VMEM(a.shape, a.dtype) for a in arrays]
+        + [pltpu.VMEM((rows, width), BF), pltpu.SemaphoreType.DMA((len(arrays) + len(plan),))],
+        compiler_params=pltpu.CompilerParams(vmem_limit_bytes=VMEM_MOST),
+        name=name,
+    )(*arrays)
 
 
 def pad_rows(array, count):
@@ -885,77 +1252,55 @@
     seg = lax.dynamic_slice_in_dim(jnp.concatenate([seg, seg], axis=0), n - 1 - place, n, axis=0)
     seg = seg.transpose(1, 0, 2).reshape(tokens)
 
-    query_key = dot_nt(rows_one, weight_one[: 2 * nk]).astype(BF)
-    value = dot_nt(rows_one, weight_one[2 * nk : 2 * nk + nv]).astype(BF)
-    gate_pre = dot_nt(rows_one, weight_one[2 * nk + nv : n_one])
-    query = query_key[:, :nk].reshape(tokens, heads, HK)
-    key = query_key[:, nk:].reshape(tokens, heads, HK)
-    value = value.reshape(tokens, heads, HV)
-
-    distance = places[:, None] - places[None, :]
-    allowed = (distance >= 0) & (seg[:, None] == seg[None, :])
     log_gamma = jnp.log1p(-jnp.exp2(-5.0 - (head_start + jnp.arange(heads)).astype(F32)))
-    exponent = jnp.where(
-        allowed[None], distance[None].astype(F32) * log_gamma[:, None, None], 0.0
+    spot = places.astype(F32)
+    powers = spot[None] * log_gamma[:, None]
+    marks = jnp.stack([spot, seg.astype(F32)])
+    col = jnp.concatenate([marks, jnp.exp(powers)], axis=0).T
+    row = jnp.concatenate([marks, jnp.exp(-powers) * HK ** (-0.5)], axis=0)
+
+    query, key, value, gate_pre, normalized, scale_group, scores, gated, cot_front = forward_call(
+        rows_one, weight_one, cotangent, col, row, n, heads
     )
-    mask = jnp.where(allowed[None], jnp.exp(exponent), 0.0) * HK ** (-0.5)
-
-    scores = (jnp.einsum("thk,shk->hts", query, key, preferred_element_type=F32) * mask).astype(BF)
-    retained = jnp.einsum("hts,shv->thv", scores, value, preferred_element_type=F32)
-    normalized, scale_group = layer_norm(retained, group_epsilon)
-    normal_flat = normalized.reshape(tokens, nv)
-    swish = jax.nn.silu(gate_pre)
-    gated = pad_columns((swish * normal_flat).astype(BF), v_wide)
-
-    rows_two, cot_rows, mid_rows, hidden, d_glu, outputs, middle_grad, second_gain = middle_call(
-        gated, weight_two, inputs, cotangent, second_norm_gain[None], n
-    )
-
-    grads_two = jnp.concatenate([dot_tn(d_glu, rows_two), dot_tn(hidden, cot_rows)], axis=0).astype(BF)
+    (
+        rows_two, cot_rows, mid_rows, hidden, d_glu, down, outputs_front, middle, middle_grad,
+        second_gain,
+    ) = middle_call(gated, weight_two, inputs, cotangent, cot_front, second_norm_gain[None], n)
+
+    plan = [(0, None, t * f_wide, f_wide, 1) for t in range(2)] + [(2, None, 0, f_wide, 3)]
+    grads_two = weight_products(plan, (d_glu, rows_two, hidden, cot_rows), "products_two")
     summed_two = lax.psum_scatter(grads_two, "dp", scatter_dimension=1, tiled=True).astype(F32)
     glu_sum = summed_two[: 2 * f_wide].reshape(f_tiles, 2, LANES, shard)
 
-    d_gated = dot_nt(mid_rows, out_weight[:nv])
-    sigmoid_gate = jax.nn.sigmoid(gate_pre)
-    d_gate_pre = (
-        d_gated * normal_flat * (sigmoid_gate + gate_pre * sigmoid_gate * (1.0 - sigmoid_gate))
-    ).astype(BF)
-    d_normalized = (d_gated * swish).reshape(tokens, heads, HV)
-    d_retained = norm_back(d_normalized, normalized, scale_group).astype(BF)
-    grads_out = jnp.concatenate(
-        [dot_tn(gated[:, :nv], mid_rows).astype(BF), dot_tn(d_gate_pre, rows_one).astype(BF)], axis=0
+    d_qk, d_value, d_gate, outputs_back = backward_call(
+        mid_rows, weight_two, gate_pre, normalized, scale_group, scores, query, key, value,
+        down, middle, col, row, n,
     )
-    summed_out = lax.psum_scatter(grads_out, "dp", scatter_dimension=1, tiled=True).astype(F32)
-
-    d_value = jnp.einsum("hts,thv->shv", scores, d_retained, preferred_element_type=F32).astype(BF)
-    d_scores = (
-        jnp.einsum("thv,shv->hts", d_retained, value, preferred_element_type=F32) * mask
-    ).astype(BF)
-    d_query = jnp.einsum("hts,shk->thk", d_scores, key, preferred_element_type=F32).astype(BF)
-    d_key = jnp.einsum("hts,thk->shk", d_scores, query, preferred_element_type=F32).astype(BF)
-    d_qkv = jnp.concatenate(
-        [d_query.reshape(tokens, nk), d_key.reshape(tokens, nk), d_value.reshape(tokens, nv)], axis=1
+    plan = [(0, h, 0, HV, 1) for h in range(heads)] + [(2, h, 0, HV, 3) for h in range(heads)]
+    plan += [(4, None, t * nk, nk, 3) for t in range(2)]
+    plan += [(5, h, 0, HV, 3) for h in range(heads)]
+    grads_one = weight_products(
+        plan, (gated, mid_rows, d_gate, rows_one, d_qk, d_value), "products_one"
     )
-    grads_one = dot_tn(d_qkv, rows_one).astype(BF)
     summed_one = lax.psum_scatter(grads_one, "dp", scatter_dimension=1, tiled=True).astype(F32)
 
-    d_one = pad_columns(jnp.concatenate([d_qkv, d_gate_pre], axis=1), one_wide)
-    first_grad = last_call(d_one, weight_one, n)
+    first_grad = last_call(d_qk, d_value, d_gate, weight_one, n)
     first_gain = jnp.sum(first_hat * first_grad, axis=0)
     input_gradient = middle_grad + norm_back(first_grad * first_norm_gain, first_hat, first_scale)
 
     gains = sum_gains(
         jnp.stack([first_gain, jnp.sum(second_gain, axis=0)]), n, lax.axis_size("dp")
     )
+    at = 2 * nv
     return (
-        outputs,
+        jnp.concatenate([outputs_front, outputs_back], axis=0),
         input_gradient,
         gains[0],
-        summed_one[:nk].T,
-        summed_one[nk : 2 * nk].T,
-        summed_one[2 * nk :].T,
-        summed_out[nv:].T,
-        summed_out[:nv],
+        summed_one[at : at + nk].T,
+        summed_one[at + nk : at + 2 * nk].T,
+        summed_one[at + 2 * nk :].T,
+        summed_one[nv : 2 * nv].T,
+        summed_one[:nv],
         gains[1],
         glu_sum[:, 0].reshape(f_wide, shard)[:nf].T,
         glu_sum[:, 1].reshape(f_wide, shard)[:nf].T,

time: 729 us -> 654 us (0.90)
  Pallas kernels: 488 us -> 579 us
  matrix products: 90.6 us -> 0 us
  local copies, waits for them, and re-layouts: 59.4 us -> 16.1 us
  other arithmetic: 42.7 us -> 15.4 us
    pallas_call x0 -> x4, Pallas kernels: none -> 130 us  [the longest x2 45.1 us: weight_products(): pl.pallas_call(functools.partial(products_kernel, plan, len(arrays)), out...]
    dot_general x15 -> x0, matrix products: 90.6 us -> none  [the longest x5 40.3 us: dot_tn(): lax.dot_general(a, b, (((0,), (0,)), ((), ())), preferred_element_type=F32)]
    pallas_call x1, Pallas kernels: 295 us -> 254 us  [middle_call(): pl.pallas_call(functools.partial(middle_kernel, n), out_shape=(shape((tok...]
    reduce_scatter x1, waiting for transfers between devices: 26.7 us -> 0.01 us  [body(): lax.psum_scatter(grads_two, 'dp', scatter_dimension=1, tiled=True)]
    reduce_scatter x1, waiting for transfers between devices: 0.01 us -> 20.9 us  [body(): lax.psum_scatter(grads_one, 'dp', scatter_dimension=1, tiled=True)]
    concatenate x2, other arithmetic: 19.9 us -> 2.95 us  [the longest x1 2.32 us: body(): jnp.concatenate([outputs_front, outputs_back], axis=0)]
    unnamed x104 -> x33, local copies, waits for them, and re-layouts: 14.5 us -> 2.83 us
    concatenate x1 -> x0, local copies, waits for them, and re-layouts: 9.79 us -> none  [body(): d_one = pad_columns(jnp.concatenate([d_qkv, d_gate_pre], axis=1), one_wide)]
  transfers between devices with their start and end apart: 4 -> 3, of which waited for: 1 -> 1; matrix products, arithmetic and copies ran while one was open for 20% -> 3% of each run, Pallas kernels for 27% -> 47%
where the time goes in v5:
time: 654 us; the launch traced here: 646 us
  Pallas kernels  579 us (89%)
  waiting for transfers between devices  21 us (3%)
  local copies, waits for them, and re-layouts  16.1 us (2%)
  other arithmetic  15.4 us (2%)
  between operations  14.6 us (2%)
    pallas_call x1, Pallas kernels, middle_call(): pl.pallas_call(functools.partial(middle_kernel, n), out_shape=(shape((tok...  254 us
    pallas_call x1, Pallas kernels, gather_rows(): pl.pallas_call(functools.partial(gather_kernel, n, m), out_shape=(jax.Sha...  106 us
    pallas_call x1, Pallas kernels, last_call(): pl.pallas_call(functools.partial(last_kernel, n), out_shape=jax.ShapeDtyp...  75.6 us
    pallas_call x2, Pallas kernels, weight_products(): pl.pallas_call(functools.partial(products_kernel, plan, len(arrays)), out...  45.1 us
    pallas_call x1, Pallas kernels, forward_call(): pl.pallas_call(functools.partial(forward_kernel, n), out_shape=outs, in_s...  44.1 us
    pallas_call x1, Pallas kernels, backward_call(): pl.pallas_call(functools.partial(backward_kernel, n), out_shape=outs, in_...  41.2 us
    reduce_scatter x1, waiting for transfers between devices, body(): lax.psum_scatter(grads_one, 'dp', scatter_dimension=1, tiled=True)  20.9 us
    pallas_call x1, Pallas kernels, sum_gains(): pl.pallas_call(functools.partial(gains_kernel, n, m), out_shape=jax.Shape...  13.7 us
  transfers between devices with their start and end apart: 3, of which 1 were waited for; matrix products, arithmetic and copies ran while one was open for 3% of the time, Pallas kernels for 47%

profile of v5, /device:TPU:0, one launch (start us, length us, event | category | flops | bytes accessed | tf_op | source)
XLA Modules:
  0.0 646.3 jit_solution(5630050540932679367)
XLA Ops:
  7.2 1.1 pad.18
  8.4 1.0 pad.19
  9.5 1.3 fusion.21
  11.3 0.5 broadcast.162
  11.8 0.7 reduce.3
  13.2 0.6 pad_maximum_fusion.3
  13.8 1.0 copy.28.col
  15.0 0.4 fusion.19
  15.5 1.2 fusion.24.pack
  16.7 1.4 fusion.13.own
  18.1 105.7 %gather_rows.1 = (bf16[1024,2048]{1,0:T(8,128)(2,1)}, bf16[2816,2048]{1,0:T(8,128)(2,1)}) custom-call(bf16[256,2048]{1,0:T(8,128)(2,1)} %fusion.13.own, bf16[2816,256]{1,0:T(8,128)(2,1)} %fusion.24.pack), custom_call_target="tpu_custom_call" | custom-call | tf_op jit(solution)/shard_map/gather_rows/pallas_call | solution.py:339
  123.8 44.1 %forward.1 = (bf16[2,1024,256]{2,1,0:T(8,128)(2,1)}, bf16[2,1024,256]{2,1,0:T(8,128)(2,1)}, bf16[2,1024,432]{2,1,0:T(8,128)(2,1)}, f32[2,1024,432]{2,1,0:T(8,128...) custom-call(bf16[1024,2048]{1,0:T(8,128)(2,1)} %get-tuple-element.37, ...), custom_call_target="tpu_custom_call" | custom-call | tf_op jit(solution)/shard_map/forward/pallas_call | solution.py:981
  167.9 253.7 %middle.1 = (bf16[1024,2048]{1,0:T(8,128)(2,1)}, bf16[1024,2048]{1,0:T(8,128)(2,1)}, bf16[1024,2048]{1,0:T(8,128)(2,1)}, bf16[1024,896]{1,0:T(8,128)(2,1)}, bf16...) custom-call(bf16[2,1024,432]{2,1,0:T(8,128)(2,1)} %get-tuple-element, ...), custom_call_target="tpu_custom_call" | custom-call | tf_op jit(solution)/shard_map/middle/pallas_call | solution.py:659
  421.6 19.0 %products_two.1 = bf16[2688,2048]{1,0:T(8,128)(2,1)} custom-call(bf16[1024,1792]{1,0:T(8,128)(2,1)} %get-tuple-element.58.refs_0_, bf16[1024,2048]{1,0:T(8,128)(2,1)} %get-tuple-element.59.refs_1_, bf16[1024,896]{1,0:T(8,128)(2,1)} %get-tuple-element.60.refs_2_, bf16[1024,2048]{1,0:T(8,128)(2,1)} %get-tuple-element.61.refs_3_), custom_call_target="tpu_custom_call" | custom-call | tf_op jit(solution)/shard_map/products_two/pallas_call | solution.py:1177
  440.7 41.2 %backward.1 = (bf16[1024,1024]{1,0:T(8,128)(2,1)}, bf16[2,1024,432]{2,1,0:T(8,128)(2,1)}, bf16[2,1024,432]{2,1,0:T(8,128)(2,1)}, bf16[128,2048]{1,0:T(8,128)(2,1)}) custom-call(bf16[1024,2048]{1,0:T(8,128)(2,1)} %get-tuple-element.42.mid.refs_1_, bf16[3584,2048]{1,0:T(8,128)(2,1)} %all-gather.2.cloned.1.call-done.weights, ...), custom_call_target="tpu_custom_call" | custom-call | tf_op jit(solution)/shard_map/backward/pallas_call | solution.py:1119
  482.0 26.1 %products_one.1 = bf16[3616,2048]{1,0:T(8,128)(2,1)} custom-call(bf16[2,1024,432]{2,1,0:T(8,128)(2,1)} %get-tuple-element.39.gated.refs_0_, bf16[1024,2048]{1,0:T(8,128)(2,1)} %get-tuple-element.42.mid.refs_1_, bf16[2,1024,432]{2,1,0:T(8,128)(2,1)} %get-tuple-element.56.d_gate.refs_2_, bf16[1024,2048]{1,0:T(8,128)(2,1)} %get-tuple-element.37.rows.refs_3_, ...), custom_call_target="tpu_custom_call" | custom-call | tf_op jit(solution)/shard_map/products_one/pallas_call | solution.py:1177
  508.1 75.6 %last.1 = f32[256,2048]{1,0:T(8,128)} custom-call(bf16[1024,1024]{1,0:T(8,128)(2,1)} %get-tuple-element.54.d_qk.refs_4_, bf16[2,1024,432]{2,1,0:T(8,128)(2,1)} %get-tuple-element.55.d_value.refs_5_, bf16[2,1024,432]{2,1,0:T(8,128)(2,1)} %get-tuple-element.56.d_gate.refs_2_, bf16[2816,2048]{1,0:T(8,128)(2,1)} %get-tuple-element.38.weight), custom_call_target="tpu_custom_call" | custom-call | tf_op jit(solution)/shard_map/last/pallas_call | solution.py:840
  583.7 2.9 fusion.18
  586.6 0.6 reshape.165.mine
  587.3 13.7 %sum_gains.1 = f32[32,128]{1,0:T(8,128)} custom-call(f32[32,128]{1,0:T(8,128)} %reshape.165.mine), custom_call_target="tpu_custom_call" | custom-call | tf_op jit(solution)/shard_map/sum_gains/pallas_call | solution.py:744
  601.1 1.5 slice_bitcast_fusion.6
  602.5 2.3 pad_maximum_fusion
  604.8 2.1 fusion.17
  606.9 2.1 slice.64
  609.3 1.0 slice_bitcast_fusion
  610.3 1.0 slice_bitcast_fusion.1
  611.3 20.9 %reduce-scatter.3.cloned.1.call-done = bf16[3616,256]{1,0:T(8,128)(2,1)} async-done(((bf16[3616,2048]{1,0:T(8,128)(2,1)}), bf16[3616,256]{1,0:T(8,128)(2,1)}) %reduce-scatter.3.cloned.1.call-update) | async-done | bytes 1851408 | tf_op jit(solution)/shard_map/reduce_scatter | solution.py:1285
  632.2 1.8 convert_element_type.68
  634.1 1.3 slice_bitcast_fusion.2
  635.4 1.0 copy.33
  636.4 1.0 copy.32
  637.4 2.0 slice.58
  (61 shorter events, 1.9 us)
Async XLA Ops:
  7.2 2.3 copy-start.6
  7.2 2.3 copy-start.5
  7.2 160.7 %all-gather.2.cloned.1.call-start = ((), (), s32[]{:S(2)}) async-start(), calls=%async_computation.2 | async-start | bytes 16515072 | tf_op jit(solution)/shard_map/all_gather | solution.py:1236
  9.5 2.3 copy-start.13
  9.5 3.2 copy-start.9
  10.9 2.0 copy-start.10
  10.9 3.9 copy-start
  10.9 4.6 copy-start.7
  10.9 4.5 copy-start.8
  11.0 596.0 %reduce-scatter.5.cloned.1.call-start = ((), (), s32[]{:S(2)}) async-start(), calls=%async_computation.4 | async-start | bytes 12386304 | tf_op jit(solution)/shard_map/reduce_scatter | solution.py:1272
  15.0 1.7 copy-start.11
  440.7 191.5 %reduce-scatter.3.cloned.1.call-start = ((), (), s32[]{:S(2)}) async-start(), calls=%async_computation.3 | async-start | bytes 16662528 | tf_op jit(solution)/shard_map/reduce_scatter | solution.py:1285
  508.1 75.6 %copy-start.12 = (f32[8,2048]{1,0:T(8,128)S(1)}, f32[8,2048]{1,0:T(8,128)}, u32[]{:S(2)}) copy-start(f32[8,2048]{1,0:T(8,128)} %get-tuple-element.57) | copy-start | bytes 196612
  583.7 21.1 %copy-start.1 = (bf16[256,2048]{1,0:T(8,128)(2,1)S(1)}, bf16[256,2048]{1,0:T(8,128)(2,1)}, u32[]{:S(2)}) copy-start(bf16[256,2048]{1,0:T(8,128)(2,1)} %own.1) | copy-start | bytes 3145732
  583.7 21.1 %copy-start.2 = (f32[256,2048]{1,0:T(8,128)S(1)}, f32[256,2048]{1,0:T(8,128)}, u32[]{:S(2)}) copy-start(f32[256,2048]{1,0:T(8,128)} %last.1) | copy-start | bytes 6291460
  601.0 3.8 copy-start.4
  606.9 2.1 copy-start.3
Sparse Core Ops, SparseCore 0:
  11.0 124.5 all-gather.1
  440.8 83.5 reduce-scatter.4
  527.9 104.2 reduce-scatter.2

commit v6 on v5

--- a/solution.py
+++ b/solution.py
@@ -13,6 +13,7 @@
 LEN = 1024
 CHUNKS = 4
 FRONT = CHUNKS // 2
+DOWNS = CHUNKS // 4
 LANES = 128
 VMEM_MOST = 66_000_000
 
@@ -273,28 +274,34 @@
 PARTS = 2
 
 
-def gather_kernel(n, m, own, pack, out, weight, send_sem, recv_sem, copy_sem, wide_send, wide_recv):
-    line = Line(n, send_sem, recv_sem)
-    piece = own.shape[0] // CHUNKS
-    per = n * piece
-    shard = pack.shape[1]
-    d = lax.axis_index("dp")
+def weight_gather(m, pack, weight, send_sem, recv_sem):
     bits = bits_of(m)
     outer = bits[1:]
     height = pack.shape[0] // (2 * PARTS)
     doubling = []
     for i in range(2 * PARTS):
         order = (outer if i % 2 == 0 else outer[::-1]) + bits[:1]
-        doubling.append(
-            Doubling(
-                m, pack, weight, pl.ds(i * height, height), order, i * (m - 1), wide_send, wide_recv
-            )
-        )
+        rows = pl.ds(i * height, height)
+        doubling.append(Doubling(m, pack, weight, rows, order, i * (m - 1), send_sem, recv_sem))
     first = doubling[0]
-    line.enter(["dp", [first.flip(d, bit) for bit in bits]])
+    return doubling, [first.flip(first.d, bit) for bit in bits]
+
+
+def own_columns(pack, weight):
+    shard = pack.shape[1]
+    at = pl.multiple_of(lax.axis_index("dp") * shard, shard)
+    return weight.at[:, pl.ds(at, shard)]
+
+
+def gather_kernel(n, m, own, pack, out, weight, send_sem, recv_sem, copy_sem, wide_send, wide_recv):
+    line = Line(n, send_sem, recv_sem)
+    piece = own.shape[0] // CHUNKS
+    per = n * piece
+    bits = bits_of(m)
+    doubling, peers = weight_gather(m, pack, weight, wide_send, wide_recv)
+    line.enter(["dp", peers])
     local, gathers = [], []
-    columns = pl.ds(pl.multiple_of(d * shard, shard), shard)
-    keep = pltpu.make_async_copy(pack, weight.at[:, columns], copy_sem.at[CHUNKS])
+    keep = pltpu.make_async_copy(pack, own_columns(pack, weight), copy_sem.at[CHUNKS])
     for h in range(CHUNKS):
         mine = own.at[pl.ds(h * piece, piece)]
         local.append(
@@ -376,11 +383,11 @@
 }
 TUNED = {
     (4, 4): [
-        2, 4, 8, 8, 5, 2, 8, 6, 9, 10, 2, 9, 12, 16, 7, 9, 11, 16, 13, 10,
-        11, 16, 16, 17, 2, 20, 11, 10, 20, 17, 15, 19, 14, 24, 17, 18, 40, 28, 17, 21,
-        18, 28, 18, 3, 21, 28, 25, 19, 18, 29, 22, 29, 32, 3, 36, 44, 19, 22, 26, 36,
-        30, 41, 30, 3, 42, 44, 19, 3, 29, 30, 23, 44, 23, 36, 34, 33, 38, 37, 27, 31,
-        38, 31, 37, 38, 31, 45, 45, 35, 39, 36, 45, 39, 49, 48, 37, 43, 37, 39, 39, 38,
+        3, 5, 4, 8, 8, 2, 8, 2, 7, 9, 12, 16, 9, 6, 16, 9, 10, 16, 3, 13,
+        11, 17, 16, 20, 10, 11, 2, 17, 20, 10, 17, 40, 11, 24, 14, 18, 2, 28, 17, 3,
+        21, 18, 28, 15, 19, 21, 25, 29, 44, 18, 18, 28, 19, 22, 29, 44, 22, 19, 32, 3,
+        36, 26, 30, 19, 29, 23, 36, 23, 36, 30, 33, 37, 30, 27, 31, 44, 34, 37, 38, 43,
+        37, 31, 41, 38, 48, 36, 42, 31, 37, 38, 35, 39, 38, 39, 39, 39,
     ],
 }
 
@@ -399,7 +406,7 @@
         for k, (first, later, each) in DUE.items()
         for h in range(CHUNKS)
         for s in range(count[k])
-        if not (k == COT and h < FRONT or k in (DOWN_SUM, END_DOWN) and h >= FRONT)
+        if not (k == COT and h < FRONT or k in (DOWN_SUM, END_DOWN) and h >= DOWNS)
     )
     taken, order = {}, []
     while todo:
@@ -418,7 +425,7 @@
 
 
 def middle_kernel(
-    n, gated, weights, own, cot, cot_front, gain,
+    n, gated, weights, out_weight, own, cot, cot_front, gain,
     rows_out, cot_out, mid_out, hidden_out, glu_out, down_out, outputs, middle_out, d_middle,
     gain_out,
     gated_v, wo_v, wg_v, wd_v, own_v, cot_v, rows_v, hidden_v, glu_v, part, part_two,
@@ -447,14 +454,16 @@
     front = pl.ds(0, FRONT * per)
     load_cot.append(local(cot_front, cot_v.at[front]))
     load_gated = local(gated, gated_v)
-    load_wo = local(weights.at[pl.ds(3 * wide, wo_v.shape[0])], wo_v)
+    load_wo = local(
+        out_weight.at[pl.ds(out_weight.shape[0] - wo_v.shape[0], wo_v.shape[0])], wo_v
+    )
     load_own = local(own, own_v)
     load_wg = local(weights.at[pl.ds(0, 2 * wide)], wg_v)
     load_wd = local(weights.at[pl.ds(2 * wide, wide)], wd_v)
     line.enter()
     for h in range(CHUNKS):
         no_neighbour_zero(n, place, left_a.at[h, n - 2], right_a.at[h, n - 2])
-    for h in range(FRONT):
+    for h in range(DOWNS):
         no_neighbour_zero(n, place, left_b.at[h, n - 2], right_b.at[h, n - 2])
     gain_out[...] = jnp.zeros_like(gain_out)
 
@@ -477,7 +486,7 @@
 
     gather_mid = [Gather(line, functools.partial(mid_slot, h)) for h in range(CHUNKS)]
     scatter_one = [scatter(part, left_a, right_a, h) for h in range(CHUNKS)]
-    scatter_two = [scatter(part_two, left_b, right_b, h) for h in range(FRONT)]
+    scatter_two = [scatter(part_two, left_b, right_b, h) for h in range(DOWNS)]
     scatter_grad = [scatter(part, left_a, right_a, h) for h in range(CHUNKS)]
 
     def chunk(ref, h):
@@ -632,8 +641,8 @@
         local(chunk(cot_v, c), chunk(cot_out, c))
         local(chunk(hidden_v, c), chunk(hidden_out, c))
         local(chunk(glu_v, c), chunk(glu_out, c))
-    local(part_two.at[pl.ds(FRONT * per, down_out.shape[0])], down_out)
-    local(middle.at[pl.ds(FRONT * piece, middle_out.shape[0])], middle_out)
+    local(part_two.at[pl.ds(DOWNS * per, down_out.shape[0])], down_out)
+    local(middle.at[pl.ds(DOWNS * piece, middle_out.shape[0])], middle_out)
     for item in list(gather_cot.values()) + gather_two + gather_mid:
         assert item.step_no == n
     for item in scatter_one + scatter_two + scatter_grad:
@@ -646,13 +655,13 @@
     line.leave()
 
 
-def middle_call(gated, weights, own, cot, cot_front, gain, n):
+def middle_call(gated, weights, out_weight, own, cot, cot_front, gain, n):
     rows, width = own.shape
     heads, tokens, size = gated.shape
     nv = heads * size
-    wide = (weights.shape[0] - -(-nv // LANES) * LANES) // 3
+    wide = weights.shape[0] // 3
     piece = rows // CHUNKS
-    back = CHUNKS - FRONT
+    back = CHUNKS - DOWNS
     sems = CHUNKS * 5 * 2 * (n - 1)
     hop = (CHUNKS, n - 1, piece, width)
     shape = jax.ShapeDtypeStruct
@@ -665,12 +674,12 @@
             shape((tokens, wide), BF),
             shape((tokens, 2 * wide), BF),
             shape((back * n * piece, width), BF),
-            shape((FRONT * piece, width), BF),
+            shape((DOWNS * piece, width), BF),
             shape((back * piece, width), F32),
             shape((rows, width), F32),
             shape((8, width), F32),
         ),
-        in_specs=[ANY] * 5 + [VM],
+        in_specs=[ANY] * 6 + [VM],
         out_specs=(ANY,) * 6 + (VM, ANY, VM, VM),
         scratch_shapes=[
             pltpu.VMEM((heads, tokens, size), BF),
@@ -686,8 +695,8 @@
             pltpu.VMEM((tokens, width), BF),
             pltpu.VMEM(hop, BF),
             pltpu.VMEM(hop, BF),
-            pltpu.VMEM((FRONT,) + hop[1:], BF),
-            pltpu.VMEM((FRONT,) + hop[1:], BF),
+            pltpu.VMEM((DOWNS,) + hop[1:], BF),
+            pltpu.VMEM((DOWNS,) + hop[1:], BF),
             pltpu.VMEM((rows, width), F32),
             pltpu.VMEM((CHUNKS, piece, width), BF),
             pltpu.SemaphoreType.DMA((8 + 6 * CHUNKS - FRONT,)),
@@ -698,20 +707,104 @@
             collective_id=1, has_side_effects=True, vmem_limit_bytes=VMEM_MOST
         ),
         name="middle",
-    )(gated, weights, own, cot, cot_front, gain)
-
-
-def gains_kernel(n, m, mine, total, first, second, send_sem, recv_sem):
-    barrier = pltpu.get_barrier_semaphore()
-    groups = (("dp", m, first), ("mp", n, second))
-    for axis, size, _ in groups:
-        me = lax.axis_index(axis)
-        for k in range(1, size):
-            peer = lax.rem(me + k, size)
-            pl.semaphore_signal(barrier, inc=1, device_id={axis: peer}, device_id_type=MESH)
-    pl.semaphore_wait(barrier, n + m - 2)
-    source = mine
-    for base, (axis, size, held) in zip((0, m), groups):
+    )(gated, weights, out_weight, own, cot, cot_front, gain)
+
+
+class Halving:
+    def __init__(self, grads, rows, bits, base, kept, held, out, send_sem, recv_sem, load_sem):
+        self.d = lax.axis_index("dp")
+        self.grads, self.rows, self.bits, self.base = grads, rows, bits, base
+        self.kept, self.held, self.out = kept, held, out
+        self.send_sem, self.recv_sem, self.load_sem = send_sem, recv_sem, load_sem
+        self.shard = out.shape[1]
+        self.masks = [0]
+        for bit in bits[:0:-1]:
+            self.masks += [k + bit for k in self.masks]
+        self.done, self.sent, self.loads = 0, [], []
+
+    def flip(self, d, mask):
+        for bit in self.bits:
+            if mask & bit:
+                d = d + bit * (1 - 2 * (lax.div(d, bit) % 2))
+        return d
+
+    def block(self, d):
+        return self.grads.at[self.rows, pl.ds(pl.multiple_of(d * self.shard, self.shard), self.shard)]
+
+    def count(self, level):
+        return 1 << (len(self.bits) - 1 - level)
+
+    def copies(self, level):
+        bit = self.bits[level]
+        partner = self.flip(self.d, bit)
+        out = []
+        for i in range(self.count(level)):
+            if level == 0:
+                src = self.block(self.flip(partner, self.masks[i]))
+            else:
+                src = self.kept.at[self.count(level) + i, self.rows]
+            index = self.base + len(out) + sum(self.count(k) for k in range(level))
+            out.append(
+                pltpu.make_async_remote_copy(
+                    src_ref=src,
+                    dst_ref=self.held[level].at[i, self.rows],
+                    send_sem=self.send_sem.at[index],
+                    recv_sem=self.recv_sem.at[index],
+                    device_id={"dp": partner},
+                    device_id_type=MESH,
+                )
+            )
+        return out
+
+    def load(self):
+        for i, mask in enumerate(self.masks):
+            c = pltpu.make_async_copy(
+                self.block(self.flip(self.d, mask)), self.kept.at[i, self.rows], self.load_sem.at[i]
+            )
+            c.start()
+            self.loads.append(c)
+
+    def add(self, level):
+        last = level == len(self.bits) - 1
+        start, size = self.rows.start, self.rows.size
+        for i in range(self.count(level)):
+
+            def step(at):
+                total = self.kept[i, at(start), :].astype(F32) + self.held[level][
+                    i, at(start), :
+                ].astype(F32)
+                if last:
+                    self.out[at(start), :] = total
+                else:
+                    self.kept[i, at(start), :] = total.astype(BF)
+
+            blocks(size, step)
+
+    def step(self):
+        level = self.done
+        if level > 0:
+            for c in self.loads:
+                c.wait()
+            self.loads = []
+            for c in self.sent[-1]:
+                c.wait_recv()
+            self.add(level - 1)
+        if level < len(self.bits):
+            out = self.copies(level)
+            for c in out:
+                c.start()
+            self.sent.append(out)
+        self.done += 1
+
+    def leave(self):
+        for group in self.sent:
+            for c in group:
+                c.wait_send()
+
+
+def exchange(groups, mine, total, send_sem, recv_sem):
+    source, base = mine, 0
+    for axis, size, held in groups:
         me = lax.axis_index(axis)
         held[me] = source[...]
 
@@ -736,31 +829,19 @@
         for c in sent:
             c.wait_send()
         total[...] = value
-        source = total
-
-
-def sum_gains(values, n, m):
-    flat = values.reshape(-1, LANES)
-    return pl.pallas_call(
-        functools.partial(gains_kernel, n, m),
-        out_shape=jax.ShapeDtypeStruct(flat.shape, F32),
-        in_specs=[VM],
-        out_specs=VM,
-        scratch_shapes=[
-            pltpu.VMEM((m,) + flat.shape, F32),
-            pltpu.VMEM((n,) + flat.shape, F32),
-            pltpu.SemaphoreType.DMA((n + m,)),
-            pltpu.SemaphoreType.DMA((n + m,)),
-        ],
-        compiler_params=pltpu.CompilerParams(collective_id=3, has_side_effects=True),
-        name="sum_gains",
-    )(flat).reshape(values.shape)
+        source, base = total, base + size
 
 
 def last_kernel(
-    n, d_qk, d_value, d_gate, weight, out,
-    qk_v, value_v, gate_v, weight_v, part, lefts, rights, copy_sem, send_sem, recv_sem
+    n, m, d_qk, d_value, d_gate, weight, grads, inputs, gain, d_middle, second_gain,
+    out, gains, summed,
+    qk_v, value_v, gate_v, weight_v, inputs_v, middle_v, part, lefts, rights, kept, *rest
 ):
+    bits = bits_of(m)
+    held, (gain_sum, mine, first, second) = rest[: len(bits)], rest[len(bits) : len(bits) + 4]
+    copy_sem, send_sem, recv_sem, wide_send, wide_recv, load_sem, gain_send, gain_recv = rest[
+        len(bits) + 4 :
+    ]
     line = Line(n, send_sem, recv_sem)
     count, width = out.shape
     piece = count // CHUNKS
@@ -770,14 +851,39 @@
     load = [
         pltpu.make_async_copy(src, dst, copy_sem.at[i])
         for i, (src, dst) in enumerate(
-            [(weight, weight_v), (d_qk, qk_v), (d_value, value_v), (d_gate, gate_v)]
+            [
+                (weight.at[pl.ds(0, weight_v.shape[0])], weight_v), (d_qk, qk_v),
+                (d_value, value_v), (d_gate, gate_v), (inputs, inputs_v), (d_middle, middle_v),
+            ]
         )
     ]
     for item in load:
         item.start()
-    line.enter()
+    barrier = pltpu.get_barrier_semaphore()
+    for axis, extent in (("dp", m), ("mp", n)):
+        me = lax.axis_index(axis)
+        for k in range(1, extent):
+            peer = lax.rem(me + k, extent)
+            pl.semaphore_signal(barrier, inc=1, device_id={axis: peer}, device_id_type=MESH)
+    pl.semaphore_wait(barrier, n + m - 2)
+
+    height = grads.shape[0] // (2 * PARTS)
+    halving = []
+    for i in range(2 * PARTS):
+        order = bits[:1] + (bits[1:] if i % 2 == 0 else bits[:0:-1])
+        halving.append(
+            Halving(
+                grads, pl.ds(i * height, height), order, i * (m - 1), kept, held, summed,
+                wide_send, wide_recv, load_sem.at[i],
+            )
+        )
+    for item in halving:
+        item.step()
+    for item in halving:
+        item.load()
     for h in range(CHUNKS):
         no_neighbour_zero(n, line.place, lefts.at[h, n - 2], rights.at[h, n - 2])
+    gain_sum[...] = jnp.zeros_like(gain_sum)
     scatters = [
         Scatter(
             line,
@@ -809,11 +915,15 @@
         scatters[h].finish()
 
         def step(at):
-            out[at(h * piece), :] = (
+            own = at(h * piece)
+            grad = (
                 part[at(h * per), :].astype(F32)
                 + lefts[h, n - 2, at(), :].astype(F32)
                 + rights[h, n - 2, at(), :].astype(F32)
             )
+            hat, scale = layer_norm(inputs_v[own, :].astype(F32), epsilon)
+            gain_sum[...] += jnp.sum((hat * grad).reshape(BLOCK // 8, 8, width), axis=0)
+            out[own, :] = middle_v[own, :] + norm_back(grad * gain[...], hat, scale)
 
         blocks(piece, step)
 
@@ -822,43 +932,80 @@
     for h in range(CHUNKS):
         product(h)
         scatters[h].step()
-    for _ in range(n - 2):
+    for s in range(n - 2):
         for h in range(CHUNKS):
+            if s < len(bits) and h < len(halving):
+                halving[h].step()
             scatters[h].step()
+    while halving[0].done < len(bits):
+        for item in halving:
+            item.step()
     for h in range(CHUNKS):
         finish(h)
+    groups = [("dp", m, first), ("mp", n, second)]
+    for i, source in enumerate((gain_sum, second_gain)):
+        flat = jnp.sum(source[...], axis=0, keepdims=True)
+        for j in range(width // LANES):
+            mine[pl.ds(i * (width // LANES) + j, 1), :] = flat[:, j * LANES : (j + 1) * LANES]
+    exchange(groups, mine, gains, gain_send, gain_recv)
+    for item in halving:
+        while item.done <= len(bits):
+            item.step()
+        item.leave()
     for h in range(CHUNKS):
         scatters[h].drain()
 
 
-def last_call(d_qk, d_value, d_gate, weight, n):
+def last_call(d_qk, d_value, d_gate, weight, grads, inputs, gain, d_middle, second_gain, n, m):
     tokens = d_qk.shape[0]
-    width = weight.shape[1]
-    rows = tokens // n
+    rows, width = inputs.shape
+    heads = d_value.shape[0]
+    shard = width // m
     sems = CHUNKS * 2 * (n - 1)
+    wide = 2 * PARTS * (m - 1)
     hop = (CHUNKS, n - 1, rows // CHUNKS, width)
+    flat = (2 * width // LANES, LANES)
+    levels = [m >> (1 + k) for k in range(len(bits_of(m)))]
+    shape = jax.ShapeDtypeStruct
     return pl.pallas_call(
-        functools.partial(last_kernel, n),
-        out_shape=jax.ShapeDtypeStruct((rows, width), F32),
-        in_specs=[ANY] * 4,
-        out_specs=VM,
+        functools.partial(last_kernel, n, m),
+        out_shape=(
+            shape((rows, width), F32), shape(flat, F32), shape((grads.shape[0], shard), F32),
+        ),
+        in_specs=[ANY] * 6 + [VM, ANY, VM],
+        out_specs=(VM,) * 3,
         scratch_shapes=[
             pltpu.VMEM(d_qk.shape, BF),
             pltpu.VMEM(d_value.shape, BF),
             pltpu.VMEM(d_gate.shape, BF),
-            pltpu.VMEM(weight.shape, BF),
+            pltpu.VMEM((2 * heads * (HK + HV), width), BF),
+            pltpu.VMEM((rows, width), BF),
+            pltpu.VMEM((rows, width), F32),
             pltpu.VMEM((tokens, width), BF),
             pltpu.VMEM(hop, BF),
             pltpu.VMEM(hop, BF),
-            pltpu.SemaphoreType.DMA((4,)),
+            pltpu.VMEM((m // 2, grads.shape[0], shard), BF),
+        ]
+        + [pltpu.VMEM((count, grads.shape[0], shard), BF) for count in levels]
+        + [
+            pltpu.VMEM((8, width), F32),
+            pltpu.VMEM(flat, F32),
+            pltpu.VMEM((m,) + flat, F32),
+            pltpu.VMEM((n,) + flat, F32),
+            pltpu.SemaphoreType.DMA((6,)),
             pltpu.SemaphoreType.DMA((sems,)),
             pltpu.SemaphoreType.DMA((sems,)),
+            pltpu.SemaphoreType.DMA((wide,)),
+            pltpu.SemaphoreType.DMA((wide,)),
+            pltpu.SemaphoreType.DMA((2 * PARTS, m // 2)),
+            pltpu.SemaphoreType.DMA((n + m,)),
+            pltpu.SemaphoreType.DMA((n + m,)),
         ],
         compiler_params=pltpu.CompilerParams(
             collective_id=2, has_side_effects=True, vmem_limit_bytes=VMEM_MOST
         ),
         name="last",
-    )(d_qk, d_value, d_gate, weight)
+    )(d_qk, d_value, d_gate, weight, grads, inputs, gain, d_middle, second_gain)
 
 
 TILE = 256
@@ -883,10 +1030,10 @@
 
 
 def forward_kernel(
-    n, rows, weight, cot, col, row,
-    query_o, key_o, value_o, gate_o, norm_o, scale_o, scores_o, gated_o, cot_o,
+    n, m, rows, weight, cot, col, row, pack,
+    query_o, key_o, value_o, gate_o, norm_o, scale_o, scores_o, gated_o, cot_o, second_o,
     rows_v, weight_v, query_v, key_v, value_v, gate_v, norm_v, scale_v, scores_v, gated_v, cot_v,
-    copy_sem, send_sem, recv_sem,
+    copy_sem, send_sem, recv_sem, wide_send, wide_recv,
 ):
     line = Line(n, send_sem, recv_sem)
     heads, tokens, deep = query_v.shape
@@ -905,16 +1052,19 @@
         local(cot.at[pl.ds(h * piece, piece)], cot_v.at[pl.ds(h * per, piece)])
         for h in range(FRONT)
     ]
-    load_rows, load_weight = local(rows, rows_v), local(weight, weight_v)
-    line.enter()
+    load_rows = local(rows, rows_v)
+    load_weight = local(weight.at[pl.ds(0, weight_v.shape[0])], weight_v)
+    doubling, peers = weight_gather(m, pack, second_o, wide_send, wide_recv)
+    line.enter(["dp", peers])
     gathers = [
         Gather(line, lambda k, h=h: cot_v.at[pl.ds(h * per + k * piece, piece)])
         for h in range(FRONT)
     ]
     for item in load_cot:
         item.wait()
-    for g in gathers:
+    for g in gathers + doubling:
         g.step()
+    local(pack, own_columns(pack, second_o))
     load_rows.wait()
     load_weight.wait()
 
@@ -950,20 +1100,31 @@
             project(gate_v, h, gates + h * size, size),
             attend(h),
         ]
-    in_order(units, [g.step for _ in range(n - 1) for g in gathers])
-    count = len(copies)
+    steps = [g.step for _ in range(n - 1) for g in gathers]
+    wide_steps = [g.step for _ in range(len(bits_of(m))) for g in doubling]
+    mixed = []
+    for i in range(max(len(steps), len(wide_steps))):
+        mixed += steps[i : i + 1] + wide_steps[i : i + 1]
+    late = mixed[-2 * PARTS :]
+    in_order(units, mixed[: -2 * PARTS])
+    count = len(copies) - 1
     for src, dst in (
         (query_v, query_o), (key_v, key_o), (value_v, value_o), (gate_v, gate_o),
         (norm_v, norm_o), (scale_v, scale_o), (scores_v, scores_o), (gated_v, gated_o),
         (cot_v, cot_o),
     ):
         local(src, dst)
+    for step in late:
+        step()
     for item in copies[count:]:
         item.wait()
+    for item in doubling:
+        assert item.done == len(bits_of(m)) + 1
+        item.leave()
     line.leave()
 
 
-def forward_call(rows, weight, cot, col, row, n, heads):
+def forward_call(rows, weight, cot, col, row, pack, n, m, heads):
     tokens, width = rows.shape
     shape = jax.ShapeDtypeStruct
     outs = (
@@ -976,25 +1137,30 @@
         shape((heads, tokens, tokens), BF),
         shape((heads, tokens, HV), BF),
         shape((tokens * FRONT // CHUNKS, width), BF),
+        shape((pack.shape[0], m * pack.shape[1]), BF),
     )
+    attention_rows = 2 * heads * (HK + HV)
+    wide = 2 * PARTS * (m - 1)
     sems = FRONT * 2 * (n - 1)
     return pl.pallas_call(
-        functools.partial(forward_kernel, n),
+        functools.partial(forward_kernel, n, m),
         out_shape=outs,
-        in_specs=[ANY] * 3 + [VM] * 2,
+        in_specs=[ANY] * 3 + [VM] * 3,
         out_specs=(ANY,) * len(outs),
-        scratch_shapes=[pltpu.VMEM(rows.shape, BF), pltpu.VMEM(weight.shape, BF)]
-        + [pltpu.VMEM(o.shape, o.dtype) for o in outs]
+        scratch_shapes=[pltpu.VMEM(rows.shape, BF), pltpu.VMEM((attention_rows, width), BF)]
+        + [pltpu.VMEM(o.shape, o.dtype) for o in outs[:-1]]
         + [
             pltpu.SemaphoreType.DMA((FRONT + 2 + len(outs),)),
             pltpu.SemaphoreType.DMA((sems,)),
             pltpu.SemaphoreType.DMA((sems,)),
+            pltpu.SemaphoreType.DMA((wide,)),
+            pltpu.SemaphoreType.DMA((wide,)),
         ],
         compiler_params=pltpu.CompilerParams(
             collective_id=4, has_side_effects=True, vmem_limit_bytes=VMEM_MOST
         ),
         name="forward",
-    )(rows, weight, cot, col, row)
+    )(rows, weight, cot, col, row, pack)
 
 
 def backward_kernel(
@@ -1006,7 +1172,7 @@
     line = Line(n, send_sem, recv_sem)
     heads, tokens, deep = query_v.shape
     size = value_v.shape[2]
-    back = CHUNKS - FRONT
+    back = CHUNKS - DOWNS
     per = part.shape[0] // back
     piece = per // n
     copies = []
@@ -1103,7 +1269,7 @@
 def backward_call(mid, weights, gate, norm, scale, scores, query, key, value, down, middle, col, row, n):
     tokens, width = mid.shape
     heads, _, size = value.shape
-    back = CHUNKS - FRONT
+    back = CHUNKS - DOWNS
     nv = heads * size
     shape = jax.ShapeDtypeStruct
     outs = (
@@ -1115,13 +1281,12 @@
     ins = (gate, norm, scale, scores, query, key, value, down, middle)
     hop = (back, n - 1, middle.shape[0] // back, width)
     sems = back * 2 * (n - 1)
-    wo_rows = -(-nv // LANES) * LANES
     return pl.pallas_call(
         functools.partial(backward_kernel, n),
         out_shape=outs,
         in_specs=[ANY] * 11 + [VM] * 2,
         out_specs=(ANY,) * 3 + (VM,),
-        scratch_shapes=[pltpu.VMEM(mid.shape, BF), pltpu.VMEM((wo_rows, width), BF)]
+        scratch_shapes=[pltpu.VMEM(mid.shape, BF), pltpu.VMEM((nv, width), BF)]
         + [pltpu.VMEM(a.shape, a.dtype) for a in ins]
         + [pltpu.VMEM(o.shape, o.dtype) for o in outs[:3]]
         + [
@@ -1167,12 +1332,20 @@
         store.start()
         stores.append(store)
         base += size
+    spare = result.shape[0] - base
+    if spare:
+        target = pl.ds(base, spare)
+        result[target, :] = jnp.zeros((spare, result.shape[1]), BF)
+        store = pltpu.make_async_copy(
+            result.at[target], out.at[target], copy_sem.at[arrays + len(stores)]
+        )
+        store.start()
+        stores.append(store)
     for item in stores:
         item.wait()
 
 
-def weight_products(plan, arrays, name):
-    rows = sum(p[3] for p in plan)
+def weight_products(plan, arrays, name, rows):
     width = arrays[plan[0][4]].shape[1]
     return pl.pallas_call(
         functools.partial(products_kernel, plan, len(arrays)),
@@ -1180,7 +1353,7 @@
         in_specs=[ANY] * len(arrays),
         out_specs=ANY,
         scratch_shapes=[pltpu.VMEM(a.shape, a.dtype) for a in arrays]
-        + [pltpu.VMEM((rows, width), BF), pltpu.SemaphoreType.DMA((len(arrays) + len(plan),))],
+        + [pltpu.VMEM((rows, width), BF), pltpu.SemaphoreType.DMA((len(arrays) + len(plan) + 1,))],
         compiler_params=pltpu.CompilerParams(vmem_limit_bytes=VMEM_MOST),
         name=name,
     )(*arrays)
@@ -1217,13 +1390,15 @@
     shard = w_query.shape[0]
     piece = rows // CHUNKS
     nk, nv, nf = heads * HK, heads * HV, w_down.shape[0]
-    n_one = 2 * nk + 2 * nv
-    one_wide = -(-n_one // (2 * LANES)) * 2 * LANES
-    v_wide, f_wide = -(-nv // LANES) * LANES, -(-nf // LANES) * LANES
+    f_wide = -(-nf // LANES) * LANES
     f_tiles = f_wide // LANES
-
-    pack_one = pad_rows(
-        jnp.concatenate([w_query.T, w_key.T, w_value.T, w_gate.T], axis=0), one_wide
+    grain = 2 * PARTS * BLOCK
+    one_rows = -(-(2 * nk + 3 * nv) // grain) * grain
+    gap = one_rows - 2 * nk - 3 * nv
+    m = lax.axis_size("dp")
+
+    pack_one = jnp.concatenate(
+        [w_query.T, w_key.T, w_value.T, w_gate.T, jnp.zeros((gap, shard), BF), w_out], axis=0
     )
     glu_pack = jnp.stack(
         [
@@ -1232,14 +1407,10 @@
         ],
         axis=1,
     ).reshape(2 * f_wide, shard)
-    pack_two = jnp.concatenate([glu_pack, pad_rows(w_down, f_wide), pad_rows(w_out, v_wide)], axis=0)
-    weight_two = lax.all_gather(pack_two, "dp", axis=1, tiled=True)
-    out_weight = weight_two[3 * f_wide :]
-
-    first_hat, first_scale = layer_norm(inputs.astype(F32), epsilon)
-    rows_one, weight_one = gather_rows(
-        (first_hat * first_norm_gain).astype(BF), pack_one, n, lax.axis_size("dp")
-    )
+    pack_two = jnp.concatenate([glu_pack, pad_rows(w_down, f_wide)], axis=0)
+
+    first_hat, _ = layer_norm(inputs.astype(F32), epsilon)
+    rows_one, weight_one = gather_rows((first_hat * first_norm_gain).astype(BF), pack_one, n, m)
     tokens = rows_one.shape[0]
 
     slot_shard = lax.rem(place - jnp.arange(n) + n, n)
@@ -1259,38 +1430,36 @@
     col = jnp.concatenate([marks, jnp.exp(powers)], axis=0).T
     row = jnp.concatenate([marks, jnp.exp(-powers) * HK ** (-0.5)], axis=0)
 
-    query, key, value, gate_pre, normalized, scale_group, scores, gated, cot_front = forward_call(
-        rows_one, weight_one, cotangent, col, row, n, heads
-    )
+    (
+        query, key, value, gate_pre, normalized, scale_group, scores, gated, cot_front, weight_two,
+    ) = forward_call(rows_one, weight_one, cotangent, col, row, pack_two, n, m, heads)
     (
         rows_two, cot_rows, mid_rows, hidden, d_glu, down, outputs_front, middle, middle_grad,
         second_gain,
-    ) = middle_call(gated, weight_two, inputs, cotangent, cot_front, second_norm_gain[None], n)
+    ) = middle_call(
+        gated, weight_two, weight_one, inputs, cotangent, cot_front, second_norm_gain[None], n
+    )
 
     plan = [(0, None, t * f_wide, f_wide, 1) for t in range(2)] + [(2, None, 0, f_wide, 3)]
-    grads_two = weight_products(plan, (d_glu, rows_two, hidden, cot_rows), "products_two")
+    grads_two = weight_products(plan, (d_glu, rows_two, hidden, cot_rows), "products_two", 3 * f_wide)
     summed_two = lax.psum_scatter(grads_two, "dp", scatter_dimension=1, tiled=True).astype(F32)
     glu_sum = summed_two[: 2 * f_wide].reshape(f_tiles, 2, LANES, shard)
 
     d_qk, d_value, d_gate, outputs_back = backward_call(
-        mid_rows, weight_two, gate_pre, normalized, scale_group, scores, query, key, value,
+        mid_rows, weight_one, gate_pre, normalized, scale_group, scores, query, key, value,
         down, middle, col, row, n,
     )
     plan = [(0, h, 0, HV, 1) for h in range(heads)] + [(2, h, 0, HV, 3) for h in range(heads)]
     plan += [(4, None, t * nk, nk, 3) for t in range(2)]
     plan += [(5, h, 0, HV, 3) for h in range(heads)]
     grads_one = weight_products(
-        plan, (gated, mid_rows, d_gate, rows_one, d_qk, d_value), "products_one"
+        plan, (gated, mid_rows, d_gate, rows_one, d_qk, d_value), "products_one", one_rows
     )
-    summed_one = lax.psum_scatter(grads_one, "dp", scatter_dimension=1, tiled=True).astype(F32)
-
-    first_grad = last_call(d_qk, d_value, d_gate, weight_one, n)
-    first_gain = jnp.sum(first_hat * first_grad, axis=0)
-    input_gradient = middle_grad + norm_back(first_grad * first_norm_gain, first_hat, first_scale)
-
-    gains = sum_gains(
-        jnp.stack([first_gain, jnp.sum(second_gain, axis=0)]), n, lax.axis_size("dp")
+    input_gradient, gains, summed_one = last_call(
+        d_qk, d_value, d_gate, weight_one, grads_one, inputs, first_norm_gain[None], middle_grad,
+        second_gain, n, m,
     )
+    gains = gains.reshape(2, width)
     at = 2 * nv
     return (
         jnp.concatenate([outputs_front, outputs_back], axis=0),
@@ -1298,7 +1467,7 @@
         gains[0],
         summed_one[at : at + nk].T,
         summed_one[at + nk : at + 2 * nk].T,
-        summed_one[at + 2 * nk :].T,
+        summed_one[at + 2 * nk : at + 2 * nk + nv].T,
         summed_one[nv : 2 * nv].T,
         summed_one[:nv],
         gains[1],

time: 654 us -> 632 us (0.966)
  waiting for transfers between devices: 21 us -> 0.02 us
  other arithmetic: 15.4 us -> 8.35 us
    pallas_call x1, Pallas kernels: 106 us -> 81 us  [gather_rows(): pl.pallas_call(functools.partial(gather_kernel, n, m), out_shape=(jax.Sha...]
    pallas_call x3 -> x2, Pallas kernels: 133 us -> 157 us  [the longest x1 99.9 us: last_call(): pl.pallas_call(functools.partial(last_kernel, n, m), out_shape=(shape((ro...]
    reduce_scatter x1 -> x0, waiting for transfers between devices: 20.9 us -> none  [body(): lax.psum_scatter(grads_one, 'dp', scatter_dimension=1, tiled=True)]
    pallas_call x1, Pallas kernels: 41.2 us -> 48.6 us  [backward_call(): pl.pallas_call(functools.partial(backward_kernel, n), out_shape=outs, in_...]
  transfers between devices with their start and end apart: 3 -> 1, of which waited for: 1 -> 0; matrix products, arithmetic and copies ran while one was open for 3% -> 1% of each run, Pallas kernels for 47% -> 28%
where the time goes in v6:
time: 632 us; the launch traced here: 622 us
  Pallas kernels  580 us (92%)
  local copies, waits for them, and re-layouts  18.8 us (3%)
  between operations  14.8 us (2%)
  other arithmetic  8.35 us (1%)
    pallas_call x1, Pallas kernels, middle_call(): pl.pallas_call(functools.partial(middle_kernel, n), out_shape=(shape((tok...  249 us
    pallas_call x1, Pallas kernels, last_call(): pl.pallas_call(functools.partial(last_kernel, n, m), out_shape=(shape((ro...  99.9 us
    pallas_call x1, Pallas kernels, gather_rows(): pl.pallas_call(functools.partial(gather_kernel, n, m), out_shape=(jax.Sha...  81 us
    pallas_call x1, Pallas kernels, forward_call(): pl.pallas_call(functools.partial(forward_kernel, n, m), out_shape=outs, i...  57.2 us
    pallas_call x1, Pallas kernels, backward_call(): pl.pallas_call(functools.partial(backward_kernel, n), out_shape=outs, in_...  48.6 us
    pallas_call x2, Pallas kernels, weight_products(): pl.pallas_call(functools.partial(products_kernel, plan, len(arrays)), out...  45.1 us
  transfers between devices with their start and end apart: 1, of which 0 were waited for; matrix products, arithmetic and copies ran while one was open for 1% of the time, Pallas kernels for 28%

profile of v6, /device:TPU:0, one launch (start us, length us, event | category | flops | bytes accessed | tf_op | source)
XLA Modules:
  0.0 622.2 jit_solution(6052630784419048225)
XLA Ops:
  7.6 1.5 convert_reduce_fusion
  9.1 1.6 fusion.3
  10.7 0.5 broadcast.130
  11.3 0.7 reduce.3
  12.2 0.1 copy.25
  12.3 0.1 copy.26
  12.6 0.6 pad_maximum_fusion.3
  13.3 1.0 copy.30.col
  14.3 1.1 bitcast_dynamic-update-slice_fusion.1
  15.4 1.0 bitcast_dynamic-update-slice_fusion
  16.6 1.2 fusion.6.pack
  17.9 1.4 fusion.5.own
  19.3 1.2 copy-done.2
  20.5 81.0 %gather_rows.1 = (bf16[1024,2048]{1,0:T(8,128)(2,1)}, bf16[3648,2048]{1,0:T(8,128)(2,1)}) custom-call(bf16[256,2048]{1,0:T(8,128)(2,1)} %fusion.5.own, bf16[3648,256]{1,0:T(8,128)(2,1)} %copy-done.2), custom_call_target="tpu_custom_call" | custom-call | tf_op jit(solution)/shard_map/gather_rows/pallas_call | solution.py:346
  101.5 57.2 %forward.1 = (bf16[2,1024,256]{2,1,0:T(8,128)(2,1)}, bf16[2,1024,256]{2,1,0:T(8,128)(2,1)}, bf16[2,1024,432]{2,1,0:T(8,128)(2,1)}, f32[2,1024,432]{2,1,0:T(8,128...) custom-call(bf16[1024,2048]{1,0:T(8,128)(2,1)} %get-tuple-element.41, ...), custom_call_target="tpu_custom_call" | custom-call | tf_op jit(solution)/shard_map/forward/pallas_call | solution.py:1145
  158.7 248.6 %middle.1 = (bf16[1024,2048]{1,0:T(8,128)(2,1)}, bf16[1024,2048]{1,0:T(8,128)(2,1)}, bf16[1024,2048]{1,0:T(8,128)(2,1)}, bf16[1024,896]{1,0:T(8,128)(2,1)}, bf16...) custom-call(bf16[2,1024,432]{2,1,0:T(8,128)(2,1)} %get-tuple-element, ...), custom_call_target="tpu_custom_call" | custom-call | tf_op jit(solution)/shard_map/middle/pallas_call | solution.py:668
  407.3 19.1 %products_two.1 = bf16[2688,2048]{1,0:T(8,128)(2,1)} custom-call(bf16[1024,1792]{1,0:T(8,128)(2,1)} %get-tuple-element.66.refs_0_, bf16[1024,2048]{1,0:T(8,128)(2,1)} %get-tuple-element.67.refs_1_, bf16[1024,896]{1,0:T(8,128)(2,1)} %get-tuple-element.68.refs_2_, bf16[1024,2048]{1,0:T(8,128)(2,1)} %get-tuple-element.69.refs_3_), custom_call_target="tpu_custom_call" | custom-call | tf_op jit(solution)/shard_map/products_two/pallas_call | solution.py:1350
  426.5 48.6 %backward.1 = (bf16[1024,1024]{1,0:T(8,128)(2,1)}, bf16[2,1024,432]{2,1,0:T(8,128)(2,1)}, bf16[2,1024,432]{2,1,0:T(8,128)(2,1)}, bf16[192,2048]{1,0:T(8,128)(2,1)}) custom-call(bf16[1024,2048]{1,0:T(8,128)(2,1)} %get-tuple-element.47.mid.refs_1_, bf16[3648,2048]{1,0:T(8,128)(2,1)} %get-tuple-element.42.weight.out_weight.weights, ...), custom_call_target="tpu_custom_call" | custom-call | tf_op jit(solution)/shard_map/backward/pallas_call | solution.py:1284
  475.0 26.0 %products_one.1.grads = bf16[3648,2048]{1,0:T(8,128)(2,1)} custom-call(bf16[2,1024,432]{2,1,0:T(8,128)(2,1)} %get-tuple-element.43.gated.refs_0_, bf16[1024,2048]{1,0:T(8,128)(2,1)} %get-tuple-element.47.mid.refs_1_, bf16[2,1024,432]{2,1,0:T(8,128)(2,1)} %get-tuple-element.60.refs_2_.d_gate, bf16[1024,2048]{1,0:T(8,128)(2,1)} %get-tuple-element.41.rows.refs_3_, ...), custom_call_target="tpu_custom_call" | custom-call | tf_op jit(solution)/shard_map/products_one/pallas_call | solution.py:1350
  501.1 99.9 %last.1 = (f32[256,2048]{1,0:T(8,128)}, f32[32,128]{1,0:T(8,128)}, f32[3648,256]{1,0:T(8,128)}) custom-call(bf16[1024,1024]{1,0:T(8,128)(2,1)} %get-tuple-element.58.refs_4_.d_qk, bf16[2,1024,432]{2,1,0:T(8,128)(2,1)} %get-tuple-element.59.refs_5_.d_value, bf16[2,1024,432]{2,1,0:T(8,128)(2,1)} %get-tuple-element.60.refs_2_.d_gate, ...), custom_call_target="tpu_custom_call" | custom-call | tf_op jit(solution)/shard_map/last/pallas_call | solution.py:970
  601.0 1.4 slice_bitcast_fusion.4
  602.3 1.0 copy.33
  603.3 1.0 copy.32
  604.3 0.6 slice_bitcast_fusion.6
  604.9 1.0 pad_maximum_fusion
  606.0 3.2 fusion.14
  609.2 1.3 slice.54
  610.5 0.1 fusion.15
  610.7 1.0 slice_bitcast_fusion
  611.7 1.0 slice_bitcast_fusion.1
  612.7 1.0 slice.59
  613.7 1.3 copy.40
  (53 shorter events, 1.1 us)
Async XLA Ops:
  7.2 4.1 copy-start.14
  7.2 5.0 copy-start.9
  7.2 5.1 copy-start.10
  7.2 5.2 copy-start.5
  7.2 602.0 %reduce-scatter.2.cloned.1.call-start = ((), (), s32[]{:S(2)}) async-start(), calls=%async_computation.1 | async-start | bytes 12386304 | tf_op jit(solution)/shard_map/reduce_scatter | solution.py:1445
  7.3 5.2 copy-start.6
  14.3 2.3 copy-start.8
  16.5 1.4 copy-start
  16.5 1.4 copy-start.12
  16.6 2.6 copy-start.7
  19.3 1.2 copy-start.2
  600.9 3.4 copy-start.13
  601.0 4.0 copy-start.4
  601.0 4.0 copy-start.11
  610.7 2.0 copy-start.1
  611.7 2.0 copy-start.3
Sparse Core Ops, SparseCore 0:
  426.6 83.6 reduce-scatter.1

commit v7 on v6

--- a/solution.py
+++ b/solution.py
@@ -373,21 +373,22 @@
         from_right[...] = jnp.zeros_like(from_right)
 
 
-(COT, OUT, ONE, END_ONE, TWO, GLU, GRAD, GRAD_SUM, END_GRAD, MID, DOWN, DOWN_SUM, END_DOWN) = range(13)
+(COT, OUT, ONE, END_ONE, TWO, GLU, GRAD, GRAD_SUM, END_GRAD, MID, DOWN, DOWN_SUM, END_DOWN, PRODUCTS) = range(14)
 
 DUE = {
     OUT: (-2.23, 1.66, 0), ONE: (-1.99, 1.12, 1.03), END_ONE: (1.46, 1.37, 0), TWO: (0.73, 1.15, 0.94),
     COT: (0.35, 1.39, 1.02), GLU: (1.14, -1.37, 1.55), GRAD: (3.09, 2.02, 0),
     GRAD_SUM: (3.48, 1.71, 0.74), END_GRAD: (7.02, -2.12, 0), MID: (5.68, 0.86, 1.11),
     DOWN: (1.3, 0.36, 0), DOWN_SUM: (1.87, 1.35, 0.95), END_DOWN: (7.9, 2.17, 0),
+    PRODUCTS: (7.5, 0, 0.4),
 }
 TUNED = {
     (4, 4): [
-        3, 5, 4, 8, 8, 2, 8, 2, 7, 9, 12, 16, 9, 6, 16, 9, 10, 16, 3, 13,
-        11, 17, 16, 20, 10, 11, 2, 17, 20, 10, 17, 40, 11, 24, 14, 18, 2, 28, 17, 3,
-        21, 18, 28, 15, 19, 21, 25, 29, 44, 18, 18, 28, 19, 22, 29, 44, 22, 19, 32, 3,
-        36, 26, 30, 19, 29, 23, 36, 23, 36, 30, 33, 37, 30, 27, 31, 44, 34, 37, 38, 43,
-        37, 31, 41, 38, 48, 36, 42, 31, 37, 38, 35, 39, 38, 39, 39, 39,
+        2, 4, 5, 8, 8, 2, 7, 9, 8, 11, 2, 9, 2, 12, 16, 9, 16, 11, 6, 16,
+        13, 10, 16, 17, 20, 10, 11, 17, 20, 10, 24, 17, 15, 3, 14, 28, 18, 17, 21, 19,
+        21, 18, 19, 25, 28, 29, 18, 40, 3, 29, 19, 28, 44, 18, 22, 29, 3, 22, 19, 32,
+        36, 26, 30, 3, 33, 37, 23, 36, 30, 23, 44, 37, 30, 43, 27, 44, 36, 34, 37, 31,
+        31, 38, 48, 52, 31, 41, 38, 52, 35, 39, 36, 42, 38, 52, 37, 39, 38, 39, 39,
     ],
 }
 
@@ -396,7 +397,7 @@
     if (n, CHUNKS) in TUNED:
         return [divmod(code, CHUNKS) for code in TUNED[n, CHUNKS]]
     count = {k: 1 for k in DUE}
-    count.update({COT: n, TWO: n, MID: n, ONE: n - 1, GRAD_SUM: n - 1, DOWN_SUM: n - 1, GLU: 2})
+    count.update({COT: n, TWO: n, MID: n, ONE: n - 1, GRAD_SUM: n - 1, DOWN_SUM: n - 1, GLU: 2, PRODUCTS: 3})
     needs = {
         ONE: [OUT], END_ONE: [ONE], TWO: [END_ONE], GLU: [TWO, COT], GRAD: [GLU], GRAD_SUM: [GRAD],
         END_GRAD: [GRAD_SUM], MID: [END_GRAD], DOWN: [GLU], DOWN_SUM: [DOWN], END_DOWN: [DOWN_SUM],
@@ -406,13 +407,16 @@
         for k, (first, later, each) in DUE.items()
         for h in range(CHUNKS)
         for s in range(count[k])
-        if not (k == COT and h < FRONT or k in (DOWN_SUM, END_DOWN) and h >= DOWNS)
+        if not (k == PRODUCTS and h > 0 or k == COT and h < FRONT or k in (DOWN_SUM, END_DOWN) and h >= DOWNS)
     )
     taken, order = {}, []
     while todo:
         for item in todo:
             _, k, h, s = item
-            ready = taken.get((k, h), 0) == s and all(
+            ready = taken.get((k, h), 0) == s and (
+                k != PRODUCTS or all(taken.get((GLU, c), 0) == 2 for c in range(CHUNKS))
+            )
+            ready = ready and all(
                 taken.get((need, h), 0) == count[need] or (need == COT and h < FRONT)
                 for need in needs.get(k, [])
             )
@@ -426,10 +430,9 @@
 
 def middle_kernel(
     n, gated, weights, out_weight, own, cot, cot_front, gain,
-    rows_out, cot_out, mid_out, hidden_out, glu_out, down_out, outputs, middle_out, d_middle,
-    gain_out,
+    mid_out, products_out, down_out, outputs, middle_out, d_middle, gain_out,
     gated_v, wo_v, wg_v, wd_v, own_v, cot_v, rows_v, hidden_v, glu_v, part, part_two,
-    left_a, right_a, left_b, right_b, middle, stage, copy_sem, send_sem, recv_sem,
+    left_a, right_a, left_b, right_b, middle, stage, result, copy_sem, send_sem, recv_sem,
 ):
     line = Line(n, send_sem, recv_sem)
     place = line.place
@@ -616,6 +619,27 @@
         scatter_one[h].drain()
         grad_product(h)
 
+    def products_action(_):
+        k = len(products)
+        if k >= 2:
+            products[k - 2].wait()
+        left = hidden_v.at[...] if k == 2 else glu_v.at[:, pl.ds(k * wide, wide)]
+        right = cot_v if k == 2 else rows_v
+        target = result.at[k % 2]
+
+        def step(j, carry):
+            at = pl.ds(pl.multiple_of(j * 2 * LANES, 2 * LANES), 2 * LANES)
+            target[:, at] = dot_tn(left[...], right[:, at]).astype(BF)
+            return carry
+
+        lax.fori_loop(0, width // (2 * LANES), step, 0)
+        store = pltpu.make_async_copy(
+            target, products_out.at[pl.ds(k * wide, wide)], copy_sem.at[spare + k]
+        )
+        store.start()
+        products.append(store)
+
+    products, spare = [], copy_sem.shape[0] - 3
     begun = set()
     actions = {
         COT: lambda h: gather_cot[h].step(),
@@ -631,16 +655,12 @@
         DOWN: down_product,
         DOWN_SUM: lambda h: scatter_two[h].step(),
         END_DOWN: finish_two,
+        PRODUCTS: products_action,
     }
     for item in load_cot:
         item.wait()
     for kind, h in middle_order(n):
         actions[kind](h)
-    for c in range(CHUNKS):
-        local(chunk(rows_v, c), chunk(rows_out, c))
-        local(chunk(cot_v, c), chunk(cot_out, c))
-        local(chunk(hidden_v, c), chunk(hidden_out, c))
-        local(chunk(glu_v, c), chunk(glu_out, c))
     local(part_two.at[pl.ds(DOWNS * per, down_out.shape[0])], down_out)
     local(middle.at[pl.ds(DOWNS * piece, middle_out.shape[0])], middle_out)
     for item in list(gather_cot.values()) + gather_two + gather_mid:
@@ -650,8 +670,9 @@
     for group in (scatter_grad, scatter_two):
         for item in group:
             item.drain()
-    for item in copies[CHUNKS - FRONT + 6 :]:
+    for item in copies[CHUNKS - FRONT + 6 :] + products[1:]:
         item.wait()
+    assert len(products) == 3
     line.leave()
 
 
@@ -669,10 +690,7 @@
         functools.partial(middle_kernel, n),
         out_shape=(
             shape((tokens, width), BF),
-            shape((tokens, width), BF),
-            shape((tokens, width), BF),
-            shape((tokens, wide), BF),
-            shape((tokens, 2 * wide), BF),
+            shape((3 * wide, width), BF),
             shape((back * n * piece, width), BF),
             shape((DOWNS * piece, width), BF),
             shape((back * piece, width), F32),
@@ -680,7 +698,7 @@
             shape((8, width), F32),
         ),
         in_specs=[ANY] * 6 + [VM],
-        out_specs=(ANY,) * 6 + (VM, ANY, VM, VM),
+        out_specs=(ANY,) * 3 + (VM, ANY, VM, VM),
         scratch_shapes=[
             pltpu.VMEM((heads, tokens, size), BF),
             pltpu.VMEM((nv, width), BF),
@@ -699,7 +717,8 @@
             pltpu.VMEM((DOWNS,) + hop[1:], BF),
             pltpu.VMEM((rows, width), F32),
             pltpu.VMEM((CHUNKS, piece, width), BF),
-            pltpu.SemaphoreType.DMA((8 + 6 * CHUNKS - FRONT,)),
+            pltpu.VMEM((2, wide, width), BF),
+            pltpu.SemaphoreType.DMA((11 + 2 * CHUNKS - FRONT,)),
             pltpu.SemaphoreType.DMA((sems,)),
             pltpu.SemaphoreType.DMA((sems,)),
         ],
@@ -802,6 +821,32 @@
                 c.wait_send()
 
 
+def grad_scatter(m, grads, kept, held, summed, send_sem, recv_sem, load_sem):
+    bits = bits_of(m)
+    height = grads.shape[0] // (2 * PARTS)
+    out = []
+    for i in range(2 * PARTS):
+        order = bits[:1] + (bits[1:] if i % 2 == 0 else bits[:0:-1])
+        rows = pl.ds(i * height, height)
+        out.append(
+            Halving(
+                grads, rows, order, i * (m - 1), kept, held, summed, send_sem, recv_sem, load_sem.at[i]
+            )
+        )
+    return out, [out[0].flip(out[0].d, bit) for bit in bits]
+
+
+def scatter_scratch(m, rows, shard):
+    wide = 2 * PARTS * (m - 1)
+    counts = [m // 2] + [m >> (1 + k) for k in range(len(bits_of(m)))]
+    return [pltpu.VMEM((count, rows, shard), BF) for count in counts] + [
+        pltpu.VMEM((rows, shard), F32),
+        pltpu.SemaphoreType.DMA((wide,)),
+        pltpu.SemaphoreType.DMA((wide,)),
+        pltpu.SemaphoreType.DMA((2 * PARTS, m // 2)),
+    ]
+
+
 def exchange(groups, mine, total, send_sem, recv_sem):
     source, base = mine, 0
     for axis, size, held in groups:
@@ -834,14 +879,14 @@
 
 def last_kernel(
     n, m, d_qk, d_value, d_gate, weight, grads, inputs, gain, d_middle, second_gain,
-    out, gains, summed,
-    qk_v, value_v, gate_v, weight_v, inputs_v, middle_v, part, lefts, rights, kept, *rest
+    out, gains, grad_query, grad_key, grad_out, grad_gate, grad_value,
+    qk_v, value_v, gate_v, weight_v, inputs_v, middle_v, part, lefts, rights, *rest
 ):
     bits = bits_of(m)
-    held, (gain_sum, mine, first, second) = rest[: len(bits)], rest[len(bits) : len(bits) + 4]
-    copy_sem, send_sem, recv_sem, wide_send, wide_recv, load_sem, gain_send, gain_recv = rest[
-        len(bits) + 4 :
-    ]
+    kept, held = rest[0], rest[1 : 1 + len(bits)]
+    summed, wide_send, wide_recv, load_sem = rest[1 + len(bits) : 5 + len(bits)]
+    gain_sum, mine, first, second = rest[5 + len(bits) : 9 + len(bits)]
+    copy_sem, send_sem, recv_sem, gain_send, gain_recv = rest[9 + len(bits) :]
     line = Line(n, send_sem, recv_sem)
     count, width = out.shape
     piece = count // CHUNKS
@@ -867,16 +912,7 @@
             pl.semaphore_signal(barrier, inc=1, device_id={axis: peer}, device_id_type=MESH)
     pl.semaphore_wait(barrier, n + m - 2)
 
-    height = grads.shape[0] // (2 * PARTS)
-    halving = []
-    for i in range(2 * PARTS):
-        order = bits[:1] + (bits[1:] if i % 2 == 0 else bits[:0:-1])
-        halving.append(
-            Halving(
-                grads, pl.ds(i * height, height), order, i * (m - 1), kept, held, summed,
-                wide_send, wide_recv, load_sem.at[i],
-            )
-        )
+    halving, _ = grad_scatter(m, grads, kept, held, summed, wide_send, wide_recv, load_sem)
     for item in halving:
         item.step()
     for item in halving:
@@ -947,11 +983,29 @@
         flat = jnp.sum(source[...], axis=0, keepdims=True)
         for j in range(width // LANES):
             mine[pl.ds(i * (width // LANES) + j, 1), :] = flat[:, j * LANES : (j + 1) * LANES]
-    exchange(groups, mine, gains, gain_send, gain_recv)
     for item in halving:
         while item.done <= len(bits):
             item.step()
+    stores, base = [], 0
+    for target in (grad_out, grad_gate):
+        source = summed.at[pl.ds(base, target.shape[0])]
+        stores.append(pltpu.make_async_copy(source, target, copy_sem.at[len(load) + len(stores)]))
+        base += target.shape[0]
+    deep = grad_query.shape[1]
+    value_base = base + 2 * deep
+    source = summed.at[pl.ds(value_base, grad_value.shape[0])]
+    stores.append(pltpu.make_async_copy(source, grad_value, copy_sem.at[len(load) + len(stores)]))
+    for store in stores:
+        store.start()
+    for target in (grad_query, grad_key):
+        for j in range(deep // LANES):
+            target[:, j * LANES : (j + 1) * LANES] = summed[pl.ds(base, LANES), :].T
+            base += LANES
+    exchange(groups, mine, gains, gain_send, gain_recv)
+    for item in halving:
         item.leave()
+    for store in stores:
+        store.wait()
     for h in range(CHUNKS):
         scatters[h].drain()
 
@@ -962,18 +1016,20 @@
     heads = d_value.shape[0]
     shard = width // m
     sems = CHUNKS * 2 * (n - 1)
-    wide = 2 * PARTS * (m - 1)
     hop = (CHUNKS, n - 1, rows // CHUNKS, width)
     flat = (2 * width // LANES, LANES)
-    levels = [m >> (1 + k) for k in range(len(bits_of(m)))]
     shape = jax.ShapeDtypeStruct
     return pl.pallas_call(
         functools.partial(last_kernel, n, m),
         out_shape=(
-            shape((rows, width), F32), shape(flat, F32), shape((grads.shape[0], shard), F32),
-        ),
+            shape((rows, width), F32),
+            shape(flat, F32),
+            shape((shard, heads * HK), F32),
+            shape((shard, heads * HK), F32),
+        )
+        + (shape((heads * HV, shard), F32),) * 3,
         in_specs=[ANY] * 6 + [VM, ANY, VM],
-        out_specs=(VM,) * 3,
+        out_specs=(VM,) * 4 + (ANY,) * 3,
         scratch_shapes=[
             pltpu.VMEM(d_qk.shape, BF),
             pltpu.VMEM(d_value.shape, BF),
@@ -984,20 +1040,16 @@
             pltpu.VMEM((tokens, width), BF),
             pltpu.VMEM(hop, BF),
             pltpu.VMEM(hop, BF),
-            pltpu.VMEM((m // 2, grads.shape[0], shard), BF),
         ]
-        + [pltpu.VMEM((count, grads.shape[0], shard), BF) for count in levels]
+        + scatter_scratch(m, grads.shape[0], shard)
         + [
             pltpu.VMEM((8, width), F32),
             pltpu.VMEM(flat, F32),
             pltpu.VMEM((m,) + flat, F32),
             pltpu.VMEM((n,) + flat, F32),
-            pltpu.SemaphoreType.DMA((6,)),
+            pltpu.SemaphoreType.DMA((9,)),
             pltpu.SemaphoreType.DMA((sems,)),
             pltpu.SemaphoreType.DMA((sems,)),
-            pltpu.SemaphoreType.DMA((wide,)),
-            pltpu.SemaphoreType.DMA((wide,)),
-            pltpu.SemaphoreType.DMA((2 * PARTS, m // 2)),
             pltpu.SemaphoreType.DMA((n + m,)),
             pltpu.SemaphoreType.DMA((n + m,)),
         ],
@@ -1164,11 +1216,15 @@
 
 
 def backward_kernel(
-    n, mid, weights, gate, norm, scale, scores, query, key, value, down, middle, col, row,
-    qk_o, value_o, gate_o, outputs,
+    n, m, mid, weights, gate, norm, scale, scores, query, key, value, down, middle, grads, col, row,
+    qk_o, value_o, gate_o, glu_gate_o, glu_up_o, down_o, outputs,
     mid_v, wo_v, gate_v, norm_v, scale_v, scores_v, query_v, key_v, value_v, part, middle_v,
-    d_qk, d_value, d_gate, d_kept, d_scores, lefts, rights, copy_sem, send_sem, recv_sem,
+    d_qk, d_value, d_gate, d_kept, d_scores, lefts, rights, *rest
 ):
+    bits = bits_of(m)
+    kept, held = rest[0], rest[1 : 1 + len(bits)]
+    summed, wide_send, wide_recv, load_sem = rest[1 + len(bits) : 5 + len(bits)]
+    copy_sem, send_sem, recv_sem = rest[5 + len(bits) :]
     line = Line(n, send_sem, recv_sem)
     heads, tokens, deep = query_v.shape
     size = value_v.shape[2]
@@ -1192,7 +1248,12 @@
             (query, query_v), (scores, scores_v), (middle, middle_v),
         )
     ]
-    line.enter()
+    halving, peers = grad_scatter(m, grads, kept, held, summed, wide_send, wide_recv, load_sem)
+    line.enter(["dp", peers])
+    for item in halving:
+        item.step()
+    for item in halving:
+        item.load()
     for h in range(back):
         no_neighbour_zero(n, line.place, lefts.at[h, n - 2], rights.at[h, n - 2])
     scatters = [
@@ -1243,11 +1304,31 @@
     units = []
     for h in range(heads):
         units += [gates(h), by_row(h), by_column(h)]
-    in_order(units, [item.step for _ in range(n - 2) for item in scatters])
+    steps = [item.step for _ in range(n - 2) for item in scatters]
+    wide_steps = [item.step for _ in bits for item in halving]
+    mixed = []
+    for i in range(max(len(steps), len(wide_steps))):
+        mixed += steps[i : i + 1] + wide_steps[i : i + 1]
+    late = mixed[-2 * PARTS :]
+    in_order(units, mixed[: -2 * PARTS])
     count = len(copies)
     local(d_qk, qk_o)
     local(d_value, value_o)
     local(d_gate, gate_o)
+    for step in late:
+        step()
+    size = down_o.shape[0]
+    wide = grads.shape[0] // 3
+    for t in range(wide // LANES):
+        have = min(LANES, size - t * LANES)
+        for i, target in enumerate((glu_gate_o, glu_up_o)):
+            local(
+                summed.at[pl.ds((2 * t + i) * LANES, have)], target.at[pl.ds(t * LANES, have)]
+            )
+    local(summed.at[pl.ds(2 * wide, size)], down_o)
+    for item in halving:
+        assert item.done == len(bits) + 1
+        item.leave()
     for h in range(back):
         scatters[h].finish()
 
@@ -1266,26 +1347,26 @@
         item.drain()
 
 
-def backward_call(mid, weights, gate, norm, scale, scores, query, key, value, down, middle, col, row, n):
+def backward_call(mid, weights, gate, norm, scale, scores, query, key, value, down, middle, grads, size_two, col, row, n, m):
     tokens, width = mid.shape
     heads, _, size = value.shape
     back = CHUNKS - DOWNS
     nv = heads * size
+    shard = width // m
     shape = jax.ShapeDtypeStruct
     outs = (
         shape((tokens, 2 * heads * HK), BF),
         shape(value.shape, BF),
         shape(value.shape, BF),
-        shape(middle.shape, BF),
-    )
+    ) + (shape((size_two, shard), F32),) * 3 + (shape(middle.shape, BF),)
     ins = (gate, norm, scale, scores, query, key, value, down, middle)
     hop = (back, n - 1, middle.shape[0] // back, width)
     sems = back * 2 * (n - 1)
     return pl.pallas_call(
-        functools.partial(backward_kernel, n),
+        functools.partial(backward_kernel, n, m),
         out_shape=outs,
-        in_specs=[ANY] * 11 + [VM] * 2,
-        out_specs=(ANY,) * 3 + (VM,),
+        in_specs=[ANY] * 12 + [VM] * 2,
+        out_specs=(ANY,) * 6 + (VM,),
         scratch_shapes=[pltpu.VMEM(mid.shape, BF), pltpu.VMEM((nv, width), BF)]
         + [pltpu.VMEM(a.shape, a.dtype) for a in ins]
         + [pltpu.VMEM(o.shape, o.dtype) for o in outs[:3]]
@@ -1294,7 +1375,10 @@
             pltpu.VMEM((tokens, tokens), BF),
             pltpu.VMEM(hop, BF),
             pltpu.VMEM(hop, BF),
-            pltpu.SemaphoreType.DMA((14,)),
+        ]
+        + scatter_scratch(m, grads.shape[0], shard)
+        + [
+            pltpu.SemaphoreType.DMA((15 + 2 * (grads.shape[0] // (3 * LANES)),)),
             pltpu.SemaphoreType.DMA((sems,)),
             pltpu.SemaphoreType.DMA((sems,)),
         ],
@@ -1302,7 +1386,7 @@
             collective_id=5, has_side_effects=True, vmem_limit_bytes=VMEM_MOST
         ),
         name="backward",
-    )(mid, weights, *ins, col, row)
+    )(mid, weights, *ins, grads, col, row)
 
 
 def products_kernel(plan, arrays, *refs):
@@ -1433,21 +1517,12 @@
     (
         query, key, value, gate_pre, normalized, scale_group, scores, gated, cot_front, weight_two,
     ) = forward_call(rows_one, weight_one, cotangent, col, row, pack_two, n, m, heads)
-    (
-        rows_two, cot_rows, mid_rows, hidden, d_glu, down, outputs_front, middle, middle_grad,
-        second_gain,
-    ) = middle_call(
+    mid_rows, grads_two, down, outputs_front, middle, middle_grad, second_gain = middle_call(
         gated, weight_two, weight_one, inputs, cotangent, cot_front, second_norm_gain[None], n
     )
-
-    plan = [(0, None, t * f_wide, f_wide, 1) for t in range(2)] + [(2, None, 0, f_wide, 3)]
-    grads_two = weight_products(plan, (d_glu, rows_two, hidden, cot_rows), "products_two", 3 * f_wide)
-    summed_two = lax.psum_scatter(grads_two, "dp", scatter_dimension=1, tiled=True).astype(F32)
-    glu_sum = summed_two[: 2 * f_wide].reshape(f_tiles, 2, LANES, shard)
-
-    d_qk, d_value, d_gate, outputs_back = backward_call(
+    d_qk, d_value, d_gate, grad_glu_gate, grad_glu_up, grad_down, outputs_back = backward_call(
         mid_rows, weight_one, gate_pre, normalized, scale_group, scores, query, key, value,
-        down, middle, col, row, n,
+        down, middle, grads_two, nf, col, row, n, m,
     )
     plan = [(0, h, 0, HV, 1) for h in range(heads)] + [(2, h, 0, HV, 3) for h in range(heads)]
     plan += [(4, None, t * nk, nk, 3) for t in range(2)]
@@ -1455,25 +1530,24 @@
     grads_one = weight_products(
         plan, (gated, mid_rows, d_gate, rows_one, d_qk, d_value), "products_one", one_rows
     )
-    input_gradient, gains, summed_one = last_call(
+    input_gradient, gains, grad_query, grad_key, grad_out, grad_gate, grad_value = last_call(
         d_qk, d_value, d_gate, weight_one, grads_one, inputs, first_norm_gain[None], middle_grad,
         second_gain, n, m,
     )
     gains = gains.reshape(2, width)
-    at = 2 * nv
     return (
         jnp.concatenate([outputs_front, outputs_back], axis=0),
         input_gradient,
         gains[0],
-        summed_one[at : at + nk].T,
-        summed_one[at + nk : at + 2 * nk].T,
-        summed_one[at + 2 * nk : at + 2 * nk + nv].T,
-        summed_one[nv : 2 * nv].T,
-        summed_one[:nv],
+        grad_query,
+        grad_key,
+        grad_value.T,
+        grad_gate.T,
+        grad_out,
         gains[1],
-        glu_sum[:, 0].reshape(f_wide, shard)[:nf].T,
-        glu_sum[:, 1].reshape(f_wide, shard)[:nf].T,
-        summed_two[2 * f_wide : 2 * f_wide + nf],
+        grad_glu_gate.T,
+        grad_glu_up.T,
+        grad_down,
     )
 
 

time: 632 us -> 603 us (0.954); the launches traced: 622 us -> 602 us
  between operations: 14.8 us -> 0.97 us
    pallas_call x2 -> x1, Pallas kernels: 45.1 us -> 26 us  [weight_products(): pl.pallas_call(functools.partial(products_kernel, plan, len(arrays)), out...]
    pallas_call x1, Pallas kernels: 48.6 us -> 67.5 us  [backward_call(): pl.pallas_call(functools.partial(backward_kernel, n, m), out_shape=outs,...]
    unnamed x41 -> x59, local copies, waits for them, and re-layouts: 7.69 us -> 13.1 us
  transfers between devices with their start and end apart: 1 -> 0, of which waited for: 0 -> 0; matrix products, arithmetic and copies ran while one was open for 1% -> 0% of each run, Pallas kernels for 28% -> 0%
where the time goes in v7:
time: 603 us; the launch traced here: 602 us
  Pallas kernels  576 us (96%)
  local copies, waits for them, and re-layouts  15.9 us (3%)
  other arithmetic  9.61 us (2%)
    pallas_call x1, Pallas kernels, middle_call(): pl.pallas_call(functools.partial(middle_kernel, n), out_shape=(shape((tok...  242 us
    pallas_call x1, Pallas kernels, last_call(): pl.pallas_call(functools.partial(last_kernel, n, m), out_shape=(shape((ro...  102 us
    pallas_call x1, Pallas kernels, gather_rows(): pl.pallas_call(functools.partial(gather_kernel, n, m), out_shape=(jax.Sha...  81 us
    pallas_call x1, Pallas kernels, backward_call(): pl.pallas_call(functools.partial(backward_kernel, n, m), out_shape=outs,...  67.5 us
    pallas_call x1, Pallas kernels, forward_call(): pl.pallas_call(functools.partial(forward_kernel, n, m), out_shape=outs, i...  57.1 us
    pallas_call x1, Pallas kernels, weight_products(): pl.pallas_call(functools.partial(products_kernel, plan, len(arrays)), out...  26 us
    unnamed x59, local copies, waits for them, and re-layouts  13.1 us

profile of v7, /device:TPU:0, one launch (start us, length us, event | category | flops | bytes accessed | tf_op | source)
XLA Modules:
  0.0 602.5 jit_solution(214939078174689051)
XLA Ops:
  0.8 1.5 convert_reduce_fusion
  2.3 1.6 fusion.3
  4.0 0.5 broadcast.130
  4.5 0.7 reduce.3
  5.3 0.1 convert_element_type.56
  5.6 0.1 fusion.8
  5.7 0.6 pad_maximum_fusion.3
  6.4 0.1 copy.25
  6.5 0.1 copy.26
  6.8 0.1 pad_maximum_fusion.1
  6.9 0.6 copy-done.15
  7.5 1.2 fusion.6.pack
  8.7 1.0 copy.30.col
  9.8 1.4 fusion.5.own
  11.3 1.2 copy-done.1
  12.6 81.0 %gather_rows.1 = (bf16[1024,2048]{1,0:T(8,128)(2,1)}, bf16[3648,2048]{1,0:T(8,128)(2,1)}) custom-call(bf16[256,2048]{1,0:T(8,128)(2,1)} %fusion.5.own, bf16[3648,256]{1,0:T(8,128)(2,1)} %copy-done.1), custom_call_target="tpu_custom_call" | custom-call | tf_op jit(solution)/shard_map/gather_rows/pallas_call | solution.py:346
  93.5 57.1 %forward.1 = (bf16[2,1024,256]{2,1,0:T(8,128)(2,1)}, bf16[2,1024,256]{2,1,0:T(8,128)(2,1)}, bf16[2,1024,432]{2,1,0:T(8,128)(2,1)}, f32[2,1024,432]{2,1,0:T(8,128...) custom-call(bf16[1024,2048]{1,0:T(8,128)(2,1)} %get-tuple-element.45, ...), custom_call_target="tpu_custom_call" | custom-call | tf_op jit(solution)/shard_map/forward/pallas_call | solution.py:1197
  150.6 242.5 %middle.1 = (bf16[1024,2048]{1,0:T(8,128)(2,1)}, bf16[2688,2048]{1,0:T(8,128)(2,1)}, bf16[768,2048]{1,0:T(8,128)(2,1)}, bf16[64,2048]{1,0:T(8,128)(2,1)}, f32[19...) custom-call(bf16[2,1024,432]{2,1,0:T(8,128)(2,1)} %get-tuple-element.47.gated.refs_0_, ...), custom_call_target="tpu_custom_call" | custom-call | tf_op jit(solution)/shard_map/middle/pallas_call | solution.py:689
  393.1 67.5 %backward.1 = (bf16[1024,1024]{1,0:T(8,128)(2,1)}, bf16[2,1024,432]{2,1,0:T(8,128)(2,1)}, bf16[2,1024,432]{2,1,0:T(8,128)(2,1)}, f32[864,256]{1,0:T(8,128)}, f32...) custom-call(bf16[1024,2048]{1,0:T(8,128)(2,1)} %get-tuple-element.51.mid.refs_1_, ...), custom_call_target="tpu_custom_call" | custom-call | tf_op jit(solution)/shard_map/backward/pallas_call | solution.py:1365
  460.6 2.2 pad_maximum_fusion
  462.8 26.0 %products_one.1.grads = bf16[3648,2048]{1,0:T(8,128)(2,1)} custom-call(bf16[2,1024,432]{2,1,0:T(8,128)(2,1)} %get-tuple-element.47.gated.refs_0_, bf16[1024,2048]{1,0:T(8,128)(2,1)} %get-tuple-element.51.mid.refs_1_, bf16[2,1024,432]{2,1,0:T(8,128)(2,1)} %get-tuple-element.65.refs_2_.d_gate, bf16[1024,2048]{1,0:T(8,128)(2,1)} %get-tuple-element.45.rows.refs_3_, ...), custom_call_target="tpu_custom_call" | custom-call | tf_op jit(solution)/shard_map/products_one/pallas_call | solution.py:1434
  488.9 102.0 %last.1 = (f32[256,2048]{1,0:T(8,128)}, f32[32,128]{1,0:T(8,128)}, f32[256,512]{1,0:T(8,128)}, f32[256,512]{1,0:T(8,128)}, f32[864,256]{1,0:T(8,128)}, /*index=5*/f32[864,256]{1,0:T(8,128)}, f32[864,256]{1,0:T(8,128)}) custom-call(bf16[1024,1024]{1,0:T(8,128)(2,1)} %get-tuple-element.63.refs_4_.d_qk, ...), custom_call_target="tpu_custom_call" | custom-call | tf_op jit(solution)/shard_map/last/pallas_call | solution.py:1022
  590.8 1.3 slice_bitcast_fusion
  592.2 3.2 copy.46
  595.4 0.8 copy.47
  596.2 0.8 copy.48
  597.0 0.9 copy.49
  597.9 0.9 copy.50
  598.8 0.9 copy.51
  599.7 0.9 copy.52
  600.7 0.9 copy.53
  601.6 0.9 copy.54
  (60 shorter events, 0.8 us)
Async XLA Ops:
  0.6 6.0 copy-start.10
  0.7 5.8 copy-start.17
  0.7 5.7 copy-start.16
  0.7 3.8 copy-start.20
  0.8 5.9 copy-start.11
  6.5 1.0 copy-start.15
  6.9 2.9 copy-start
  6.9 2.9 copy-start.19
  8.7 2.4 copy-start.12
  9.8 1.5 copy-start.13
  9.8 1.5 copy-start.14
  11.3 1.2 copy-start.1
  393.1 67.5 %copy-start.18 = (bf16[64,2048]{1,0:T(8,128)(2,1)S(1)}, bf16[64,2048]{1,0:T(8,128)(2,1)}, u32[]{:S(2)}) copy-start(bf16[64,2048]{1,0:T(8,128)(2,1)} %get-tuple-element.50) | copy-start | bytes 786436
  592.2 3.2 copy-start.9
  592.2 4.0 copy-start.8
  595.4 1.6 copy-start.7
  595.4 2.5 copy-start.6
  596.2 2.6 copy-start.5
  597.9 1.8 copy-start.4
  598.8 1.8 copy-start.3
  599.7 1.8 copy-start.2

commit v8 on v7

--- a/solution.py
+++ b/solution.py
@@ -14,6 +14,7 @@
 CHUNKS = 4
 FRONT = CHUNKS // 2
 DOWNS = CHUNKS // 4
+ENDS = CHUNKS // 4
 LANES = 128
 VMEM_MOST = 66_000_000
 
@@ -373,31 +374,32 @@
         from_right[...] = jnp.zeros_like(from_right)
 
 
-(COT, OUT, ONE, END_ONE, TWO, GLU, GRAD, GRAD_SUM, END_GRAD, MID, DOWN, DOWN_SUM, END_DOWN, PRODUCTS) = range(14)
+(COT, OUT, ONE, END_ONE, TWO, GLU, GRAD, GRAD_SUM, END_GRAD, MID, DOWN, DOWN_SUM, END_DOWN, PRODUCTS, WIDE) = range(15)
 
 DUE = {
     OUT: (-2.23, 1.66, 0), ONE: (-1.99, 1.12, 1.03), END_ONE: (1.46, 1.37, 0), TWO: (0.73, 1.15, 0.94),
     COT: (0.35, 1.39, 1.02), GLU: (1.14, -1.37, 1.55), GRAD: (3.09, 2.02, 0),
     GRAD_SUM: (3.48, 1.71, 0.74), END_GRAD: (7.02, -2.12, 0), MID: (5.68, 0.86, 1.11),
     DOWN: (1.3, 0.36, 0), DOWN_SUM: (1.87, 1.35, 0.95), END_DOWN: (7.9, 2.17, 0),
-    PRODUCTS: (7.5, 0, 0.4),
+    PRODUCTS: (7.5, 0, 0.4), WIDE: (-4, 0.05, 1.5),
 }
 TUNED = {
-    (4, 4): [
-        2, 4, 5, 8, 8, 2, 7, 9, 8, 11, 2, 9, 2, 12, 16, 9, 16, 11, 6, 16,
-        13, 10, 16, 17, 20, 10, 11, 17, 20, 10, 24, 17, 15, 3, 14, 28, 18, 17, 21, 19,
-        21, 18, 19, 25, 28, 29, 18, 40, 3, 29, 19, 28, 44, 18, 22, 29, 3, 22, 19, 32,
-        36, 26, 30, 3, 33, 37, 23, 36, 30, 23, 44, 37, 30, 43, 27, 44, 36, 34, 37, 31,
-        31, 38, 48, 52, 31, 41, 38, 52, 35, 39, 36, 42, 38, 52, 37, 39, 38, 39, 39,
+    (4, 4, 3): [
+        58, 2, 4, 57, 59, 8, 56, 2, 5, 57, 8, 58, 8, 9, 3, 59, 7, 12, 56, 2,
+        16, 9, 58, 6, 16, 9, 57, 10, 59, 56, 16, 13, 11, 17, 57, 3, 10, 16, 58, 17,
+        11, 56, 59, 20, 10, 20, 17, 24, 11, 14, 28, 18, 3, 15, 28, 18, 19, 2, 17, 21,
+        28, 21, 40, 44, 18, 19, 25, 32, 29, 36, 18, 22, 29, 19, 44, 22, 29, 26, 36, 30,
+        44, 19, 3, 23, 33, 36, 37, 30, 23, 27, 37, 31, 30, 52, 37, 31, 34, 38, 42, 41,
+        48, 31, 38, 52, 35, 39, 38, 39, 36, 37, 38, 52, 39, 43, 39,
     ],
 }
 
 
-def middle_order(n):
-    if (n, CHUNKS) in TUNED:
-        return [divmod(code, CHUNKS) for code in TUNED[n, CHUNKS]]
+def middle_order(n, levels):
+    if (n, CHUNKS, levels) in TUNED:
+        return [divmod(code, CHUNKS) for code in TUNED[n, CHUNKS, levels]]
     count = {k: 1 for k in DUE}
-    count.update({COT: n, TWO: n, MID: n, ONE: n - 1, GRAD_SUM: n - 1, DOWN_SUM: n - 1, GLU: 2, PRODUCTS: 3})
+    count.update({COT: n, TWO: n, MID: n, ONE: n - 1, GRAD_SUM: n - 1, DOWN_SUM: n - 1, GLU: 2, PRODUCTS: 3, WIDE: levels + 1})
     needs = {
         ONE: [OUT], END_ONE: [ONE], TWO: [END_ONE], GLU: [TWO, COT], GRAD: [GLU], GRAD_SUM: [GRAD],
         END_GRAD: [GRAD_SUM], MID: [END_GRAD], DOWN: [GLU], DOWN_SUM: [DOWN], END_DOWN: [DOWN_SUM],
@@ -416,6 +418,9 @@
             ready = taken.get((k, h), 0) == s and (
                 k != PRODUCTS or all(taken.get((GLU, c), 0) == 2 for c in range(CHUNKS))
             )
+            ready = ready and (
+                k != GLU or all(taken.get((WIDE, c), 0) == levels + 1 for c in range(2 * PARTS))
+            )
             ready = ready and all(
                 taken.get((need, h), 0) == count[need] or (need == COT and h < FRONT)
                 for need in needs.get(k, [])
@@ -429,10 +434,11 @@
 
 
 def middle_kernel(
-    n, gated, weights, out_weight, own, cot, cot_front, gain,
-    mid_out, products_out, down_out, outputs, middle_out, d_middle, gain_out,
-    gated_v, wo_v, wg_v, wd_v, own_v, cot_v, rows_v, hidden_v, glu_v, part, part_two,
+    n, m, gated, pack, out_weight, own, cot, cot_front, gain,
+    mid_out, glu_out, product_out, down_out, outputs, middle_out, d_middle, gain_out,
+    gated_v, wo_v, weights_v, own_v, cot_v, rows_v, hidden_v, glu_v, part, part_two,
     left_a, right_a, left_b, right_b, middle, stage, result, copy_sem, send_sem, recv_sem,
+    wide_send, wide_recv,
 ):
     line = Line(n, send_sem, recv_sem)
     place = line.place
@@ -461,9 +467,10 @@
         out_weight.at[pl.ds(out_weight.shape[0] - wo_v.shape[0], wo_v.shape[0])], wo_v
     )
     load_own = local(own, own_v)
-    load_wg = local(weights.at[pl.ds(0, 2 * wide)], wg_v)
-    load_wd = local(weights.at[pl.ds(2 * wide, wide)], wd_v)
-    line.enter()
+    load_pack = local(pack, own_columns(pack, weights_v))
+    wg_v, wd_v = weights_v.at[pl.ds(0, 2 * wide)], weights_v.at[pl.ds(2 * wide, wide)]
+    doubling, peers = weight_gather(m, pack, weights_v, wide_send, wide_recv)
+    line.enter(["dp", peers])
     for h in range(CHUNKS):
         no_neighbour_zero(n, place, left_a.at[h, n - 2], right_a.at[h, n - 2])
     for h in range(DOWNS):
@@ -597,7 +604,7 @@
         items.clear()
 
     first_loads, own_load = [load_gated, load_wo], [load_own]
-    later_loads = [load_wg, load_wd]
+    later_loads = [load_pack]
 
     def out_action(h):
         wait_for(first_loads)
@@ -609,6 +616,7 @@
 
     def glu_action(h):
         wait_for(later_loads)
+        assert all(item.done == len(bits_of(m)) + 1 for item in doubling)
         if h in begun:
             glu_tiles(h, cut, tiles)
         else:
@@ -633,9 +641,8 @@
             return carry
 
         lax.fori_loop(0, width // (2 * LANES), step, 0)
-        store = pltpu.make_async_copy(
-            target, products_out.at[pl.ds(k * wide, wide)], copy_sem.at[spare + k]
-        )
+        place_out = product_out if k == 2 else glu_out.at[pl.ds(k * wide, wide)]
+        store = pltpu.make_async_copy(target, place_out, copy_sem.at[spare + k])
         store.start()
         products.append(store)
 
@@ -656,10 +663,11 @@
         DOWN_SUM: lambda h: scatter_two[h].step(),
         END_DOWN: finish_two,
         PRODUCTS: products_action,
+        WIDE: lambda h: doubling[h].step(),
     }
     for item in load_cot:
         item.wait()
-    for kind, h in middle_order(n):
+    for kind, h in middle_order(n, len(bits_of(m))):
         actions[kind](h)
     local(part_two.at[pl.ds(DOWNS * per, down_out.shape[0])], down_out)
     local(middle.at[pl.ds(DOWNS * piece, middle_out.shape[0])], middle_out)
@@ -670,40 +678,42 @@
     for group in (scatter_grad, scatter_two):
         for item in group:
             item.drain()
-    for item in copies[CHUNKS - FRONT + 6 :] + products[1:]:
+    for item in copies[CHUNKS - FRONT + 5 :] + products[1:]:
         item.wait()
     assert len(products) == 3
+    for item in doubling:
+        item.leave()
     line.leave()
 
 
-def middle_call(gated, weights, out_weight, own, cot, cot_front, gain, n):
+def middle_call(gated, pack, out_weight, own, cot, cot_front, gain, n, m):
     rows, width = own.shape
     heads, tokens, size = gated.shape
     nv = heads * size
-    wide = weights.shape[0] // 3
+    wide = pack.shape[0] // 3
     piece = rows // CHUNKS
     back = CHUNKS - DOWNS
     sems = CHUNKS * 5 * 2 * (n - 1)
     hop = (CHUNKS, n - 1, piece, width)
     shape = jax.ShapeDtypeStruct
     return pl.pallas_call(
-        functools.partial(middle_kernel, n),
+        functools.partial(middle_kernel, n, m),
         out_shape=(
             shape((tokens, width), BF),
-            shape((3 * wide, width), BF),
+            shape((2 * wide, width), BF),
+            shape((wide, width), BF),
             shape((back * n * piece, width), BF),
             shape((DOWNS * piece, width), BF),
             shape((back * piece, width), F32),
             shape((rows, width), F32),
             shape((8, width), F32),
         ),
-        in_specs=[ANY] * 6 + [VM],
-        out_specs=(ANY,) * 3 + (VM, ANY, VM, VM),
+        in_specs=[ANY, VM] + [ANY] * 4 + [VM],
+        out_specs=(ANY,) * 4 + (VM, ANY, VM, VM),
         scratch_shapes=[
             pltpu.VMEM((heads, tokens, size), BF),
             pltpu.VMEM((nv, width), BF),
-            pltpu.VMEM((2 * wide, width), BF),
-            pltpu.VMEM((wide, width), BF),
+            pltpu.VMEM((3 * wide, width), BF),
             pltpu.VMEM((rows, width), BF),
             pltpu.VMEM((tokens, width), BF),
             pltpu.VMEM((tokens, width), BF),
@@ -721,12 +731,14 @@
             pltpu.SemaphoreType.DMA((11 + 2 * CHUNKS - FRONT,)),
             pltpu.SemaphoreType.DMA((sems,)),
             pltpu.SemaphoreType.DMA((sems,)),
+            pltpu.SemaphoreType.DMA((2 * PARTS * (m - 1),)),
+            pltpu.SemaphoreType.DMA((2 * PARTS * (m - 1),)),
         ],
         compiler_params=pltpu.CompilerParams(
             collective_id=1, has_side_effects=True, vmem_limit_bytes=VMEM_MOST
         ),
         name="middle",
-    )(gated, weights, out_weight, own, cot, cot_front, gain)
+    )(gated, pack, out_weight, own, cot, cot_front, gain)
 
 
 class Halving:
@@ -1082,10 +1094,10 @@
 
 
 def forward_kernel(
-    n, m, rows, weight, cot, col, row, pack,
-    query_o, key_o, value_o, gate_o, norm_o, scale_o, scores_o, gated_o, cot_o, second_o,
+    n, rows, weight, cot, col, row,
+    query_o, key_o, value_o, gate_o, norm_o, scale_o, scores_o, gated_o, cot_o,
     rows_v, weight_v, query_v, key_v, value_v, gate_v, norm_v, scale_v, scores_v, gated_v, cot_v,
-    copy_sem, send_sem, recv_sem, wide_send, wide_recv,
+    copy_sem, send_sem, recv_sem,
 ):
     line = Line(n, send_sem, recv_sem)
     heads, tokens, deep = query_v.shape
@@ -1106,17 +1118,15 @@
     ]
     load_rows = local(rows, rows_v)
     load_weight = local(weight.at[pl.ds(0, weight_v.shape[0])], weight_v)
-    doubling, peers = weight_gather(m, pack, second_o, wide_send, wide_recv)
-    line.enter(["dp", peers])
+    line.enter()
     gathers = [
         Gather(line, lambda k, h=h: cot_v.at[pl.ds(h * per + k * piece, piece)])
         for h in range(FRONT)
     ]
     for item in load_cot:
         item.wait()
-    for g in gathers + doubling:
+    for g in gathers:
         g.step()
-    local(pack, own_columns(pack, second_o))
     load_rows.wait()
     load_weight.wait()
 
@@ -1152,31 +1162,20 @@
             project(gate_v, h, gates + h * size, size),
             attend(h),
         ]
-    steps = [g.step for _ in range(n - 1) for g in gathers]
-    wide_steps = [g.step for _ in range(len(bits_of(m))) for g in doubling]
-    mixed = []
-    for i in range(max(len(steps), len(wide_steps))):
-        mixed += steps[i : i + 1] + wide_steps[i : i + 1]
-    late = mixed[-2 * PARTS :]
-    in_order(units, mixed[: -2 * PARTS])
-    count = len(copies) - 1
+    in_order(units, [g.step for _ in range(n - 1) for g in gathers])
+    count = len(copies)
     for src, dst in (
         (query_v, query_o), (key_v, key_o), (value_v, value_o), (gate_v, gate_o),
         (norm_v, norm_o), (scale_v, scale_o), (scores_v, scores_o), (gated_v, gated_o),
         (cot_v, cot_o),
     ):
         local(src, dst)
-    for step in late:
-        step()
     for item in copies[count:]:
         item.wait()
-    for item in doubling:
-        assert item.done == len(bits_of(m)) + 1
-        item.leave()
     line.leave()
 
 
-def forward_call(rows, weight, cot, col, row, pack, n, m, heads):
+def forward_call(rows, weight, cot, col, row, n, heads):
     tokens, width = rows.shape
     shape = jax.ShapeDtypeStruct
     outs = (
@@ -1189,35 +1188,31 @@
         shape((heads, tokens, tokens), BF),
         shape((heads, tokens, HV), BF),
         shape((tokens * FRONT // CHUNKS, width), BF),
-        shape((pack.shape[0], m * pack.shape[1]), BF),
     )
     attention_rows = 2 * heads * (HK + HV)
-    wide = 2 * PARTS * (m - 1)
     sems = FRONT * 2 * (n - 1)
     return pl.pallas_call(
-        functools.partial(forward_kernel, n, m),
+        functools.partial(forward_kernel, n),
         out_shape=outs,
-        in_specs=[ANY] * 3 + [VM] * 3,
+        in_specs=[ANY] * 3 + [VM] * 2,
         out_specs=(ANY,) * len(outs),
         scratch_shapes=[pltpu.VMEM(rows.shape, BF), pltpu.VMEM((attention_rows, width), BF)]
-        + [pltpu.VMEM(o.shape, o.dtype) for o in outs[:-1]]
+        + [pltpu.VMEM(o.shape, o.dtype) for o in outs]
         + [
             pltpu.SemaphoreType.DMA((FRONT + 2 + len(outs),)),
             pltpu.SemaphoreType.DMA((sems,)),
             pltpu.SemaphoreType.DMA((sems,)),
-            pltpu.SemaphoreType.DMA((wide,)),
-            pltpu.SemaphoreType.DMA((wide,)),
         ],
         compiler_params=pltpu.CompilerParams(
             collective_id=4, has_side_effects=True, vmem_limit_bytes=VMEM_MOST
         ),
         name="forward",
-    )(rows, weight, cot, col, row, pack)
+    )(rows, weight, cot, col, row)
 
 
 def backward_kernel(
     n, m, mid, weights, gate, norm, scale, scores, query, key, value, down, middle, grads, col, row,
-    qk_o, value_o, gate_o, glu_gate_o, glu_up_o, down_o, outputs,
+    qk_o, value_o, gate_o, glu_gate_o, glu_up_o, outputs,
     mid_v, wo_v, gate_v, norm_v, scale_v, scores_v, query_v, key_v, value_v, part, middle_v,
     d_qk, d_value, d_gate, d_kept, d_scores, lefts, rights, *rest
 ):
@@ -1228,7 +1223,7 @@
     line = Line(n, send_sem, recv_sem)
     heads, tokens, deep = query_v.shape
     size = value_v.shape[2]
-    back = CHUNKS - DOWNS
+    back = CHUNKS - DOWNS - ENDS
     per = part.shape[0] // back
     piece = per // n
     copies = []
@@ -1239,13 +1234,14 @@
         c.start()
         return c
 
-    load_part = local(down, part)
+    load_part = local(down.at[pl.ds(0, part.shape[0])], part)
     loads = [
         local(src, dst)
         for src, dst in (
             (mid, mid_v), (weights.at[pl.ds(weights.shape[0] - wo_v.shape[0], wo_v.shape[0])], wo_v),
             (gate, gate_v), (norm, norm_v), (scale, scale_v), (value, value_v), (key, key_v),
-            (query, query_v), (scores, scores_v), (middle, middle_v),
+            (query, query_v), (scores, scores_v),
+            (middle.at[pl.ds(0, middle_v.shape[0])], middle_v),
         )
     ]
     halving, peers = grad_scatter(m, grads, kept, held, summed, wide_send, wide_recv, load_sem)
@@ -1317,15 +1313,14 @@
     local(d_gate, gate_o)
     for step in late:
         step()
-    size = down_o.shape[0]
-    wide = grads.shape[0] // 3
+    size = glu_up_o.shape[0]
+    wide = grads.shape[0] // 2
     for t in range(wide // LANES):
         have = min(LANES, size - t * LANES)
         for i, target in enumerate((glu_gate_o, glu_up_o)):
             local(
                 summed.at[pl.ds((2 * t + i) * LANES, have)], target.at[pl.ds(t * LANES, have)]
             )
-    local(summed.at[pl.ds(2 * wide, size)], down_o)
     for item in halving:
         assert item.done == len(bits) + 1
         item.leave()
@@ -1350,25 +1345,27 @@
 def backward_call(mid, weights, gate, norm, scale, scores, query, key, value, down, middle, grads, size_two, col, row, n, m):
     tokens, width = mid.shape
     heads, _, size = value.shape
-    back = CHUNKS - DOWNS
+    back = CHUNKS - DOWNS - ENDS
     nv = heads * size
     shard = width // m
+    piece = tokens // n // CHUNKS
     shape = jax.ShapeDtypeStruct
     outs = (
         shape((tokens, 2 * heads * HK), BF),
         shape(value.shape, BF),
         shape(value.shape, BF),
-    ) + (shape((size_two, shard), F32),) * 3 + (shape(middle.shape, BF),)
+    ) + (shape((size_two, shard), F32),) * 2 + (shape((back * piece, width), BF),)
     ins = (gate, norm, scale, scores, query, key, value, down, middle)
-    hop = (back, n - 1, middle.shape[0] // back, width)
+    hop = (back, n - 1, piece, width)
     sems = back * 2 * (n - 1)
     return pl.pallas_call(
         functools.partial(backward_kernel, n, m),
         out_shape=outs,
         in_specs=[ANY] * 12 + [VM] * 2,
-        out_specs=(ANY,) * 6 + (VM,),
+        out_specs=(ANY,) * 5 + (VM,),
         scratch_shapes=[pltpu.VMEM(mid.shape, BF), pltpu.VMEM((nv, width), BF)]
-        + [pltpu.VMEM(a.shape, a.dtype) for a in ins]
+        + [pltpu.VMEM(a.shape, a.dtype) for a in ins[:-2]]
+        + [pltpu.VMEM((back * n * piece, width), BF), pltpu.VMEM((back * piece, width), F32)]
         + [pltpu.VMEM(o.shape, o.dtype) for o in outs[:3]]
         + [
             pltpu.VMEM(value.shape, BF),
@@ -1378,7 +1375,7 @@
         ]
         + scatter_scratch(m, grads.shape[0], shard)
         + [
-            pltpu.SemaphoreType.DMA((15 + 2 * (grads.shape[0] // (3 * LANES)),)),
+            pltpu.SemaphoreType.DMA((15 + grads.shape[0] // LANES,)),
             pltpu.SemaphoreType.DMA((sems,)),
             pltpu.SemaphoreType.DMA((sems,)),
         ],
@@ -1389,58 +1386,148 @@
     )(mid, weights, *ins, grads, col, row)
 
 
-def products_kernel(plan, arrays, *refs):
-    ins, out = refs[:arrays], refs[arrays]
-    held, result, copy_sem = refs[arrays + 1 : 2 * arrays + 1], refs[-2], refs[-1]
-    loads = [pltpu.make_async_copy(a, b, copy_sem.at[i]) for i, (a, b) in enumerate(zip(ins, held))]
-    for item in loads:
+def products_kernel(n, m, plan, arrays, *refs):
+    ins, (down, middle, grads) = refs[:arrays], refs[arrays : arrays + 3]
+    out, down_o, outputs = refs[arrays + 3 : arrays + 6]
+    held_in = refs[arrays + 6 : 2 * arrays + 6]
+    part, middle_v, lefts, rights, result, kept, *rest = refs[2 * arrays + 6 :]
+    bits = bits_of(m)
+    held = rest[: len(bits)]
+    summed, wide_send, wide_recv, load_sem, copy_sem, send_sem, recv_sem = rest[len(bits) :]
+    line = Line(n, send_sem, recv_sem)
+    count, width = outputs.shape
+    piece = count // ENDS
+    per = n * piece
+    sources = list(zip(ins, held_in))
+    sources.append((middle.at[pl.ds(middle.shape[0] - count, count)], middle_v))
+    sources.append((down.at[pl.ds(down.shape[0] - n * count, n * count)], part))
+    loads = [pltpu.make_async_copy(a, b, copy_sem.at[i]) for i, (a, b) in enumerate(sources)]
+    for item in loads[::-1]:
         item.start()
-    waited, stores, base = set(), [], 0
-    for left, head, start, size, right in plan:
-        for i in (left, right):
-            if i not in waited:
-                loads[i].wait()
-                waited.add(i)
-        target = pl.ds(base, size)
-
-        def step(j, carry):
-            at = pl.ds(pl.multiple_of(j * 4 * LANES, 4 * LANES), 4 * LANES)
-            source = held[left][head] if head is not None else held[left][:, pl.ds(start, size)]
-            result[target, at] = dot_tn(source, held[right][:, at]).astype(BF)
-            return carry
-
-        lax.fori_loop(0, result.shape[1] // (4 * LANES), step, 0)
-        store = pltpu.make_async_copy(
-            result.at[target], out.at[target], copy_sem.at[arrays + len(stores)]
+    halving, peers = grad_scatter(m, grads, kept, held, summed, wide_send, wide_recv, load_sem)
+    line.enter(["dp", peers])
+    for item in halving:
+        item.step()
+    for item in halving:
+        item.load()
+    for h in range(ENDS):
+        no_neighbour_zero(n, line.place, lefts.at[h, n - 2], rights.at[h, n - 2])
+    scatters = [
+        Scatter(
+            line,
+            lambda k, h=h: part.at[pl.ds(h * per + k * piece, piece)],
+            lambda s, h=h: lefts.at[h, s - 1],
+            lambda s, h=h: rights.at[h, s - 1],
+            add_into,
         )
-        store.start()
-        stores.append(store)
-        base += size
+        for h in range(ENDS)
+    ]
+    loads[-1].wait()
+    for item in scatters:
+        item.step()
+    waited, stores = set(), []
+
+    def product(left, head, start, size, right, base):
+        def run():
+            for i in (left, right):
+                if i not in waited:
+                    loads[i].wait()
+                    waited.add(i)
+            target = pl.ds(base, size)
+
+            def step(j, carry):
+                at = pl.ds(pl.multiple_of(j * 4 * LANES, 4 * LANES), 4 * LANES)
+                source = (
+                    held_in[left][:, pl.ds(start, size)] if head is None else held_in[left][head]
+                )
+                result[target, at] = dot_tn(source, held_in[right][:, at]).astype(BF)
+                return carry
+
+            lax.fori_loop(0, width // (4 * LANES), step, 0)
+            store(target)
+
+        return run
+
+    def store(target):
+        c = pltpu.make_async_copy(
+            result.at[target], out.at[target], copy_sem.at[len(loads) + len(stores)]
+        )
+        c.start()
+        stores.append(c)
+
+    units, base = [], 0
+    for item in plan:
+        units.append(product(*item, base))
+        base += item[3]
+    steps = [item.step for _ in range(n - 2) for item in scatters]
+    wide_steps = [item.step for _ in bits for item in halving]
+    mixed = []
+    for i in range(max(len(steps), len(wide_steps))):
+        mixed += steps[i : i + 1] + wide_steps[i : i + 1]
+    in_order(units, mixed)
     spare = result.shape[0] - base
     if spare:
-        target = pl.ds(base, spare)
-        result[target, :] = jnp.zeros((spare, result.shape[1]), BF)
-        store = pltpu.make_async_copy(
-            result.at[target], out.at[target], copy_sem.at[arrays + len(stores)]
-        )
-        store.start()
-        stores.append(store)
-    for item in stores:
+        result[pl.ds(base, spare), :] = jnp.zeros((spare, width), BF)
+        store(pl.ds(base, spare))
+    keep = pltpu.make_async_copy(
+        summed.at[pl.ds(0, down_o.shape[0])], down_o, copy_sem.at[len(loads) + len(stores)]
+    )
+    keep.start()
+    loads[-2].wait()
+    for h in range(ENDS):
+        scatters[h].finish()
+
+        def step(at):
+            outputs[at(h * piece), :] = (
+                middle_v[at(h * piece), :]
+                + part[at(h * per), :].astype(F32)
+                + lefts[h, n - 2, at(), :].astype(F32)
+                + rights[h, n - 2, at(), :].astype(F32)
+            ).astype(BF)
+
+        blocks(piece, step)
+    for item in halving:
+        assert item.done == len(bits) + 1
+        item.leave()
+    for item in scatters:
+        item.drain()
+    for item in stores + [keep]:
         item.wait()
 
 
-def weight_products(plan, arrays, name, rows):
-    width = arrays[plan[0][4]].shape[1]
+def products_call(plan, arrays, down, middle, grads, size_two, rows, n, m):
+    width = grads.shape[1]
+    shard = width // m
+    piece = arrays[1].shape[0] // n // CHUNKS
+    sems = ENDS * 2 * (n - 1)
+    hop = (ENDS, n - 1, piece, width)
+    shape = jax.ShapeDtypeStruct
     return pl.pallas_call(
-        functools.partial(products_kernel, plan, len(arrays)),
-        out_shape=jax.ShapeDtypeStruct((rows, width), BF),
-        in_specs=[ANY] * len(arrays),
-        out_specs=ANY,
+        functools.partial(products_kernel, n, m, plan, len(arrays)),
+        out_shape=(
+            shape((rows, width), BF), shape((size_two, shard), F32), shape((ENDS * piece, width), BF),
+        ),
+        in_specs=[ANY] * (len(arrays) + 3),
+        out_specs=(ANY, ANY, VM),
         scratch_shapes=[pltpu.VMEM(a.shape, a.dtype) for a in arrays]
-        + [pltpu.VMEM((rows, width), BF), pltpu.SemaphoreType.DMA((len(arrays) + len(plan) + 1,))],
-        compiler_params=pltpu.CompilerParams(vmem_limit_bytes=VMEM_MOST),
-        name=name,
-    )(*arrays)
+        + [
+            pltpu.VMEM((ENDS * n * piece, width), BF),
+            pltpu.VMEM((ENDS * piece, width), F32),
+            pltpu.VMEM(hop, BF),
+            pltpu.VMEM(hop, BF),
+            pltpu.VMEM((rows, width), BF),
+        ]
+        + scatter_scratch(m, grads.shape[0], shard)
+        + [
+            pltpu.SemaphoreType.DMA((len(arrays) + len(plan) + 4,)),
+            pltpu.SemaphoreType.DMA((sems,)),
+            pltpu.SemaphoreType.DMA((sems,)),
+        ],
+        compiler_params=pltpu.CompilerParams(
+            collective_id=3, has_side_effects=True, vmem_limit_bytes=VMEM_MOST
+        ),
+        name="products",
+    )(*arrays, down, middle, grads)
 
 
 def pad_rows(array, count):
@@ -1515,20 +1602,23 @@
     row = jnp.concatenate([marks, jnp.exp(-powers) * HK ** (-0.5)], axis=0)
 
     (
-        query, key, value, gate_pre, normalized, scale_group, scores, gated, cot_front, weight_two,
-    ) = forward_call(rows_one, weight_one, cotangent, col, row, pack_two, n, m, heads)
-    mid_rows, grads_two, down, outputs_front, middle, middle_grad, second_gain = middle_call(
-        gated, weight_two, weight_one, inputs, cotangent, cot_front, second_norm_gain[None], n
+        query, key, value, gate_pre, normalized, scale_group, scores, gated, cot_front,
+    ) = forward_call(rows_one, weight_one, cotangent, col, row, n, heads)
+    (
+        mid_rows, grads_glu, grads_two, down, outputs_front, middle, middle_grad, second_gain,
+    ) = middle_call(
+        gated, pack_two, weight_one, inputs, cotangent, cot_front, second_norm_gain[None], n, m
     )
-    d_qk, d_value, d_gate, grad_glu_gate, grad_glu_up, grad_down, outputs_back = backward_call(
+    d_qk, d_value, d_gate, grad_glu_gate, grad_glu_up, outputs_back = backward_call(
         mid_rows, weight_one, gate_pre, normalized, scale_group, scores, query, key, value,
-        down, middle, grads_two, nf, col, row, n, m,
+        down, middle, grads_glu, nf, col, row, n, m,
     )
     plan = [(0, h, 0, HV, 1) for h in range(heads)] + [(2, h, 0, HV, 3) for h in range(heads)]
     plan += [(4, None, t * nk, nk, 3) for t in range(2)]
     plan += [(5, h, 0, HV, 3) for h in range(heads)]
-    grads_one = weight_products(
-        plan, (gated, mid_rows, d_gate, rows_one, d_qk, d_value), "products_one", one_rows
+    grads_one, grad_down, outputs_end = products_call(
+        plan, (gated, mid_rows, d_gate, rows_one, d_qk, d_value), down, middle, grads_two, nf,
+        one_rows, n, m,
     )
     input_gradient, gains, grad_query, grad_key, grad_out, grad_gate, grad_value = last_call(
         d_qk, d_value, d_gate, weight_one, grads_one, inputs, first_norm_gain[None], middle_grad,
@@ -1536,7 +1626,7 @@
     )
     gains = gains.reshape(2, width)
     return (
-        jnp.concatenate([outputs_front, outputs_back], axis=0),
+        jnp.concatenate([outputs_front, outputs_back, outputs_end], axis=0),
         input_gradient,
         gains[0],
         grad_query,

time: 603 us -> 592 us (0.982)
  Pallas kernels: 576 us -> 563 us
    pallas_call x1, Pallas kernels: 67.5 us -> 58.3 us  [backward_call(): pl.pallas_call(functools.partial(backward_kernel, n, m), out_shape=outs,...]
    pallas_call x3, Pallas kernels: 326 us -> 319 us  [the longest x1 241 us: middle_call(): pl.pallas_call(functools.partial(middle_kernel, n, m), out_shape=(shape((...]
    unnamed x59 -> x65, local copies, waits for them, and re-layouts: 13.1 us -> 11.3 us
where the time goes in v8:
time: 592 us; the launch traced here: 587 us
  Pallas kernels  563 us (95%)
  local copies, waits for them, and re-layouts  13.4 us (2%)
  other arithmetic  9.57 us (2%)
    pallas_call x1, Pallas kernels, middle_call(): pl.pallas_call(functools.partial(middle_kernel, n, m), out_shape=(shape((...  241 us
    pallas_call x1, Pallas kernels, last_call(): pl.pallas_call(functools.partial(last_kernel, n, m), out_shape=(shape((ro...  104 us
    pallas_call x1, Pallas kernels, gather_rows(): pl.pallas_call(functools.partial(gather_kernel, n, m), out_shape=(jax.Sha...  81 us
    pallas_call x1, Pallas kernels, backward_call(): pl.pallas_call(functools.partial(backward_kernel, n, m), out_shape=outs,...  58.3 us
    pallas_call x1, Pallas kernels, forward_call(): pl.pallas_call(functools.partial(forward_kernel, n), out_shape=outs, in_s...  44.4 us
    pallas_call x1, Pallas kernels, products_call(): pl.pallas_call(functools.partial(products_kernel, n, m, plan, len(arrays)...  34.2 us

profile of v8, /device:TPU:0, one launch (start us, length us, event | category | flops | bytes accessed | tf_op | source)
XLA Modules:
  0.0 586.7 jit_solution(15982354148178815187)
XLA Ops:
  0.8 1.5 convert_reduce_fusion
  2.3 1.6 fusion.3
  4.0 0.5 broadcast.130
  4.5 0.7 reduce.3
  5.3 0.1 convert_element_type.56
  5.6 0.1 fusion.8
  5.7 0.6 pad_maximum_fusion.3
  6.4 0.1 copy.25
  6.5 0.1 copy.26
  6.8 0.1 pad_maximum_fusion.1
  6.9 0.6 copy-done.17
  7.5 1.2 fusion.6.pack
  8.8 1.0 copy.28.col
  9.8 1.4 fusion.5.own
  11.4 1.2 copy-done.1
  12.6 81.0 %gather_rows.1 = (bf16[1024,2048]{1,0:T(8,128)(2,1)}, bf16[3648,2048]{1,0:T(8,128)(2,1)}) custom-call(bf16[256,2048]{1,0:T(8,128)(2,1)} %fusion.5.own, bf16[3648,256]{1,0:T(8,128)(2,1)} %copy-done.1), custom_call_target="tpu_custom_call" | custom-call | tf_op jit(solution)/shard_map/gather_rows/pallas_call | solution.py:347
  93.6 44.4 %forward.1 = (bf16[2,1024,256]{2,1,0:T(8,128)(2,1)}, bf16[2,1024,256]{2,1,0:T(8,128)(2,1)}, bf16[2,1024,432]{2,1,0:T(8,128)(2,1)}, f32[2,1024,432]{2,1,0:T(8,128...) custom-call(bf16[1024,2048]{1,0:T(8,128)(2,1)} %get-tuple-element.47, ...), custom_call_target="tpu_custom_call" | custom-call | tf_op jit(solution)/shard_map/forward/pallas_call | solution.py:1194
  138.0 240.6 %middle.1 = (bf16[1024,2048]{1,0:T(8,128)(2,1)}, bf16[1792,2048]{1,0:T(8,128)(2,1)}, bf16[896,2048]{1,0:T(8,128)(2,1)}, bf16[768,2048]{1,0:T(8,128)(2,1)}, bf16[...) custom-call(bf16[2,1024,432]{2,1,0:T(8,128)(2,1)} %get-tuple-element.49.gated.refs_0_, ...), custom_call_target="tpu_custom_call" | custom-call | tf_op jit(solution)/shard_map/middle/pallas_call | solution.py:699
  378.6 58.3 %backward.1 = (bf16[1024,1024]{1,0:T(8,128)(2,1)}, bf16[2,1024,432]{2,1,0:T(8,128)(2,1)}, bf16[2,1024,432]{2,1,0:T(8,128)(2,1)}, f32[864,256]{1,0:T(8,128)}, f32...) custom-call(bf16[1024,2048]{1,0:T(8,128)(2,1)} %get-tuple-element.52.mid.refs_1_, ...), custom_call_target="tpu_custom_call" | custom-call | tf_op jit(solution)/shard_map/backward/pallas_call | solution.py:1361
  436.9 34.2 %products.1 = (bf16[3648,2048]{1,0:T(8,128)(2,1)}, f32[864,256]{1,0:T(8,128)}, bf16[64,2048]{1,0:T(8,128)(2,1)}) custom-call(bf16[2,1024,432]{2,1,0:T(8,128)(2,1)} %get-tuple-element.49.gated.refs_0_, bf16[1024,2048]{1,0:T(8,128)(2,1)} %get-tuple-element.52.mid.refs_1_, bf16[2,1024,432]{2,1,0:T(8,128)(2,1)} %get-tuple-element.64.refs_2_.d_gate, ...), custom_call_target="tpu_custom_call" | custom-call | tf_op jit(solution)/shard_map/products/pallas_call | solution.py:1505
  471.1 104.2 %last.1 = (f32[256,2048]{1,0:T(8,128)}, f32[32,128]{1,0:T(8,128)}, f32[256,512]{1,0:T(8,128)}, f32[256,512]{1,0:T(8,128)}, f32[864,256]{1,0:T(8,128)}, /*index=5*/f32[864,256]{1,0:T(8,128)}, f32[864,256]{1,0:T(8,128)}) custom-call(bf16[1024,1024]{1,0:T(8,128)(2,1)} %get-tuple-element.65.refs_4_.d_qk, ...), custom_call_target="tpu_custom_call" | custom-call | tf_op jit(solution)/shard_map/last/pallas_call | solution.py:1034
  575.3 2.1 pad_maximum_fusion
  577.5 0.6 slice_bitcast_fusion
  578.1 1.3 copy.46
  579.5 0.8 copy.47
  580.3 0.8 copy.48
  581.1 0.9 copy.49
  582.0 0.9 copy.50
  582.9 0.9 copy.51
  583.8 0.9 copy.52
  584.7 0.9 copy.53
  585.6 0.9 copy.54
  (66 shorter events, 0.8 us)
Async XLA Ops:
  0.6 6.0 %copy-start.12 = (bf16[256,864]{0,1:T(8,128)(2,1)S(1)}, bf16[256,864]{0,1:T(8,128)(2,1)}, u32[]{:S(2)}) copy-start(bf16[256,864]{0,1:T(8,128)(2,1)} %param.22) | copy-start | bytes 1327108
  0.7 5.8 copy-start.19
  0.7 5.7 copy-start.18
  0.7 3.8 copy-start.23
  0.8 5.9 %copy-start.13 = (bf16[256,864]{0,1:T(8,128)(2,1)S(1)}, bf16[256,864]{0,1:T(8,128)(2,1)}, u32[]{:S(2)}) copy-start(bf16[256,864]{0,1:T(8,128)(2,1)} %param.23) | copy-start | bytes 1327108
  6.5 1.0 copy-start.17
  6.9 2.9 copy-start
  6.9 2.9 copy-start.21
  8.8 2.4 copy-start.14
  9.8 1.5 copy-start.15
  9.8 1.5 copy-start.16
  11.4 1.2 copy-start.1
  471.1 104.2 %copy-start.11 = (bf16[128,2048]{1,0:T(8,128)(2,1)S(1)}, bf16[128,2048]{1,0:T(8,128)(2,1)}, u32[]{:S(2)}) copy-start(bf16[128,2048]{1,0:T(8,128)(2,1)} %get-tuple-element.63) | copy-start | bytes 1572868
  471.1 104.2 %copy-start.20 = (bf16[64,2048]{1,0:T(8,128)(2,1)S(1)}, bf16[64,2048]{1,0:T(8,128)(2,1)}, u32[]{:S(2)}) copy-start(bf16[64,2048]{1,0:T(8,128)(2,1)} %get-tuple-element.51) | copy-start | bytes 786436
  575.3 2.2 copy-start.22
  575.3 2.8 copy-start.2
  578.1 1.4 copy-start.10
  578.1 2.2 copy-start.9
  579.5 1.6 copy-start.8
  579.5 2.5 copy-start.7
  580.3 2.6 copy-start.6
  582.0 1.8 copy-start.4
  582.9 1.8 copy-start.3
  583.8 1.8 copy-start.5

commit v9 on v8

--- a/solution.py
+++ b/solution.py
@@ -294,76 +294,6 @@
     return weight.at[:, pl.ds(at, shard)]
 
 
-def gather_kernel(n, m, own, pack, out, weight, send_sem, recv_sem, copy_sem, wide_send, wide_recv):
-    line = Line(n, send_sem, recv_sem)
-    piece = own.shape[0] // CHUNKS
-    per = n * piece
-    bits = bits_of(m)
-    doubling, peers = weight_gather(m, pack, weight, wide_send, wide_recv)
-    line.enter(["dp", peers])
-    local, gathers = [], []
-    keep = pltpu.make_async_copy(pack, own_columns(pack, weight), copy_sem.at[CHUNKS])
-    for h in range(CHUNKS):
-        mine = own.at[pl.ds(h * piece, piece)]
-        local.append(
-            pltpu.make_async_copy(mine, out.at[pl.ds(h * per, piece)], copy_sem.at[h])
-        )
-
-        def slot(k, h=h, mine=mine):
-            return mine if k == 0 else out.at[pl.ds(h * per + k * piece, piece)]
-
-        gathers.append(Gather(line, slot))
-    local.append(keep)
-
-    def line_step(items):
-        for item in items:
-            item.step()
-
-    half = CHUNKS // 2
-    line_step(gathers)
-    line_step(doubling)
-    for item in local:
-        item.start()
-    for level in range(1, max(n, len(bits) + 1)):
-        for side in range(2):
-            if level <= len(bits):
-                line_step(doubling[side * PARTS : (side + 1) * PARTS])
-            if level < n:
-                line_step(gathers[side * half : (side + 1) * half])
-    for item in local:
-        item.wait()
-    for item in gathers:
-        assert item.step_no == n
-    for item in doubling:
-        assert item.done == len(bits) + 1
-        item.leave()
-    line.leave()
-
-
-def gather_rows(own, pack, n, m):
-    rows, width = own.shape
-    count = CHUNKS * 2 * (n - 1)
-    wide = 2 * PARTS * (m - 1)
-    return pl.pallas_call(
-        functools.partial(gather_kernel, n, m),
-        out_shape=(
-            jax.ShapeDtypeStruct((n * rows, width), own.dtype),
-            jax.ShapeDtypeStruct((pack.shape[0], m * pack.shape[1]), pack.dtype),
-        ),
-        in_specs=[VM, VM],
-        out_specs=(ANY, ANY),
-        scratch_shapes=[
-            pltpu.SemaphoreType.DMA((count,)),
-            pltpu.SemaphoreType.DMA((count,)),
-            pltpu.SemaphoreType.DMA((CHUNKS + 1,)),
-            pltpu.SemaphoreType.DMA((wide,)),
-            pltpu.SemaphoreType.DMA((wide,)),
-        ],
-        compiler_params=pltpu.CompilerParams(collective_id=0, has_side_effects=True),
-        name="gather_rows",
-    )(own, pack)
-
-
 def no_neighbour_zero(n, place, from_left, from_right):
     @pl.when(place == 0)
     def _():
@@ -385,12 +315,12 @@
 }
 TUNED = {
     (4, 4, 3): [
-        58, 2, 4, 57, 59, 8, 56, 2, 5, 57, 8, 58, 8, 9, 3, 59, 7, 12, 56, 2,
-        16, 9, 58, 6, 16, 9, 57, 10, 59, 56, 16, 13, 11, 17, 57, 3, 10, 16, 58, 17,
-        11, 56, 59, 20, 10, 20, 17, 24, 11, 14, 28, 18, 3, 15, 28, 18, 19, 2, 17, 21,
+        2, 58, 7, 57, 4, 59, 8, 56, 5, 2, 8, 57, 58, 56, 8, 9, 3, 6, 59, 12,
+        2, 16, 9, 58, 16, 10, 9, 57, 59, 56, 16, 13, 11, 17, 58, 57, 3, 10, 16, 17,
+        56, 11, 59, 20, 10, 20, 17, 24, 28, 11, 14, 18, 3, 15, 28, 19, 18, 2, 17, 21,
         28, 21, 40, 44, 18, 19, 25, 32, 29, 36, 18, 22, 29, 19, 44, 22, 29, 26, 36, 30,
-        44, 19, 3, 23, 33, 36, 37, 30, 23, 27, 37, 31, 30, 52, 37, 31, 34, 38, 42, 41,
-        48, 31, 38, 52, 35, 39, 38, 39, 36, 37, 38, 52, 39, 43, 39,
+        44, 19, 3, 23, 33, 37, 30, 36, 23, 27, 37, 31, 30, 52, 37, 31, 34, 38, 42, 41,
+        31, 38, 35, 39, 38, 52, 48, 39, 36, 37, 38, 52, 39, 43, 39,
     ],
 }
 
@@ -859,46 +789,55 @@
     ]
 
 
-def exchange(groups, mine, total, send_sem, recv_sem):
-    source, base = mine, 0
-    for axis, size, held in groups:
+class Exchange:
+    def __init__(self, groups, mine, total, send_sem, recv_sem):
+        self.groups, self.source, self.total = groups, mine, total
+        self.send_sem, self.recv_sem = send_sem, recv_sem
+        self.done, self.base, self.sent = 0, 0, []
+
+    def copy(self, k, slot):
+        axis, size, held = self.groups[self.done]
+        return pltpu.make_async_remote_copy(
+            src_ref=self.source,
+            dst_ref=held.at[slot],
+            send_sem=self.send_sem.at[self.base + k],
+            recv_sem=self.recv_sem.at[self.base + k],
+            device_id={axis: lax.rem(lax.axis_index(axis) + k, size)},
+            device_id_type=MESH,
+        )
+
+    def send(self):
+        axis, size, held = self.groups[self.done]
         me = lax.axis_index(axis)
-        held[me] = source[...]
-
-        def copy(k, slot):
-            return pltpu.make_async_remote_copy(
-                src_ref=source,
-                dst_ref=held.at[slot],
-                send_sem=send_sem.at[base + k],
-                recv_sem=recv_sem.at[base + k],
-                device_id={axis: lax.rem(me + k, size)},
-                device_id_type=MESH,
-            )
-
-        sent = [copy(k, me) for k in range(1, size)]
-        for c in sent:
+        held[me] = self.source[...]
+        self.sent = [self.copy(k, me) for k in range(1, size)]
+        for c in self.sent:
             c.start()
+
+    def receive(self):
+        axis, size, held = self.groups[self.done]
+        me = lax.axis_index(axis)
         for k in range(1, size):
-            copy(k, lax.rem(me - k + size, size)).wait_recv()
+            self.copy(k, lax.rem(me - k + size, size)).wait_recv()
         value = held[0]
         for k in range(1, size):
             value = value + held[k]
-        for c in sent:
+        for c in self.sent:
             c.wait_send()
-        total[...] = value
-        source, base = total, base + size
+        self.total[...] = value
+        self.source, self.base, self.done = self.total, self.base + size, self.done + 1
 
 
 def last_kernel(
-    n, m, d_qk, d_value, d_gate, weight, grads, inputs, gain, d_middle, second_gain,
+    n, m, d_qk, d_value, d_gate, weight, grads, inputs, gain, d_middle, second_gain, rows,
     out, gains, grad_query, grad_key, grad_out, grad_gate, grad_value,
     qk_v, value_v, gate_v, weight_v, inputs_v, middle_v, part, lefts, rights, *rest
 ):
     bits = bits_of(m)
     kept, held = rest[0], rest[1 : 1 + len(bits)]
     summed, wide_send, wide_recv, load_sem = rest[1 + len(bits) : 5 + len(bits)]
-    gain_sum, mine, first, second = rest[5 + len(bits) : 9 + len(bits)]
-    copy_sem, send_sem, recv_sem, gain_send, gain_recv = rest[9 + len(bits) :]
+    gain_sum, mine, first, second, rows_v = rest[5 + len(bits) : 10 + len(bits)]
+    copy_sem, send_sem, recv_sem, gain_send, gain_recv = rest[10 + len(bits) :]
     line = Line(n, send_sem, recv_sem)
     count, width = out.shape
     piece = count // CHUNKS
@@ -910,7 +849,8 @@
         for i, (src, dst) in enumerate(
             [
                 (weight.at[pl.ds(0, weight_v.shape[0])], weight_v), (d_qk, qk_v),
-                (d_value, value_v), (d_gate, gate_v), (inputs, inputs_v), (d_middle, middle_v),
+                (d_value, value_v), (d_gate, gate_v), (rows, rows_v), (inputs, inputs_v),
+                (d_middle, middle_v),
             ]
         )
     ]
@@ -970,17 +910,41 @@
                 + rights[h, n - 2, at(), :].astype(F32)
             )
             hat, scale = layer_norm(inputs_v[own, :].astype(F32), epsilon)
-            gain_sum[...] += jnp.sum((hat * grad).reshape(BLOCK // 8, 8, width), axis=0)
             out[own, :] = middle_v[own, :] + norm_back(grad * gain[...], hat, scale)
 
         blocks(piece, step)
 
-    for item in load:
+    def gain_part(h):
+        def step(at):
+            here = at(h * per)
+            term = rows_v[here, :].astype(F32) * part[here, :].astype(F32)
+            gain_sum[...] += jnp.sum(term.reshape(BLOCK // 8, 8, width), axis=0)
+
+        blocks(per, step)
+
+    for item in load[:5]:
         item.wait()
     for h in range(CHUNKS):
         product(h)
         scatters[h].step()
+        gain_part(h)
+    flats = (
+        jnp.sum(gain_sum[...], axis=0, keepdims=True) / gain[...],
+        jnp.sum(second_gain[...], axis=0, keepdims=True),
+    )
+    for i, flat in enumerate(flats):
+        for j in range(width // LANES):
+            mine[pl.ds(i * (width // LANES) + j, 1), :] = flat[:, j * LANES : (j + 1) * LANES]
+    total_gain = Exchange(
+        [("dp", m, first), ("mp", n, second)], mine, gains, gain_send, gain_recv
+    )
+    total_gain.send()
+    for item in load[5:]:
+        item.wait()
     for s in range(n - 2):
+        if s == 1:
+            total_gain.receive()
+            total_gain.send()
         for h in range(CHUNKS):
             if s < len(bits) and h < len(halving):
                 halving[h].step()
@@ -990,11 +954,6 @@
             item.step()
     for h in range(CHUNKS):
         finish(h)
-    groups = [("dp", m, first), ("mp", n, second)]
-    for i, source in enumerate((gain_sum, second_gain)):
-        flat = jnp.sum(source[...], axis=0, keepdims=True)
-        for j in range(width // LANES):
-            mine[pl.ds(i * (width // LANES) + j, 1), :] = flat[:, j * LANES : (j + 1) * LANES]
     for item in halving:
         while item.done <= len(bits):
             item.step()
@@ -1013,7 +972,7 @@
         for j in range(deep // LANES):
             target[:, j * LANES : (j + 1) * LANES] = summed[pl.ds(base, LANES), :].T
             base += LANES
-    exchange(groups, mine, gains, gain_send, gain_recv)
+    total_gain.receive()
     for item in halving:
         item.leave()
     for store in stores:
@@ -1022,7 +981,9 @@
         scatters[h].drain()
 
 
-def last_call(d_qk, d_value, d_gate, weight, grads, inputs, gain, d_middle, second_gain, n, m):
+def last_call(
+    d_qk, d_value, d_gate, weight, grads, inputs, gain, d_middle, second_gain, rows_one, n, m
+):
     tokens = d_qk.shape[0]
     rows, width = inputs.shape
     heads = d_value.shape[0]
@@ -1040,7 +1001,7 @@
             shape((shard, heads * HK), F32),
         )
         + (shape((heads * HV, shard), F32),) * 3,
-        in_specs=[ANY] * 6 + [VM, ANY, VM],
+        in_specs=[ANY] * 6 + [VM, ANY, VM, ANY],
         out_specs=(VM,) * 4 + (ANY,) * 3,
         scratch_shapes=[
             pltpu.VMEM(d_qk.shape, BF),
@@ -1059,7 +1020,8 @@
             pltpu.VMEM(flat, F32),
             pltpu.VMEM((m,) + flat, F32),
             pltpu.VMEM((n,) + flat, F32),
-            pltpu.SemaphoreType.DMA((9,)),
+            pltpu.VMEM((tokens, width), BF),
+            pltpu.SemaphoreType.DMA((10,)),
             pltpu.SemaphoreType.DMA((sems,)),
             pltpu.SemaphoreType.DMA((sems,)),
             pltpu.SemaphoreType.DMA((n + m,)),
@@ -1069,18 +1031,21 @@
             collective_id=2, has_side_effects=True, vmem_limit_bytes=VMEM_MOST
         ),
         name="last",
-    )(d_qk, d_value, d_gate, weight, grads, inputs, gain, d_middle, second_gain)
+    )(d_qk, d_value, d_gate, weight, grads, inputs, gain, d_middle, second_gain, rows_one)
 
 
 TILE = 256
 
 
-def tiles_of(count, step):
+def tiles_of(count, step, start=None):
     def run(i, carry):
         step(pl.ds(pl.multiple_of(i * TILE, TILE), TILE))
         return carry
 
-    lax.fori_loop(0, count // TILE, run, 0)
+    if start is None:
+        lax.fori_loop(0, count // TILE, run, 0)
+    else:
+        lax.fori_loop(start, start + count, run, 0)
 
 
 def in_order(units, steps):
@@ -1094,14 +1059,14 @@
 
 
 def forward_kernel(
-    n, rows, weight, cot, col, row,
-    query_o, key_o, value_o, gate_o, norm_o, scale_o, scores_o, gated_o, cot_o,
-    rows_v, weight_v, query_v, key_v, value_v, gate_v, norm_v, scale_v, scores_v, gated_v, cot_v,
-    copy_sem, send_sem, recv_sem,
+    n, m, own, pack, cot, col, row,
+    rows_o, weight_o, query_o, key_o, value_o, gate_o, norm_o, scale_o, scores_o, gated_o, cot_o,
+    rows_v, weight_v, both_v, value_v, gate_v, norm_v, scale_v, scores_v, gated_v, cot_v,
+    copy_sem, send_sem, recv_sem, wide_send, wide_recv,
 ):
     line = Line(n, send_sem, recv_sem)
-    heads, tokens, deep = query_v.shape
-    size = value_v.shape[2]
+    heads, tokens, size = value_v.shape
+    deep = both_v.shape[2]
     per = cot_v.shape[0] // FRONT
     piece = per // n
     copies = []
@@ -1112,36 +1077,41 @@
         c.start()
         return c
 
-    load_cot = [
-        local(cot.at[pl.ds(h * piece, piece)], cot_v.at[pl.ds(h * per, piece)])
-        for h in range(FRONT)
-    ]
-    load_rows = local(rows, rows_v)
-    load_weight = local(weight.at[pl.ds(0, weight_v.shape[0])], weight_v)
-    line.enter()
-    gathers = [
-        Gather(line, lambda k, h=h: cot_v.at[pl.ds(h * per + k * piece, piece)])
-        for h in range(FRONT)
-    ]
-    for item in load_cot:
-        item.wait()
-    for g in gathers:
-        g.step()
-    load_rows.wait()
-    load_weight.wait()
-
-    def project(target, h, base, width):
+    doubling, peers = weight_gather(m, pack, weight_v, wide_send, wide_recv)
+    line.enter(["dp", peers])
+
+    def row_slot(h, k):
+        if k == 0:
+            return own.at[pl.ds(h * piece, piece)]
+        return rows_v.at[pl.ds(h * per + k * piece, piece)]
+
+    def cot_slot(h, k):
+        return cot_v.at[pl.ds(h * per + k * piece, piece)]
+
+    gathers = [Gather(line, functools.partial(row_slot, h)) for h in range(CHUNKS)]
+    cots = [Gather(line, functools.partial(cot_slot, h)) for h in range(FRONT)]
+    half = CHUNKS // 2
+    levels = len(bits_of(m))
+
+    def go(items):
+        for item in items:
+            item.step()
+
+    def project(target, first, last, base, width, start, count):
         def step(at):
-            target[h, at, :] = dot_nt(rows_v[at, :], weight_v[pl.ds(base, width), :]).astype(
-                target.dtype
-            )
-
-        return lambda: tiles_of(tokens, step)
+            def one(j, carry):
+                rows = pl.ds(pl.multiple_of(base + j * width, BLOCK), width)
+                target[j, at, :] = dot_nt(rows_v[at, :], weight_v[rows, :]).astype(target.dtype)
+                return carry
+
+            lax.fori_loop(first, last, one, 0)
+
+        return lambda: tiles_of(count, step, start)
 
     def attend(h):
         def step(at):
             allowed = (col[at, 0:1] >= row[0:1, :]) & (col[at, 1:2] == row[1:2, :])
-            scores = dot_nt(query_v[h, at, :], key_v[h]) * col[at, 2 + h : 3 + h]
+            scores = dot_nt(both_v[h, at, :], both_v[heads + h]) * col[at, 2 + h : 3 + h]
             scores = jnp.where(allowed, scores * row[2 + h : 3 + h, :], 0.0).astype(BF)
             scores_v[h, at, :] = scores
             hat, scale = layer_norm(dot_nn(scores, value_v[h]), group_epsilon)
@@ -1153,32 +1123,77 @@
         return lambda: tiles_of(tokens, step)
 
     values, gates = 2 * heads * deep, 2 * heads * deep + heads * size
-    units = []
-    for h in range(heads):
-        units += [
-            project(query_v, h, h * deep, deep),
-            project(key_v, h, (heads + h) * deep, deep),
-            project(value_v, h, values + h * size, size),
-            project(gate_v, h, gates + h * size, size),
-            attend(h),
-        ]
-    in_order(units, [g.step for _ in range(n - 1) for g in gathers])
+    assert values <= PARTS * (weight_v.shape[0] // (2 * PARTS))
+    near, far = gathers[:half], gathers[half:]
+    soon, later = doubling[:PARTS], doubling[PARTS:]
+    go(near)
+    go(soon)
+    for h in range(CHUNKS):
+        local(row_slot(h, 0), rows_v.at[pl.ds(h * per, piece)])
+    local(pack, own_columns(pack, weight_v))
+    for h in range(FRONT):
+        local(cot.at[pl.ds(h * piece, piece)], cot_slot(h, 0))
+    first_copies = list(copies)
+    go(near)
+    go(soon)
+    go(later)
+    for _ in range(n - 3):
+        go(near)
+    go(far)
+    for _ in range(levels - 1):
+        go(soon)
+    go(near)
+    for item in first_copies:
+        item.wait()
+    tail = [g.step for _ in range(n - 2) for g in far]
+    tail_wide = [g.step for _ in range(levels - 1) for g in later]
+    mixed = []
+    for i in range(max(len(tail), len(tail_wide))):
+        mixed += tail[i : i + 1] + tail_wide[i : i + 1]
+    early = tokens // 2 // TILE
+    in_order(
+        [
+            project(both_v, 0, 2 * heads, 0, deep, t, 1)
+            for t in range(early)
+        ],
+        mixed,
+    )
+    go(cots)
+    go(later)
+    go(far)
+    units = [
+        project(both_v, 0, 2 * heads, 0, deep, early, early),
+        project(value_v, 0, heads, values, size, 0, 2 * early),
+        project(gate_v, 0, heads, gates, size, 0, early),
+        project(gate_v, 0, heads, gates, size, early, early),
+    ] + [attend(h) for h in range(heads)]
     count = len(copies)
+    local(rows_v, rows_o)
+    local(weight_v, weight_o)
+    in_order(units, [g.step for _ in range(n - 1) for g in cots])
     for src, dst in (
-        (query_v, query_o), (key_v, key_o), (value_v, value_o), (gate_v, gate_o),
-        (norm_v, norm_o), (scale_v, scale_o), (scores_v, scores_o), (gated_v, gated_o),
-        (cot_v, cot_o),
+        (both_v.at[pl.ds(0, heads)], query_o), (both_v.at[pl.ds(heads, heads)], key_o),
+        (value_v, value_o), (gate_v, gate_o), (norm_v, norm_o), (scale_v, scale_o),
+        (scores_v, scores_o), (gated_v, gated_o), (cot_v, cot_o),
     ):
         local(src, dst)
     for item in copies[count:]:
         item.wait()
+    for item in gathers + cots:
+        assert item.step_no == n
+    for item in doubling:
+        assert item.done == levels + 1
+        item.leave()
     line.leave()
 
 
-def forward_call(rows, weight, cot, col, row, n, heads):
-    tokens, width = rows.shape
+def forward_call(own, pack, cot, col, row, n, m, heads):
+    rows, width = own.shape
+    tokens = n * rows
     shape = jax.ShapeDtypeStruct
     outs = (
+        shape((tokens, width), BF),
+        shape((pack.shape[0], m * pack.shape[1]), BF),
         shape((heads, tokens, HK), BF),
         shape((heads, tokens, HK), BF),
         shape((heads, tokens, HV), BF),
@@ -1189,25 +1204,27 @@
         shape((heads, tokens, HV), BF),
         shape((tokens * FRONT // CHUNKS, width), BF),
     )
-    attention_rows = 2 * heads * (HK + HV)
-    sems = FRONT * 2 * (n - 1)
+    held = outs[:2] + (shape((2 * heads, tokens, HK), BF),) + outs[4:]
+    sems = (CHUNKS + FRONT) * 2 * (n - 1)
+    wide = 2 * PARTS * (m - 1)
     return pl.pallas_call(
-        functools.partial(forward_kernel, n),
+        functools.partial(forward_kernel, n, m),
         out_shape=outs,
-        in_specs=[ANY] * 3 + [VM] * 2,
+        in_specs=[VM, VM, ANY, VM, VM],
         out_specs=(ANY,) * len(outs),
-        scratch_shapes=[pltpu.VMEM(rows.shape, BF), pltpu.VMEM((attention_rows, width), BF)]
-        + [pltpu.VMEM(o.shape, o.dtype) for o in outs]
+        scratch_shapes=[pltpu.VMEM(o.shape, o.dtype) for o in held]
         + [
-            pltpu.SemaphoreType.DMA((FRONT + 2 + len(outs),)),
+            pltpu.SemaphoreType.DMA((CHUNKS + FRONT + 1 + len(outs),)),
             pltpu.SemaphoreType.DMA((sems,)),
             pltpu.SemaphoreType.DMA((sems,)),
+            pltpu.SemaphoreType.DMA((wide,)),
+            pltpu.SemaphoreType.DMA((wide,)),
         ],
         compiler_params=pltpu.CompilerParams(
             collective_id=4, has_side_effects=True, vmem_limit_bytes=VMEM_MOST
         ),
         name="forward",
-    )(rows, weight, cot, col, row)
+    )(own, pack, cot, col, row)
 
 
 def backward_kernel(
@@ -1581,8 +1598,8 @@
     pack_two = jnp.concatenate([glu_pack, pad_rows(w_down, f_wide)], axis=0)
 
     first_hat, _ = layer_norm(inputs.astype(F32), epsilon)
-    rows_one, weight_one = gather_rows((first_hat * first_norm_gain).astype(BF), pack_one, n, m)
-    tokens = rows_one.shape[0]
+    first_rows = (first_hat * first_norm_gain).astype(BF)
+    tokens = n * rows
 
     slot_shard = lax.rem(place - jnp.arange(n) + n, n)
     places = (
@@ -1602,8 +1619,9 @@
     row = jnp.concatenate([marks, jnp.exp(-powers) * HK ** (-0.5)], axis=0)
 
     (
-        query, key, value, gate_pre, normalized, scale_group, scores, gated, cot_front,
-    ) = forward_call(rows_one, weight_one, cotangent, col, row, n, heads)
+        rows_one, weight_one, query, key, value, gate_pre, normalized, scale_group, scores, gated,
+        cot_front,
+    ) = forward_call(first_rows, pack_one, cotangent, col, row, n, m, heads)
     (
         mid_rows, grads_glu, grads_two, down, outputs_front, middle, middle_grad, second_gain,
     ) = middle_call(
@@ -1622,7 +1640,7 @@
     )
     input_gradient, gains, grad_query, grad_key, grad_out, grad_gate, grad_value = last_call(
         d_qk, d_value, d_gate, weight_one, grads_one, inputs, first_norm_gain[None], middle_grad,
-        second_gain, n, m,
+        second_gain, rows_one, n, m,
     )
     gains = gains.reshape(2, width)
     return (

time: 592 us -> 575 us (0.971)
  Pallas kernels: 563 us -> 546 us
    pallas_call x1, Pallas kernels: 58.3 us -> 50.8 us  [backward_call(): pl.pallas_call(functools.partial(backward_kernel, n, m), out_shape=outs,...]
    pallas_call x1, Pallas kernels: 104 us -> 97.1 us  [last_call(): pl.pallas_call(functools.partial(last_kernel, n, m), out_shape=(shape((ro...]
    pallas_call x2 -> x1, Pallas kernels: 125 us -> 123 us  [forward_call(): pl.pallas_call(functools.partial(forward_kernel, n, m), out_shape=outs, i...]
    unnamed x65 -> x63, local copies, waits for them, and re-layouts: 11.3 us -> 13.6 us
where the time goes in v9:
time: 575 us; the launch traced here: 573 us
  Pallas kernels  546 us (95%)
  local copies, waits for them, and re-layouts  16.4 us (3%)
  other arithmetic  9.59 us (2%)
    pallas_call x1, Pallas kernels, middle_call(): pl.pallas_call(functools.partial(middle_kernel, n, m), out_shape=(shape((...  241 us
    pallas_call x1, Pallas kernels, forward_call(): pl.pallas_call(functools.partial(forward_kernel, n, m), out_shape=outs, i...  123 us
    pallas_call x1, Pallas kernels, last_call(): pl.pallas_call(functools.partial(last_kernel, n, m), out_shape=(shape((ro...  97.1 us
    pallas_call x1, Pallas kernels, backward_call(): pl.pallas_call(functools.partial(backward_kernel, n, m), out_shape=outs,...  50.8 us
    pallas_call x1, Pallas kernels, products_call(): pl.pallas_call(functools.partial(products_kernel, n, m, plan, len(arrays)...  35 us
    unnamed x63, local copies, waits for them, and re-layouts  13.6 us

profile of v9, /device:TPU:0, one launch (start us, length us, event | category | flops | bytes accessed | tf_op | source)
XLA Modules:
  0.0 573.4 jit_solution(4569764415468546537)
XLA Ops:
  0.8 1.5 convert_reduce_fusion
  2.3 1.6 fusion.3
  4.0 0.5 broadcast.130
  4.5 0.7 reduce.3
  5.7 0.6 pad_maximum_fusion.3
  6.5 0.1 copy.26
  6.9 0.6 copy-done.16
  7.5 1.3 fusion.6.pack
  8.8 1.0 copy.28.col
  9.8 1.4 fusion.5.own
  11.2 0.7 bitcast_dynamic-update-slice_fusion.3
  11.9 0.7 bitcast_dynamic-update-slice_fusion.2
  12.6 0.8 bitcast_dynamic-update-slice_fusion.1
  13.4 0.8 bitcast_dynamic-update-slice_fusion
  14.2 0.6 constant_dynamic-update-slice_fusion.1
  14.8 0.8 constant_dynamic-update-slice_fusion.pack
  15.6 122.6 %forward.1 = (bf16[1024,2048]{1,0:T(8,128)(2,1)}, bf16[3648,2048]{1,0:T(8,128)(2,1)}, bf16[2,1024,256]{2,1,0:T(8,128)(2,1)}, bf16[2,1024,256]{2,1,0:T(8,128)(2,1...) custom-call(bf16[256,2048]{1,0:T(8,128)(2,1)} %fusion.5.own, ...), custom_call_target="tpu_custom_call" | custom-call | tf_op jit(solution)/shard_map/forward/pallas_call | solution.py:1210
  138.2 241.1 %middle.1 = (bf16[1024,2048]{1,0:T(8,128)(2,1)}, bf16[1792,2048]{1,0:T(8,128)(2,1)}, bf16[896,2048]{1,0:T(8,128)(2,1)}, bf16[768,2048]{1,0:T(8,128)(2,1)}, bf16[...) custom-call(bf16[2,1024,432]{2,1,0:T(8,128)(2,1)} %get-tuple-element.47.gated.refs_0_, ...), custom_call_target="tpu_custom_call" | custom-call | tf_op jit(solution)/shard_map/middle/pallas_call | solution.py:629
  379.2 50.8 %backward.1 = (bf16[1024,1024]{1,0:T(8,128)(2,1)}, bf16[2,1024,432]{2,1,0:T(8,128)(2,1)}, bf16[2,1024,432]{2,1,0:T(8,128)(2,1)}, f32[864,256]{1,0:T(8,128)}, f32...) custom-call(bf16[1024,2048]{1,0:T(8,128)(2,1)} %get-tuple-element.51.mid.refs_1_, ...), custom_call_target="tpu_custom_call" | custom-call | tf_op jit(solution)/shard_map/backward/pallas_call | solution.py:1378
  430.0 35.0 %products.1 = (bf16[3648,2048]{1,0:T(8,128)(2,1)}, f32[864,256]{1,0:T(8,128)}, bf16[64,2048]{1,0:T(8,128)(2,1)}) custom-call(bf16[2,1024,432]{2,1,0:T(8,128)(2,1)} %get-tuple-element.47.gated.refs_0_, bf16[1024,2048]{1,0:T(8,128)(2,1)} %get-tuple-element.51.mid.refs_1_, bf16[2,1024,432]{2,1,0:T(8,128)(2,1)} %get-tuple-element.63.refs_2_.d_gate, ...), custom_call_target="tpu_custom_call" | custom-call | tf_op jit(solution)/shard_map/products/pallas_call | solution.py:1522
  465.1 97.1 %last.1 = (f32[256,2048]{1,0:T(8,128)}, f32[32,128]{1,0:T(8,128)}, f32[256,512]{1,0:T(8,128)}, f32[256,512]{1,0:T(8,128)}, f32[864,256]{1,0:T(8,128)}, /*index=5*/f32[864,256]{1,0:T(8,128)}, f32[864,256]{1,0:T(8,128)}) custom-call(bf16[1024,1024]{1,0:T(8,128)(2,1)} %get-tuple-element.65.refs_4_.d_qk, ...), custom_call_target="tpu_custom_call" | custom-call | tf_op jit(solution)/shard_map/last/pallas_call | solution.py:995
  562.2 2.1 pad_maximum_fusion
  564.4 0.6 slice_bitcast_fusion
  565.0 1.3 copy.46
  566.3 0.8 copy.47
  567.1 0.8 copy.48
  567.9 0.9 copy.49
  568.9 0.9 copy.50
  569.8 0.9 copy.51
  570.7 0.9 copy.52
  571.6 0.9 copy.53
  572.5 0.9 copy.54
  (63 shorter events, 1.1 us)
Async XLA Ops:
  0.6 6.0 %copy-start.11 = (bf16[256,864]{0,1:T(8,128)(2,1)S(1)}, bf16[256,864]{0,1:T(8,128)(2,1)}, u32[]{:S(2)}) copy-start(bf16[256,864]{0,1:T(8,128)(2,1)} %param.22) | copy-start | bytes 1327108
  0.7 5.8 %copy-start.18 = (bf16[256,512]{1,0:T(8,128)(2,1)S(1)}, bf16[256,512]{1,0:T(8,128)(2,1)}, u32[]{:S(2)}) copy-start(bf16[256,512]{1,0:T(8,128)(2,1)} %param.17) | copy-start | bytes 786436
  0.7 5.7 copy-start.17
  0.7 3.8 copy-start.22
  0.8 5.9 %copy-start.12 = (bf16[256,864]{0,1:T(8,128)(2,1)S(1)}, bf16[256,864]{0,1:T(8,128)(2,1)}, u32[]{:S(2)}) copy-start(bf16[256,864]{0,1:T(8,128)(2,1)} %param.23) | copy-start | bytes 1327108
  6.5 1.0 copy-start.16
  6.9 3.0 copy-start
  6.9 2.9 copy-start.20
  8.8 3.8 copy-start.13
  9.8 3.6 copy-start.14
  9.8 5.0 copy-start.15
  465.0 97.1 %copy-start.10 = (bf16[128,2048]{1,0:T(8,128)(2,1)S(1)}, bf16[128,2048]{1,0:T(8,128)(2,1)}, u32[]{:S(2)}) copy-start(bf16[128,2048]{1,0:T(8,128)(2,1)} %get-tuple-element.62) | copy-start | bytes 1572868
  465.1 97.1 %copy-start.19 = (bf16[64,2048]{1,0:T(8,128)(2,1)S(1)}, bf16[64,2048]{1,0:T(8,128)(2,1)}, u32[]{:S(2)}) copy-start(bf16[64,2048]{1,0:T(8,128)(2,1)} %get-tuple-element.50) | copy-start | bytes 786436
  562.2 2.2 copy-start.21
  562.2 2.8 copy-start.1
  565.0 1.4 copy-start.9
  565.0 2.2 copy-start.8
  566.3 1.6 copy-start.7
  566.3 2.5 copy-start.6
  567.1 2.6 copy-start.5
  568.9 1.8 copy-start.3
  569.8 1.8 copy-start.2
  570.7 1.8 copy-start.4

commit v10 on v9

--- a/solution.py
+++ b/solution.py
@@ -1059,9 +1059,9 @@
 
 
 def forward_kernel(
-    n, m, own, pack, cot, col, row,
+    n, m, inputs, gain, pack, cot, col, row,
     rows_o, weight_o, query_o, key_o, value_o, gate_o, norm_o, scale_o, scores_o, gated_o, cot_o,
-    rows_v, weight_v, both_v, value_v, gate_v, norm_v, scale_v, scores_v, gated_v, cot_v,
+    own, rows_v, weight_v, both_v, value_v, gate_v, norm_v, scale_v, scores_v, gated_v, cot_v,
     copy_sem, send_sem, recv_sem, wide_send, wide_recv,
 ):
     line = Line(n, send_sem, recv_sem)
@@ -1126,8 +1126,17 @@
     assert values <= PARTS * (weight_v.shape[0] // (2 * PARTS))
     near, far = gathers[:half], gathers[half:]
     soon, later = doubling[:PARTS], doubling[PARTS:]
+    def normalize(first, count):
+        def step(at):
+            hat, _ = layer_norm(inputs[at(first), :].astype(F32), epsilon)
+            own[at(first), :] = (hat * gain[...]).astype(BF)
+
+        blocks(count, step)
+
+    go(soon)
+    normalize(0, half * piece)
     go(near)
-    go(soon)
+    normalize(half * piece, (CHUNKS - half) * piece)
     for h in range(CHUNKS):
         local(row_slot(h, 0), rows_v.at[pl.ds(h * per, piece)])
     local(pack, own_columns(pack, weight_v))
@@ -1187,8 +1196,8 @@
     line.leave()
 
 
-def forward_call(own, pack, cot, col, row, n, m, heads):
-    rows, width = own.shape
+def forward_call(inputs, gain, pack, cot, col, row, n, m, heads):
+    rows, width = inputs.shape
     tokens = n * rows
     shape = jax.ShapeDtypeStruct
     outs = (
@@ -1210,9 +1219,10 @@
     return pl.pallas_call(
         functools.partial(forward_kernel, n, m),
         out_shape=outs,
-        in_specs=[VM, VM, ANY, VM, VM],
+        in_specs=[VM, VM, VM, ANY, VM, VM],
         out_specs=(ANY,) * len(outs),
-        scratch_shapes=[pltpu.VMEM(o.shape, o.dtype) for o in held]
+        scratch_shapes=[pltpu.VMEM((rows, width), BF)]
+        + [pltpu.VMEM(o.shape, o.dtype) for o in held]
         + [
             pltpu.SemaphoreType.DMA((CHUNKS + FRONT + 1 + len(outs),)),
             pltpu.SemaphoreType.DMA((sems,)),
@@ -1224,7 +1234,7 @@
             collective_id=4, has_side_effects=True, vmem_limit_bytes=VMEM_MOST
         ),
         name="forward",
-    )(own, pack, cot, col, row)
+    )(inputs, gain, pack, cot, col, row)
 
 
 def backward_kernel(
@@ -1547,6 +1557,43 @@
     )(*arrays, down, middle, grads)
 
 
+def results_kernel(plan, *refs):
+    count = len(plan)
+    results = refs[count : -count - 1]
+    held, sem = refs[-count - 1 : -1], refs[-1]
+    ins = [pltpu.make_async_copy(refs[i], held[i], sem.at[0, i]) for i in range(count)]
+    for item in ins:
+        item.start()
+    outs = []
+    for i, (result, start) in enumerate(plan):
+        ins[i].wait()
+        target = results[result].at[pl.ds(start, held[i].shape[0])]
+        outs.append(pltpu.make_async_copy(held[i], target, sem.at[1, i]))
+        outs[-1].start()
+    for item in outs:
+        item.wait()
+
+
+def write_results(groups):
+    plan, arrays, shapes = [], [], []
+    for r, group in enumerate(groups):
+        start = 0
+        for array in group:
+            plan.append((r, start))
+            arrays.append(array)
+            start += array.shape[0]
+        shapes.append(jax.ShapeDtypeStruct((start,) + group[0].shape[1:], group[0].dtype))
+    return pl.pallas_call(
+        functools.partial(results_kernel, plan),
+        out_shape=shapes,
+        in_specs=[ANY] * len(arrays),
+        out_specs=[ANY] * len(shapes),
+        scratch_shapes=[pltpu.VMEM(a.shape, a.dtype) for a in arrays]
+        + [pltpu.SemaphoreType.DMA((2, len(arrays)))],
+        name="results",
+    )(*arrays)
+
+
 def pad_rows(array, count):
     return jnp.pad(array, ((0, count - array.shape[0]), (0, 0)))
 
@@ -1597,8 +1644,6 @@
     ).reshape(2 * f_wide, shard)
     pack_two = jnp.concatenate([glu_pack, pad_rows(w_down, f_wide)], axis=0)
 
-    first_hat, _ = layer_norm(inputs.astype(F32), epsilon)
-    first_rows = (first_hat * first_norm_gain).astype(BF)
     tokens = n * rows
 
     slot_shard = lax.rem(place - jnp.arange(n) + n, n)
@@ -1621,7 +1666,9 @@
     (
         rows_one, weight_one, query, key, value, gate_pre, normalized, scale_group, scores, gated,
         cot_front,
-    ) = forward_call(first_rows, pack_one, cotangent, col, row, n, m, heads)
+    ) = forward_call(
+        inputs, first_norm_gain[None], pack_one, cotangent, col, row, n, m, heads
+    )
     (
         mid_rows, grads_glu, grads_two, down, outputs_front, middle, middle_grad, second_gain,
     ) = middle_call(
@@ -1643,8 +1690,17 @@
         second_gain, rows_one, n, m,
     )
     gains = gains.reshape(2, width)
+    (
+        outputs, input_gradient, grad_query, grad_key, grad_value, grad_gate, grad_out,
+        grad_glu_gate, grad_glu_up, grad_down,
+    ) = write_results(
+        [
+            (outputs_front, outputs_back, outputs_end), (input_gradient,), (grad_query,), (grad_key,),
+            (grad_value,), (grad_gate,), (grad_out,), (grad_glu_gate,), (grad_glu_up,), (grad_down,),
+        ]
+    )
     return (
-        jnp.concatenate([outputs_front, outputs_back, outputs_end], axis=0),
+        outputs,
         input_gradient,
         gains[0],
         grad_query,

time: 575 us -> 572 us (level)
  Pallas kernels: 546 us -> 554 us
  local copies, waits for them, and re-layouts: 16.4 us -> 10.2 us
  other arithmetic: 9.59 us -> 3.53 us
    pallas_call x0 -> x1, Pallas kernels: none -> 7.25 us  [write_results(): pl.pallas_call(functools.partial(results_kernel, plan), out_shape=shapes,...]
    unnamed x63 -> x20, local copies, waits for them, and re-layouts: 13.6 us -> 6.33 us
where the time goes in v10:
time: 572 us; the launch traced here: 569 us
  Pallas kernels  554 us (97%)
  local copies, waits for them, and re-layouts  10.2 us (2%)
    pallas_call x1, Pallas kernels, middle_call(): pl.pallas_call(functools.partial(middle_kernel, n, m), out_shape=(shape((...  241 us
    pallas_call x1, Pallas kernels, forward_call(): pl.pallas_call(functools.partial(forward_kernel, n, m), out_shape=outs, i...  124 us
    pallas_call x1, Pallas kernels, last_call(): pl.pallas_call(functools.partial(last_kernel, n, m), out_shape=(shape((ro...  96.3 us
    pallas_call x1, Pallas kernels, backward_call(): pl.pallas_call(functools.partial(backward_kernel, n, m), out_shape=outs,...  50.6 us
    pallas_call x1, Pallas kernels, products_call(): pl.pallas_call(functools.partial(products_kernel, n, m, plan, len(arrays)...  35.2 us

profile of v10, /device:TPU:0, one launch (start us, length us, event | category | flops | bytes accessed | tf_op | source)
XLA Modules:
  0.0 569.0 jit_solution(8797824292188554932)
XLA Ops:
  0.7 0.1 broadcast_add_fusion
  0.8 0.5 broadcast.106
  1.3 1.3 reduce.3
  2.6 0.1 reshape.136
  2.8 0.1 convert_element_type.48
  2.9 0.1 add_convert_fusion
  2.9 0.1 convert_element_type.49
  3.0 0.1 convert_element_type.45
  3.1 0.1 fusion.3
  3.2 0.6 pad_maximum_fusion.2
  3.8 1.1 copy.25
  4.9 1.1 copy.26
  6.0 0.0 copy-start.4
  6.0 1.1 pad.10
  7.1 0.0 copy-done
  7.1 0.1 pad_maximum_fusion
  7.3 0.0 copy-start.1
  7.3 1.2 fusion.1.pack
  8.5 1.0 copy.28.col
  9.5 0.7 bitcast_dynamic-update-slice_fusion.3
  10.2 0.7 bitcast_dynamic-update-slice_fusion.2
  10.9 0.8 bitcast_dynamic-update-slice_fusion.1
  11.7 0.8 bitcast_dynamic-update-slice_fusion
  12.5 0.6 constant_dynamic-update-slice_fusion.1
  13.1 0.8 constant_dynamic-update-slice_fusion.pack
  13.9 124.1 %forward.1 = (bf16[1024,2048]{1,0:T(8,128)(2,1)}, bf16[3648,2048]{1,0:T(8,128)(2,1)}, bf16[2,1024,256]{2,1,0:T(8,128)(2,1)}, bf16[2,1024,256]{2,1,0:T(8,128)(2,1...) custom-call(bf16[256,2048]{1,0:T(8,128)(2,1)} %inputs.3, ...), custom_call_target="tpu_custom_call" | custom-call | tf_op jit(solution)/shard_map/forward/pallas_call | solution.py:1219
  138.0 241.1 %middle.1 = (bf16[1024,2048]{1,0:T(8,128)(2,1)}, bf16[1792,2048]{1,0:T(8,128)(2,1)}, bf16[896,2048]{1,0:T(8,128)(2,1)}, bf16[768,2048]{1,0:T(8,128)(2,1)}, bf16[...) custom-call(bf16[2,1024,432]{2,1,0:T(8,128)(2,1)} %get-tuple-element.57.gated.refs_0_, ...), custom_call_target="tpu_custom_call" | custom-call | tf_op jit(solution)/shard_map/middle/pallas_call | solution.py:629
  379.1 50.6 %backward.1 = (bf16[1024,1024]{1,0:T(8,128)(2,1)}, bf16[2,1024,432]{2,1,0:T(8,128)(2,1)}, bf16[2,1024,432]{2,1,0:T(8,128)(2,1)}, f32[864,256]{1,0:T(8,128)}, f32...) custom-call(bf16[1024,2048]{1,0:T(8,128)(2,1)} %get-tuple-element.61.mid.refs_1_, ...), custom_call_target="tpu_custom_call" | custom-call | tf_op jit(solution)/shard_map/backward/pallas_call | solution.py:1388
  429.7 35.2 %products.1 = (bf16[3648,2048]{1,0:T(8,128)(2,1)}, f32[864,256]{1,0:T(8,128)}, bf16[64,2048]{1,0:T(8,128)(2,1)}) custom-call(bf16[2,1024,432]{2,1,0:T(8,128)(2,1)} %get-tuple-element.57.gated.refs_0_, bf16[1024,2048]{1,0:T(8,128)(2,1)} %get-tuple-element.61.mid.refs_1_, bf16[2,1024,432]{2,1,0:T(8,128)(2,1)} %get-tuple-element.73.refs_2_.d_gate, ...), custom_call_target="tpu_custom_call" | custom-call | tf_op jit(solution)/shard_map/products/pallas_call | solution.py:1532
  464.8 96.3 %last.1 = (f32[256,2048]{1,0:T(8,128)}, f32[32,128]{1,0:T(8,128)}, f32[256,512]{1,0:T(8,128)}, f32[256,512]{1,0:T(8,128)}, f32[864,256]{1,0:T(8,128)}, /*index=5*/f32[864,256]{1,0:T(8,128)}, f32[864,256]{1,0:T(8,128)}) custom-call(bf16[1024,1024]{1,0:T(8,128)(2,1)} %get-tuple-element.75.refs_4_.d_qk, ...), custom_call_target="tpu_custom_call" | custom-call | tf_op jit(solution)/shard_map/last/pallas_call | solution.py:995
  561.1 7.3 %results.1 = (bf16[256,2048]{1,0:T(8,128)(2,1)}, f32[256,2048]{1,0:T(8,128)}, f32[256,512]{1,0:T(8,128)}, f32[256,512]{1,0:T(8,128)}, f32[864,256]{1,0:T(8,128)}...) custom-call(bf16[64,2048]{1,0:T(8,128)(2,1)} %get-tuple-element.60.r, ...), custom_call_target="tpu_custom_call" | custom-call | tf_op jit(solution)/shard_map/results/pallas_call | solution.py:1586
  568.4 0.6 slice_bitcast_fusion
  (15 shorter events, 0.1 us)
Async XLA Ops:
  0.6 6.5 %copy-start = (bf16[256,864]{0,1:T(8,128)(2,1)S(1)}, bf16[256,864]{0,1:T(8,128)(2,1)}, u32[]{:S(2)}) copy-start(bf16[256,864]{0,1:T(8,128)(2,1)} %param.23) | copy-start | bytes 1327108
  6.0 1.3 copy-start.4
  7.3 3.7 copy-start.1
  8.5 3.3 copy-start.2
  8.5 4.7 copy-start.3
  561.1 7.3 %copy-start.5 = (f32[32,128]{1,0:T(8,128)S(1)}, f32[32,128]{1,0:T(8,128)}, u32[]{:S(2)}) copy-start(f32[32,128]{1,0:T(8,128)} %get-tuple-element.93) | copy-start | bytes 49156
